TPU v7x, 32 devices: a whole 2x2x4 slice. The times are simulated.
32 devices in a mesh: gy: 8 (over z, x), gx: 4 (over y, core).
Axes of the slice: x: 2, y: 2, z: 4, core: 2. Of those that a mesh axis runs over, the one named last changes fastest.
Arguments:
- imbalance: float32 [4, 1024, 2048], P(None, 'gy', 'gx'), may hold values from -9 to 9
- flow: float32 [2, 4, 1024, 2048], P(None, None, 'gy', 'gx'), may hold values from -3 to 3
- potential: float32 [4, 1024, 2048], P(None, 'gy', 'gx'), may hold values from -5 to 5
- cost: float32 [1024, 2048], P('gy', 'gx'), may hold values from 0.2 to 2
Outputs:
- flow_out: float32 [2, 4, 1024, 2048], P(None, None, 'gy', 'gx')
- potential_out: float32 [4, 1024, 2048], P(None, 'gy', 'gx')
- residual: float32 [4], replicated
All inputs are finite; a program needn't handle non-finite values.
Results may differ from a plain program's by a relative error of at most 0.0001.
Values sent between devices are 32-bit elements; how exact they have to be, the bound alone decides.
No kernel may reach another device: no remote copies, remote signals or barrier semaphores. Data moves between devices by JAX's collectives and lax.ppermute only.
A program may use at most 64 MiB of HBM per device.

v0:
```python
import jax
import jax.numpy as jnp
from jax import lax
from jax.sharding import PartitionSpec as P

ITERS = 12


initial_step = 0.35
epsilon = 1e-06


def shifted(value, axis, steps):
    count = lax.axis_size(axis)
    leading, last = (max(0, -steps), min(count, count - steps))
    return lax.ppermute(value, axis, [(source, source + steps) for source in range(leading, last)])


def gradient(potential):
    from_below = shifted(potential[:, 0, :], "gy", -1)
    from_right = shifted(potential[:, :, 0], "gx", -1)
    slope_down = jnp.concatenate([potential[:, 1:, :], from_below[:, None, :]], 1) - potential
    slope_right = jnp.concatenate([potential[:, :, 1:], from_right[:, :, None]], 2) - potential
    return (slope_down, slope_right)


def divergence(flow_down, flow_right):
    from_above = shifted(flow_down[:, -1, :], "gy", 1)
    from_left = shifted(flow_right[:, :, -1], "gx", 1)
    above_rows = jnp.concatenate([from_above[:, None, :], flow_down[:, :-1, :]], 1)
    left_cols = jnp.concatenate([from_left[:, :, None], flow_right[:, :, :-1]], 2)
    return flow_down - above_rows + flow_right - left_cols


def shrink(moved_down, moved_right, threshold):
    magnitude = jnp.sqrt(moved_down * moved_down + moved_right * moved_right)
    factor = jnp.maximum(magnitude - threshold, 0.0) / jnp.maximum(magnitude, threshold)
    return (factor * moved_down, factor * moved_right)


def local(imbalance, flow, potential, cost):
    local_rows, local_cols = cost.shape

    def primal(flow_down, flow_right, field, spread_old, primal_rate):
        slope_down, slope_right = gradient(field)
        rate_now = primal_rate[:, None, None]
        new_down, new_right = shrink(
            flow_down + rate_now * slope_down,
            flow_right + rate_now * slope_right,
            rate_now * cost[None],
        )
        return (new_down, new_right, spread_old, None)

    spread_start = divergence(flow[0], flow[1])

    def iterate(carried, with_stats):
        flow_down, flow_right, field, spread_old, primal_rate, dual_rate = carried
        new_down, new_right, spread_old, spread_new = primal(
            flow_down, flow_right, field, spread_old, primal_rate
        )
        if with_stats:
            diff_down = new_down - flow_down
            diff_right = new_right - flow_right
            primal_local = jnp.sum(diff_down * diff_down + diff_right * diff_right, axis=(1, 2))
        spread_new = divergence(new_down, new_right)
        new_field = field + dual_rate[:, None, None] * (2.0 * spread_new - spread_old - imbalance)
        if with_stats:
            change = new_field - field
            dual_local = jnp.sum(change * change, axis=(1, 2))
            primal_change, dual_change = lax.psum((primal_local, dual_local), ("gy", "gx"))
            rescale = jnp.sqrt(jnp.sqrt((primal_change + epsilon) / (dual_change + epsilon)))
            primal_rate = primal_rate / rescale
            dual_rate = dual_rate * rescale
        return (new_down, new_right, new_field, spread_new, primal_rate, dual_rate)

    def loop_turn(counter, carried):
        return iterate(carried, True)

    starting = jnp.full((potential.shape[0],), initial_step, jnp.float32)
    carried = (flow[0], flow[1], potential, spread_start, starting, starting)
    carried = lax.fori_loop(0, ITERS - 1, loop_turn, carried)
    closing = iterate(carried, False)
    shortfall = closing[3] - imbalance
    total_sum = lax.psum(jnp.sum(shortfall * shortfall, axis=(1, 2)), ("gy", "gx"))
    cell_count = local_rows * lax.axis_size("gy") * local_cols * lax.axis_size("gx")
    residual = total_sum / cell_count
    return (jnp.stack([closing[0], closing[1]]), closing[2], residual)


def solution(mesh):
    placed = (P(None, "gy", "gx"), P(None, None, "gy", "gx"), P(None, "gy", "gx"), P("gy", "gx"))
    return jax.shard_map(
        local,
        mesh=mesh,
        in_specs=placed,
        out_specs=(P(None, None, "gy", "gx"), P(None, "gy", "gx"), P()),
        check_vma=False,
    )
```

profile of v0, /device:TPU:0, one launch (start us, length us, event | category | flops | bytes accessed | tf_op | source)
XLA Modules:
  0.0 887.7 jit_solution(16072063486011655081)
XLA Ops:
  21.5 791.1 %while.21 = (s32[]{:T(128)}, f32[4,128,512]{1,0,2:T(4,128)S(1)}, f32[4,128,512]{1,0,2:T(4,128)S(1)}, f32[4,128,512]{1,0,2:T(4,128)S(1)}, f32[4,128,512]{1,0,2:T(...) while((s32[]{:T(128)}, f32[4,128,512]{1,0,2:T(4,128)S(1)}, ...), condition=%wide.region_5.0_spmd.clone, body=%wide.region_0.0_spmd.clone.sunk | while | flops 10747943 | bytes 36053636 | solution.py:81
  48.4 5.4 multiply_reduce_fusion.3
  53.8 42.1 %all-reduce.2 = (f32[4]{0:T(128)S(1)}, f32[4]{0:T(128)S(1)}) all-reduce(f32[4]{0:T(128)S(1)} %get-tuple-element.228, f32[4]{0:T(128)S(1)} %get-tuple-element.229), channel_id=1, replica_groups=mesh['gy'=8,'gx'=4] {'gy','gx'}, use_global_device_ids=true, to_apply=%region_4.0 | all-reduce | flops 8 | bytes 64 | tf_op jit(solution)/shard_map/while/body/eval_jaxpr/psum | solution.py:70
  122.2 5.4 multiply_reduce_fusion.3
  127.5 39.6 %all-reduce.2 = (f32[4]{0:T(128)S(1)}, f32[4]{0:T(128)S(1)}) all-reduce(f32[4]{0:T(128)S(1)} %get-tuple-element.228, f32[4]{0:T(128)S(1)} %get-tuple-element.229), channel_id=1, replica_groups=mesh['gy'=8,'gx'=4] {'gy','gx'}, use_global_device_ids=true, to_apply=%region_4.0 | all-reduce | flops 8 | bytes 64 | tf_op jit(solution)/shard_map/while/body/eval_jaxpr/psum | solution.py:70
  193.4 5.4 multiply_reduce_fusion.3
  198.8 40.4 %all-reduce.2 = (f32[4]{0:T(128)S(1)}, f32[4]{0:T(128)S(1)}) all-reduce(f32[4]{0:T(128)S(1)} %get-tuple-element.228, f32[4]{0:T(128)S(1)} %get-tuple-element.229), channel_id=1, replica_groups=mesh['gy'=8,'gx'=4] {'gy','gx'}, use_global_device_ids=true, to_apply=%region_4.0 | all-reduce | flops 8 | bytes 64 | tf_op jit(solution)/shard_map/while/body/eval_jaxpr/psum | solution.py:70
  265.5 5.4 multiply_reduce_fusion.3
  270.9 39.6 %all-reduce.2 = (f32[4]{0:T(128)S(1)}, f32[4]{0:T(128)S(1)}) all-reduce(f32[4]{0:T(128)S(1)} %get-tuple-element.228, f32[4]{0:T(128)S(1)} %get-tuple-element.229), channel_id=1, replica_groups=mesh['gy'=8,'gx'=4] {'gy','gx'}, use_global_device_ids=true, to_apply=%region_4.0 | all-reduce | flops 8 | bytes 64 | tf_op jit(solution)/shard_map/while/body/eval_jaxpr/psum | solution.py:70
  336.7 5.4 multiply_reduce_fusion.3
  342.1 40.4 %all-reduce.2 = (f32[4]{0:T(128)S(1)}, f32[4]{0:T(128)S(1)}) all-reduce(f32[4]{0:T(128)S(1)} %get-tuple-element.228, f32[4]{0:T(128)S(1)} %get-tuple-element.229), channel_id=1, replica_groups=mesh['gy'=8,'gx'=4] {'gy','gx'}, use_global_device_ids=true, to_apply=%region_4.0 | all-reduce | flops 8 | bytes 64 | tf_op jit(solution)/shard_map/while/body/eval_jaxpr/psum | solution.py:70
  408.8 5.4 multiply_reduce_fusion.3
  414.2 39.6 %all-reduce.2 = (f32[4]{0:T(128)S(1)}, f32[4]{0:T(128)S(1)}) all-reduce(f32[4]{0:T(128)S(1)} %get-tuple-element.228, f32[4]{0:T(128)S(1)} %get-tuple-element.229), channel_id=1, replica_groups=mesh['gy'=8,'gx'=4] {'gy','gx'}, use_global_device_ids=true, to_apply=%region_4.0 | all-reduce | flops 8 | bytes 64 | tf_op jit(solution)/shard_map/while/body/eval_jaxpr/psum | solution.py:70
  480.1 5.4 multiply_reduce_fusion.3
  485.5 40.4 %all-reduce.2 = (f32[4]{0:T(128)S(1)}, f32[4]{0:T(128)S(1)}) all-reduce(f32[4]{0:T(128)S(1)} %get-tuple-element.228, f32[4]{0:T(128)S(1)} %get-tuple-element.229), channel_id=1, replica_groups=mesh['gy'=8,'gx'=4] {'gy','gx'}, use_global_device_ids=true, to_apply=%region_4.0 | all-reduce | flops 8 | bytes 64 | tf_op jit(solution)/shard_map/while/body/eval_jaxpr/psum | solution.py:70
  552.1 5.4 multiply_reduce_fusion.3
  557.5 39.6 %all-reduce.2 = (f32[4]{0:T(128)S(1)}, f32[4]{0:T(128)S(1)}) all-reduce(f32[4]{0:T(128)S(1)} %get-tuple-element.228, f32[4]{0:T(128)S(1)} %get-tuple-element.229), channel_id=1, replica_groups=mesh['gy'=8,'gx'=4] {'gy','gx'}, use_global_device_ids=true, to_apply=%region_4.0 | all-reduce | flops 8 | bytes 64 | tf_op jit(solution)/shard_map/while/body/eval_jaxpr/psum | solution.py:70
  623.4 5.4 multiply_reduce_fusion.3
  628.8 40.4 %all-reduce.2 = (f32[4]{0:T(128)S(1)}, f32[4]{0:T(128)S(1)}) all-reduce(f32[4]{0:T(128)S(1)} %get-tuple-element.228, f32[4]{0:T(128)S(1)} %get-tuple-element.229), channel_id=1, replica_groups=mesh['gy'=8,'gx'=4] {'gy','gx'}, use_global_device_ids=true, to_apply=%region_4.0 | all-reduce | flops 8 | bytes 64 | tf_op jit(solution)/shard_map/while/body/eval_jaxpr/psum | solution.py:70
  695.5 5.4 multiply_reduce_fusion.3
  700.9 39.6 %all-reduce.2 = (f32[4]{0:T(128)S(1)}, f32[4]{0:T(128)S(1)}) all-reduce(f32[4]{0:T(128)S(1)} %get-tuple-element.228, f32[4]{0:T(128)S(1)} %get-tuple-element.229), channel_id=1, replica_groups=mesh['gy'=8,'gx'=4] {'gy','gx'}, use_global_device_ids=true, to_apply=%region_4.0 | all-reduce | flops 8 | bytes 64 | tf_op jit(solution)/shard_map/while/body/eval_jaxpr/psum | solution.py:70
  766.7 5.4 multiply_reduce_fusion.3
  772.1 40.4 %all-reduce.2 = (f32[4]{0:T(128)S(1)}, f32[4]{0:T(128)S(1)}) all-reduce(f32[4]{0:T(128)S(1)} %get-tuple-element.228, f32[4]{0:T(128)S(1)} %get-tuple-element.229), channel_id=1, replica_groups=mesh['gy'=8,'gx'=4] {'gy','gx'}, use_global_device_ids=true, to_apply=%region_4.0 | all-reduce | flops 8 | bytes 64 | tf_op jit(solution)/shard_map/while/body/eval_jaxpr/psum | solution.py:70
  841.9 42.0 %psum.21 = f32[4]{0:T(128)S(1)} all-reduce(f32[4]{0:T(128)S(1)} %get-tuple-element.148), channel_id=1, replica_groups=mesh['gy'=8,'gx'=4] {'gy','gx'}, use_global_device_ids=true, to_apply=%region_7.0 | all-reduce | flops 4 | bytes 32 | tf_op jit(solution)/shard_map/psum | solution.py:84
  (343 shorter events, 341.9 us)
Async XLA Ops:
  3.7 13.1 %collective-permute-start.4 = (f32[4,512]{1,0:T(4,128)S(1)}, f32[4,512]{1,0:T(4,128)S(1)}, u32[]{:S(2)}, u32[]{:S(2)}) collective-permute-start(f32[4,512]{1,0:T(4,128)S(1)} %bitcast.78), channel_id=1, source_target_pairs={{0,4},{4,8},{8,12},{12,16},{16,20},{20,24},{24,28},{1,5},{5,9},{9,... | collective-permute-start | bytes 24584 | tf_op jit(solution)/shard_map/ppermute | solution.py:16
  9.0 9.1 %collective-permute-start.5 = (f32[4,128]{1,0:T(4,128)S(1)}, f32[4,128]{1,0:T(4,128)S(1)}, u32[]{:S(2)}, u32[]{:S(2)}) collective-permute-start(f32[4,128]{1,0:T(4,128)S(1)} %slice_bitcast_fusion.2), channel_id=1, source_target_pairs={{0,1},{1,2},{2,3},{4,5},{5,6},{6,7},{8,9},{9,10},{10,11},{12,13},{... | collective-permute-start | bytes 6152 | tf_op jit(solution)/shard_map/ppermute | solution.py:16
  21.5 8.5 collective-permute-start
  38.4 8.7 collective-permute-start.3
  96.0 8.8 collective-permute-start
  113.1 7.7 collective-permute-start.3
  167.2 8.8 collective-permute-start
  184.4 7.7 collective-permute-start.3
  239.3 8.8 collective-permute-start
  256.4 7.7 collective-permute-start.3
  310.6 8.8 collective-permute-start
  382.6 8.8 collective-permute-start
  453.9 8.8 collective-permute-start
  471.0 7.7 collective-permute-start.3
  526.0 8.8 collective-permute-start
  543.1 7.7 collective-permute-start.3
  597.2 8.8 collective-permute-start
  614.3 7.7 collective-permute-start.3
  669.3 8.8 collective-permute-start
  686.4 7.7 collective-permute-start.3
  740.5 8.8 collective-permute-start
  813.0 12.8 %collective-permute-start.6 = (f32[4,512]{1,0:T(4,128)S(1)}, f32[4,512]{1,0:T(4,128)S(1)}, u32[]{:S(2)}, u32[]{:S(2)}) collective-permute-start(f32[4,512]{1,0:T(4,128)S(1)} %bitcast.77), channel_id=1, source_target_pairs={{4,0},{8,4},{12,8},{16,12},{20,16},{24,20},{28,24},{5,1},{9,5},{13... | collective-permute-start | bytes 24584 | tf_op jit(solution)/shard_map/ppermute | solution.py:16
  814.3 10.7 %collective-permute-start.7 = (f32[4,128]{1,0:T(4,128)S(1)}, f32[4,128]{1,0:T(4,128)S(1)}, u32[]{:S(2)}, u32[]{:S(2)}) collective-permute-start(f32[4,128]{1,0:T(4,128)S(1)} %slice_bitcast_fusion.3), channel_id=1, source_target_pairs={{1,0},{2,1},{3,2},{5,4},{6,5},{7,6},{9,8},{10,9},{11,10},{13,12},{... | collective-permute-start | bytes 6152 | tf_op jit(solution)/shard_map/ppermute | solution.py:16
  829.6 9.4 %collective-permute-start.9 = (f32[4,128]{1,0:T(4,128)S(1)}, f32[4,128]{1,0:T(4,128)S(1)}, u32[]{:S(2)}, u32[]{:S(2)}) collective-permute-start(f32[4,128]{1,0:T(4,128)S(1)} %slice_reduce_fusion), channel_id=1, source_target_pairs={{0,1},{1,2},{2,3},{4,5},{5,6},{6,7},{8,9},{9,10},{10,11},{12,13},{... | collective-permute-start | bytes 6152 | tf_op jit(solution)/shard_map/ppermute | solution.py:16
  (42 other events, 197.9 us)
where the time goes:
time: 891 us; the launch traced here: 888 us
  blocking collectives  484 us (54%)
  local copies, waits for them, and re-layouts  132 us (15%)
  other arithmetic  131 us (15%)
  starting transfers between devices  118 us (13%)
  waiting for transfers between devices  19.6 us (2%)
    psum x11, blocking collectives, iterate(): lax.psum((primal_local, dual_local), ('gy', 'gx'))  442 us
    ppermute x50, starting transfers between devices, shifted(): lax.ppermute(value, axis, [(source, source + steps) for source in range(l...  118 us
    reduce_sum x11, other arithmetic, iterate(): dual_local = jnp.sum(change * change, axis=(1, 2))  59.3 us
    div x11, other arithmetic, shrink(): jnp.maximum(magnitude - threshold, 0.0) / jnp.maximum(magnitude, threshold)  42.2 us
    psum x1, blocking collectives, local(): lax.psum(jnp.sum(shortfall * shortfall, axis=(1, 2)), ('gy', 'gx'))  42 us
    slice x25, local copies, waits for them, and re-layouts, divergence(): from_above = shifted(flow_down[:, -1, :], 'gy', 1)  35.4 us
    slice x12, local copies, waits for them, and re-layouts, gradient(): potential[:, 1:, :]  20.5 us
    ppermute x50, waiting for transfers between devices, shifted(): lax.ppermute(value, axis, [(source, source + steps) for source in range(l...  19.6 us
  transfers between devices with their start and end apart: 50, of which 11 were waited for; matrix products, arithmetic and copies ran while one was open for 11% of the time, Pallas kernels for 0%

commit v1 on v0

v1 whole, which is shorter than its diff:
```python
import functools

import jax
import jax.numpy as jnp
from jax import lax
from jax.experimental import pallas as pl
from jax.experimental.pallas import tpu as pltpu
from jax.sharding import PartitionSpec as P

ITERS = 12
initial_step = 0.35
epsilon = 1e-06

DEEP = 12
SLAB = 16
PAD = 8
TOP = PAD + SLAB
LANES = 128
AXES = ("gy", "gx")


def neighbour(value, axis, steps):
    count = lax.axis_size(axis)
    leading, last = (max(0, -steps), min(count, count - steps))
    return lax.ppermute(value, axis, [(source, source + steps) for source in range(leading, last)])


def lane_iota(rows):
    return lax.broadcasted_iota(jnp.int32, (rows, LANES), 1)


def pack_kernel(pairs, imb, flow, pot, cost, up, down, left, right):
    rows, cols = cost.shape
    group = LANES // pairs
    fields = [pot, flow.at[0], flow.at[1], imb]
    for k, field in enumerate(fields):
        for p in range(pairs):
            up[k * pairs + p] = field[p, 0:SLAB, :]
            down[k * pairs + p] = field[p, rows - SLAB : rows, :]
    up[4 * pairs] = cost[0:SLAB, :]
    down[4 * pairs] = cost[rows - SLAB : rows, :]
    lane = lane_iota(rows)
    inner = lane % group
    which = lane // group
    for k in range(5):
        first = jnp.zeros((rows, LANES), jnp.float32)
        last = jnp.zeros((rows, LANES), jnp.float32)
        for p in range(pairs):
            if k < 4:
                head, tail = fields[k][p, :, 0:LANES], fields[k][p, :, cols - LANES : cols]
            else:
                head, tail = cost[:, 0:LANES], cost[:, cols - LANES : cols]
            head = pltpu.roll(head, group * p, 1) if p else head
            shift = (group * (p + 1)) % LANES
            tail = pltpu.roll(tail, shift, 1) if shift else tail
            first = jnp.where((which == p) & (inner < DEEP), head, first)
            last = jnp.where((which == p) & (inner >= group - DEEP), tail, last)
        left[k] = first
        right[k] = last


def own_masks(pairs):
    gy, gx = lax.axis_index("gy"), lax.axis_index("gx")
    above = jnp.where(gy > 0, 1.0, 0.0).astype(jnp.float32)
    below = jnp.where(gy < lax.axis_size("gy") - 1, 1.0, 0.0).astype(jnp.float32)
    inner = lax.broadcasted_iota(jnp.int32, (1, LANES), 1) % (LANES // pairs)
    to_right = (inner < DEEP) & (gx < lax.axis_size("gx") - 1)
    to_left = (inner >= LANES // pairs - DEEP) & (gx > 0)
    sides = jnp.where(to_right | to_left, 1.0, 0.0).astype(jnp.float32)
    return above, below, sides


def assemble_kernel(
    pairs, imb, flow, pot, cost, top, bottom, side, side_top, side_bottom, u, a, b, q, source, price
):
    rows, cols = cost.shape
    per = cols // LANES
    tiles = pairs * per
    end = TOP + rows
    fields = [(u, pot), (a, flow.at[0]), (b, flow.at[1]), (source, imb)]
    for k, (into, field) in enumerate(fields):
        for t in range(tiles + 1):
            into[t, 0:PAD, :] = jnp.zeros((PAD, LANES), jnp.float32)
            into[t, end + SLAB :, :] = jnp.zeros((PAD, LANES), jnp.float32)
        for p in range(pairs):
            for c in range(per):
                t, span = p * per + c, slice(c * LANES, (c + 1) * LANES)
                into[t, PAD:TOP, :] = top[k * pairs + p, :, span]
                into[t, TOP:end, :] = field[p, :, span]
                into[t, end : end + SLAB, :] = bottom[k * pairs + p, :, span]
        into[tiles, PAD:TOP, :] = side_top[k]
        into[tiles, TOP:end, :] = side[k]
        into[tiles, end : end + SLAB, :] = side_bottom[k]
    above, below, sides = own_masks(pairs)
    outside = 1.0 - sides
    for c in range(per):
        span = slice(c * LANES, (c + 1) * LANES)
        price[c, 0:PAD, :] = jnp.ones((PAD, LANES), jnp.float32)
        price[c, end + SLAB :, :] = jnp.ones((PAD, LANES), jnp.float32)
        price[c, PAD:TOP, :] = top[4 * pairs, :, span] + (1.0 - above)
        price[c, TOP:end, :] = cost[:, span]
        price[c, end : end + SLAB, :] = bottom[4 * pairs, :, span] + (1.0 - below)
    price[per, 0:PAD, :] = jnp.ones((PAD, LANES), jnp.float32)
    price[per, end + SLAB :, :] = jnp.ones((PAD, LANES), jnp.float32)
    price[per, PAD:TOP, :] = jnp.where(sides * above > 0.0, side_top[4], 1.0)
    price[per, TOP:end, :] = side[4] + outside
    price[per, end : end + SLAB, :] = jnp.where(sides * below > 0.0, side_bottom[4], 1.0)
    for start, count in chunks(rows, SLAB):
        divergence_rows(pairs, per, start, count, a, b, q)


def chunks(rows, size):
    return [(PAD + k * size, size) for k in range((rows + 2 * SLAB) // size)]


def from_left(pairs, per, b, span):
    group = LANES // pairs
    tiles = pairs * per
    lane = lax.broadcasted_iota(jnp.int32, (span[1], LANES), 1)
    rows = pl.ds(*span)
    side = b[tiles, rows, :]
    moved_side = pltpu.roll(side, 1, 1)
    out = []
    for p in range(pairs):
        shift = (-(group * p + group - 1)) % LANES
        before = pltpu.roll(side, shift, 1) if shift else side
        for c in range(per):
            moved = pltpu.roll(b[p * per + c, rows, :], 1, 1)
            out.append(jnp.where(lane == 0, before, moved))
            before = moved
        landed = pltpu.roll(before, group * p, 1) if p else before
        moved_side = jnp.where(lane == group * p, landed, moved_side)
    return out + [moved_side]


def from_right(pairs, per, u, span):
    group = LANES // pairs
    tiles = pairs * per
    lane = lax.broadcasted_iota(jnp.int32, (span[1], LANES), 1)
    rows = pl.ds(*span)
    side = u[tiles, rows, :]
    moved_side = pltpu.roll(side, LANES - 1, 1)
    out = [None] * tiles
    for p in range(pairs):
        shift = (LANES - 1 - group * p) % LANES
        after = pltpu.roll(side, shift, 1) if shift else side
        for c in reversed(range(per)):
            moved = pltpu.roll(u[p * per + c, rows, :], LANES - 1, 1)
            out[p * per + c] = jnp.where(lane == LANES - 1, after, moved)
            after = moved
        shift = (group * p + group) % LANES
        landed = pltpu.roll(after, shift, 1) if shift else after
        moved_side = jnp.where(lane == group * p + group - 1, landed, moved_side)
    return out + [moved_side]


def divergence_rows(pairs, per, start, count, a, b, q):
    rows, earlier = pl.ds(start, count), pl.ds(start - 1, count)
    left = from_left(pairs, per, b, (start, count))
    for t in range(pairs * per + 1):
        q[t, rows, :] = a[t, rows, :] - a[t, earlier, :] + b[t, rows, :] - left[t]


def folded(value):
    return jnp.sum(value.reshape(-1, 8, LANES), axis=0)


def next_rates(recv, rates):
    total = jnp.sum(recv[...], axis=0, keepdims=True)
    primal = total + epsilon
    dual = pltpu.roll(jnp.broadcast_to(total, (8, LANES)), LANES // 2, 1)[0:1] + epsilon
    rescale = jnp.sqrt(jnp.sqrt(primal / dual))
    return rates[0:1, :] / rescale, rates[1:2, :] * rescale


def spread_rates(pairs, values):
    lane = lax.broadcasted_iota(jnp.int32, (1, LANES), 1)
    each = [jnp.sum(jnp.where(lane == p, values, 0.0)) for p in range(pairs)]
    side = jnp.zeros((1, LANES), jnp.float32)
    for p in range(pairs):
        side = jnp.where(lane // (LANES // pairs) == p, each[p], side)
    return each, side


def lanes_of(parts):
    row = lax.broadcasted_iota(jnp.int32, (8, LANES), 0)
    lane = lax.broadcasted_iota(jnp.int32, (8, LANES), 1)
    matrix = jnp.zeros((8, LANES), jnp.float32)
    where = jnp.zeros((8, LANES), jnp.int32)
    for k, (place, part) in enumerate(parts.items()):
        matrix = jnp.where(row == k, jnp.sum(part, axis=0, keepdims=True), matrix)
        where = jnp.where(row == k, place, where)
    sums = jnp.sum(matrix, axis=1, keepdims=True)
    used = row < len(parts)
    return jnp.sum(jnp.where((lane == where) & used, sums, 0.0), axis=0, keepdims=True)


def primal_rows(pairs, per, start, count, taus, tau_side, masks, price, u, a, b, a_out, b_out, sums):
    rows, later = pl.ds(start, count), pl.ds(start + 1, count)
    right = from_right(pairs, per, u, (start, count))
    row_mask, sides = masks
    for t in range(pairs * per + 1):
        if t < pairs * per:
            rate, cost = taus[t // per], price[t % per, rows, :]
            grad_rate = rate if row_mask is None else rate * row_mask
        else:
            rate, cost = tau_side, price[per, rows, :]
            grad_rate = rate * sides if row_mask is None else rate * sides * row_mask
        here = u[t, rows, :]
        old_down, old_right = a[t, rows, :], b[t, rows, :]
        down = old_down + grad_rate * (u[t, later, :] - here)
        across = old_right + grad_rate * (right[t] - here)
        square = down * down + across * across
        factor = jnp.maximum(1.0 - (rate * cost) * lax.rsqrt(square), 0.0)
        new_down, new_right = factor * down, factor * across
        a_out[t, rows, :] = new_down
        b_out[t, rows, :] = new_right
        if sums is not None and t < pairs * per:
            change_down, change_right = new_down - old_down, new_right - old_right
            p = t // per
            sums[p] = sums[p] + folded(change_down * change_down + change_right * change_right)
    return sums


def iterate_kernel(pairs, rows, recv, rates, price, source, u, a, b, q, u_out, a_out, b_out, q_out, send, rates_out):
    per = price.shape[0] - 1
    tiles = pairs * per
    tau, sigma = next_rates(recv, rates)
    rates_out[0:1, :] = tau
    rates_out[1:2, :] = sigma
    taus, tau_side = spread_rates(pairs, tau)
    sigmas, sigma_side = spread_rates(pairs, sigma)
    above, below, sides = own_masks(pairs)
    primal = [jnp.zeros((8, LANES), jnp.float32)] * pairs
    dual = [jnp.zeros((8, LANES), jnp.float32)] * pairs
    plan = [
        (start, count, above if start < TOP else below if start >= TOP + rows else None)
        for start, count in chunks(rows, SLAB)
    ]
    for start, count, mask in plan:
        found = primal_rows(
            pairs, per, start, count, taus, tau_side, (mask, sides), price, u, a, b, a_out, b_out, primal if mask is None else None
        )
        primal = primal if found is None else found
    for start, count, mask in plan:
        span, earlier = pl.ds(start, count), pl.ds(start - 1, count)
        left = from_left(pairs, per, b_out, (start, count))
        for t in range(tiles + 1):
            rate = sigmas[t // per] if t < tiles else sigma_side * sides
            rate = rate if mask is None else rate * mask
            spread = a_out[t, span, :] - a_out[t, earlier, :] + b_out[t, span, :] - left[t]
            here = u[t, span, :]
            change = rate * (2.0 * spread - q[t, span, :] - source[t, span, :])
            q_out[t, span, :] = spread
            u_out[t, span, :] = here + change
            if mask is None and t < tiles:
                p = t // per
                dual[p] = dual[p] + folded(change * change)
    parts = {p: primal[p] for p in range(pairs)} | {LANES // 2 + p: dual[p] for p in range(pairs)}
    send[...] = jnp.broadcast_to(lanes_of(parts), send.shape)


def closing_kernel(pairs, recv, rates, price, source, u, a, b, q, flow_out, pot_out, send, a_new, b_new):
    per = price.shape[0] - 1
    rows = pot_out.shape[1]
    tiles = pairs * per
    tau, sigma = next_rates(recv, rates)
    taus, tau_side = spread_rates(pairs, tau)
    sigmas, _ = spread_rates(pairs, sigma)
    above, _, sides = own_masks(pairs)
    a_new[:, 0:TOP, :] = jnp.zeros((tiles + 1, TOP, LANES), jnp.float32)
    for start, count in chunks(rows, SLAB)[:-1]:
        mask = above if start < TOP else None
        primal_rows(pairs, per, start, count, taus, tau_side, (mask, sides), price, u, a, b, a_new, b_new, None)
    short = [jnp.zeros((8, LANES), jnp.float32)] * pairs
    for start, count in chunks(rows, SLAB)[1:-1]:
        span, earlier = pl.ds(start, count), pl.ds(start - 1, count)
        left = from_left(pairs, per, b_new, (start, count))
        own = slice(start - TOP, start - TOP + count)
        for t in range(tiles):
            p, c = t // per, t % per
            lanes = slice(c * LANES, (c + 1) * LANES)
            new_down, new_right = a_new[t, span, :], b_new[t, span, :]
            spread = new_down - a_new[t, earlier, :] + new_right - left[t]
            imbalance = source[t, span, :]
            missing = spread - imbalance
            flow_out[0, p, own, lanes] = new_down
            flow_out[1, p, own, lanes] = new_right
            pot_out[p, own, lanes] = u[t, span, :] + sigmas[p] * (2.0 * spread - q[t, span, :] - imbalance)
            short[p] = short[p] + folded(missing * missing)
    send[...] = jnp.broadcast_to(lanes_of({p: short[p] for p in range(pairs)}), send.shape)


def call(kernel, out_shape, operands, aliases=None, scratch=(), limit=24):
    vmem = pl.BlockSpec(memory_space=pltpu.VMEM)
    return pl.pallas_call(
        kernel,
        out_shape=out_shape,
        in_specs=[vmem] * len(operands),
        out_specs=jax.tree.map(lambda _: vmem, out_shape),
        input_output_aliases=aliases or {},
        scratch_shapes=list(scratch),
        compiler_params=pltpu.CompilerParams(vmem_limit_bytes=limit << 20),
    )(*operands)


def shape(*dims):
    return jax.ShapeDtypeStruct(dims, jnp.float32)


def exchange(send):
    return lax.all_to_all(send, AXES, 0, 0, tiled=True)


def local(imbalance, flow, potential, cost):
    pairs, rows, cols = imbalance.shape
    per = cols // LANES
    tiles = pairs * per
    height = rows + 2 * TOP
    devices = lax.axis_size("gy") * lax.axis_size("gx")

    slab, edge = shape(4 * pairs + 1, SLAB, cols), shape(5, rows, LANES)
    up, down, left, right = call(
        functools.partial(pack_kernel, pairs), [slab, slab, edge, edge], [imbalance, flow, potential, cost]
    )
    bottom, top = neighbour(up, "gy", -1), neighbour(down, "gy", 1)
    side = neighbour(left, "gx", -1) + neighbour(right, "gx", 1)
    side_bottom = neighbour(side[:, :SLAB], "gy", -1)
    side_top = neighbour(side[:, rows - SLAB :], "gy", 1)

    field = shape(tiles + 1, height, LANES)
    u, a, b, q, source, price = call(
        functools.partial(assemble_kernel, pairs),
        [field] * 5 + [shape(per + 1, height, LANES)],
        [imbalance, flow, potential, cost, top, bottom, side, side_top, side_bottom],
        limit=32,
    )
    rates = jnp.full((8, LANES), initial_step, jnp.float32)
    recv = jnp.zeros((devices, LANES), jnp.float32)

    def turn(_, carried):
        u, a, b, q, recv, rates = carried
        u, a, b, q, send, rates = call(
            functools.partial(iterate_kernel, pairs, rows),
            [field] * 4 + [shape(devices, LANES), shape(8, LANES)],
            [recv, rates, price, source, u, a, b, q],
            aliases={4: 0, 5: 1, 6: 2, 7: 3, 1: 5},
        )
        return u, a, b, q, exchange(send), rates

    u, a, b, q, recv, rates = lax.fori_loop(0, ITERS - 1, turn, (u, a, b, q, recv, rates))
    new = pltpu.VMEM((tiles + 1, height, LANES), jnp.float32)
    flow_out, pot_out, send = call(
        functools.partial(closing_kernel, pairs),
        [shape(2, pairs, rows, cols), shape(pairs, rows, cols), shape(devices, LANES)],
        [recv, rates, price, source, u, a, b, q],
        scratch=[new, new],
    )
    cells = rows * lax.axis_size("gy") * cols * lax.axis_size("gx")
    residual = jnp.sum(exchange(send), axis=0)[:pairs] / cells
    return flow_out, pot_out, residual


def solution(mesh):
    placed = (P(None, "gy", "gx"), P(None, None, "gy", "gx"), P(None, "gy", "gx"), P("gy", "gx"))
    return jax.shard_map(
        local,
        mesh=mesh,
        in_specs=placed,
        out_specs=(P(None, None, "gy", "gx"), P(None, "gy", "gx"), P()),
        check_vma=False,
    )
```

time: 891 us -> 294 us (0.33)
  blocking collectives: 484 us -> 8.85 us
  other arithmetic: 131 us -> 0.6 us
  Pallas kernels: 0 us -> 130 us
  local copies, waits for them, and re-layouts: 132 us -> 7.8 us
  waiting for transfers between devices: 19.6 us -> 95.6 us
  starting transfers between devices: 118 us -> 49.3 us
    psum x12 -> x0, blocking collectives: 484 us -> none  [the longest x11 442 us: iterate(): lax.psum((primal_local, dual_local), ('gy', 'gx'))]
    pallas_call x0 -> x14, Pallas kernels: none -> 130 us  [call(): pl.pallas_call(kernel, out_shape=out_shape, in_specs=[vmem] * len(operand...]
    ppermute x50 -> x6, starting transfers between devices: 118 us -> 17.9 us  [neighbour(): lax.ppermute(value, axis, [(source, source + steps) for source in range(l...]
    slice x75 -> x1, local copies, waits for them, and re-layouts: 88.3 us -> 0.64 us  [local(): side_bottom = neighbour(side[:, :SLAB], 'gy', -1)]
    all_to_all x0 -> x11, waiting for transfers between devices: none -> 78.1 us  [exchange(): return lax.all_to_all(send, AXES, 0, 0, tiled=True)]
    reduce_sum x23 -> x1, other arithmetic: 76.7 us -> 0.05 us  [local(): residual = jnp.sum(exchange(send), axis=0)[:pairs] / cells]
    div x23 -> x1, other arithmetic: 42.8 us -> 0.52 us  [local(): residual = jnp.sum(exchange(send), axis=0)[:pairs] / cells]
    broadcast_in_dim x27 -> x2, local copies, waits for them, and re-layouts: 32 us -> 0.01 us  [the longest x1 0.01 us: local(): recv = jnp.zeros((devices, LANES), jnp.float32)]
  transfers between devices with their start and end apart: 50 -> 17, of which waited for: 11 -> 13; matrix products, arithmetic and copies ran while one was open for 11% -> 0% of each run, Pallas kernels for 0% -> 0%
where the time goes in v1:
time: 294 us; the launch traced here: 293 us
  Pallas kernels  130 us (44%)
  waiting for transfers between devices  95.6 us (33%)
  starting transfers between devices  49.3 us (17%)
  blocking collectives  8.85 us (3%)
  local copies, waits for them, and re-layouts  7.8 us (3%)
    pallas_call x14, Pallas kernels, call(): pl.pallas_call(kernel, out_shape=out_shape, in_specs=[vmem] * len(operand...  130 us
    all_to_all x11, waiting for transfers between devices, exchange(): return lax.all_to_all(send, AXES, 0, 0, tiled=True)  78.1 us
    all_to_all x11, starting transfers between devices, exchange(): return lax.all_to_all(send, AXES, 0, 0, tiled=True)  31.4 us
    ppermute x6, starting transfers between devices, neighbour(): lax.ppermute(value, axis, [(source, source + steps) for source in range(l...  17.9 us
    ppermute x6, waiting for transfers between devices, neighbour(): lax.ppermute(value, axis, [(source, source + steps) for source in range(l...  17.5 us
    all_to_all x1, blocking collectives, exchange(): return lax.all_to_all(send, AXES, 0, 0, tiled=True)  8.85 us
    unnamed x16, local copies, waits for them, and re-layouts  7.16 us
  transfers between devices with their start and end apart: 17, of which 13 were waited for; matrix products, arithmetic and copies ran while one was open for 0% of the time, Pallas kernels for 0%

profile of v1, /device:TPU:0, one launch (start us, length us, event | category | flops | bytes accessed | tf_op | source)
XLA Modules:
  0.0 293.4 jit_solution(17645796217717423877)
XLA Ops:
  25.8 9.9 %collective-permute-done.5.side_bottom = f32[5,16,128]{2,1,0:T(8,128)S(1)} collective-permute-done((f32[5,16,128]{2,1,0:T(8,128)}, f32[5,16,128]{2,1,0:T(8,128)S(1)}, u32[]{:S(2)}, u32[]{:S(2)}) %collective-permute-start.5) | collective-permute-done | bytes 40992 | tf_op jit(solution)/shard_map/ppermute | solution.py:25
  35.7 7.7 %collective-permute-done.4.side_top = f32[5,16,128]{2,1,0:T(8,128)S(1)} collective-permute-done((f32[5,16,128]{2,1,0:T(8,128)}, f32[5,16,128]{2,1,0:T(8,128)S(1)}, u32[]{:S(2)}, u32[]{:S(2)}) %collective-permute-start.4) | collective-permute-done | bytes 40992 | tf_op jit(solution)/shard_map/ppermute | solution.py:25
  51.9 224.4 %while.20 = (s32[]{:T(128)}, f32[17,176,128]{2,1,0:T(8,128)}, f32[17,176,128]{2,1,0:T(8,128)}, f32[17,176,128]{2,1,0:T(8,128)}, f32[17,176,128]{2,1,0:T(8,128)},...) while((s32[]{:T(128)}, f32[17,176,128]{2,1,0:T(8,128)}, ...), condition=%wide.region_1.0_spmd, body=%wide.region_0.0_spmd.sunk | while | flops 2 | bytes 49285 | solution.py:351
  51.9 10.4 %eval_jaxpr.1 = (f32[17,176,128]{2,1,0:T(8,128)}, f32[17,176,128]{2,1,0:T(8,128)}, f32[17,176,128]{2,1,0:T(8,128)}, f32[17,176,128]{2,1,0:T(8,128)}, f32[32,128]{1,0:T(8,128)}, /*index=5*/f32[8,128]{1,0:T(8,128)S(1)}) custom-call(f32[32,128]{1,0:T(8,128)S(1)} %get-tuple-element.195.rec, ...), custom_call_target="tpu_custom_call", output_to_operand_aliasing={{0}: (4, {}), {1}: (5, {}), {2}: (6, {}), {3}: (7, {}), {5}... | custom-call | tf_op jit(solution)/shard_map/while/body/eval_jaxpr/pallas_call | solution.py:296
  68.3 7.1 %all-to-all-done = f32[32,1,128]{2,1,0:T(1,128)S(1)} async-done(((f32[32,1,128]{2,1,0:T(1,128)}), f32[32,1,128]{2,1,0:T(1,128)S(1)}, u32[]{:S(2)}, u32[]{:S(2)}) %all-to-all-start) | async-done | bytes 16416 | tf_op jit(solution)/shard_map/while/body/eval_jaxpr/all_to_all | solution.py:312
  75.4 10.4 %eval_jaxpr.1 = (f32[17,176,128]{2,1,0:T(8,128)}, f32[17,176,128]{2,1,0:T(8,128)}, f32[17,176,128]{2,1,0:T(8,128)}, f32[17,176,128]{2,1,0:T(8,128)}, f32[32,128]{1,0:T(8,128)}, /*index=5*/f32[8,128]{1,0:T(8,128)S(1)}) custom-call(f32[32,128]{1,0:T(8,128)S(1)} %get-tuple-element.195.rec, ...), custom_call_target="tpu_custom_call", output_to_operand_aliasing={{0}: (4, {}), {1}: (5, {}), {2}: (6, {}), {3}: (7, {}), {5}... | custom-call | tf_op jit(solution)/shard_map/while/body/eval_jaxpr/pallas_call | solution.py:296
  88.4 7.1 %all-to-all-done = f32[32,1,128]{2,1,0:T(1,128)S(1)} async-done(((f32[32,1,128]{2,1,0:T(1,128)}), f32[32,1,128]{2,1,0:T(1,128)S(1)}, u32[]{:S(2)}, u32[]{:S(2)}) %all-to-all-start) | async-done | bytes 16416 | tf_op jit(solution)/shard_map/while/body/eval_jaxpr/all_to_all | solution.py:312
  95.5 10.4 %eval_jaxpr.1 = (f32[17,176,128]{2,1,0:T(8,128)}, f32[17,176,128]{2,1,0:T(8,128)}, f32[17,176,128]{2,1,0:T(8,128)}, f32[17,176,128]{2,1,0:T(8,128)}, f32[32,128]{1,0:T(8,128)}, /*index=5*/f32[8,128]{1,0:T(8,128)S(1)}) custom-call(f32[32,128]{1,0:T(8,128)S(1)} %get-tuple-element.195.rec, ...), custom_call_target="tpu_custom_call", output_to_operand_aliasing={{0}: (4, {}), {1}: (5, {}), {2}: (6, {}), {3}: (7, {}), {5}... | custom-call | tf_op jit(solution)/shard_map/while/body/eval_jaxpr/pallas_call | solution.py:296
  108.5 7.1 %all-to-all-done = f32[32,1,128]{2,1,0:T(1,128)S(1)} async-done(((f32[32,1,128]{2,1,0:T(1,128)}), f32[32,1,128]{2,1,0:T(1,128)S(1)}, u32[]{:S(2)}, u32[]{:S(2)}) %all-to-all-start) | async-done | bytes 16416 | tf_op jit(solution)/shard_map/while/body/eval_jaxpr/all_to_all | solution.py:312
  115.6 10.4 %eval_jaxpr.1 = (f32[17,176,128]{2,1,0:T(8,128)}, f32[17,176,128]{2,1,0:T(8,128)}, f32[17,176,128]{2,1,0:T(8,128)}, f32[17,176,128]{2,1,0:T(8,128)}, f32[32,128]{1,0:T(8,128)}, /*index=5*/f32[8,128]{1,0:T(8,128)S(1)}) custom-call(f32[32,128]{1,0:T(8,128)S(1)} %get-tuple-element.195.rec, ...), custom_call_target="tpu_custom_call", output_to_operand_aliasing={{0}: (4, {}), {1}: (5, {}), {2}: (6, {}), {3}: (7, {}), {5}... | custom-call | tf_op jit(solution)/shard_map/while/body/eval_jaxpr/pallas_call | solution.py:296
  128.6 7.1 %all-to-all-done = f32[32,1,128]{2,1,0:T(1,128)S(1)} async-done(((f32[32,1,128]{2,1,0:T(1,128)}), f32[32,1,128]{2,1,0:T(1,128)S(1)}, u32[]{:S(2)}, u32[]{:S(2)}) %all-to-all-start) | async-done | bytes 16416 | tf_op jit(solution)/shard_map/while/body/eval_jaxpr/all_to_all | solution.py:312
  135.7 10.4 %eval_jaxpr.1 = (f32[17,176,128]{2,1,0:T(8,128)}, f32[17,176,128]{2,1,0:T(8,128)}, f32[17,176,128]{2,1,0:T(8,128)}, f32[17,176,128]{2,1,0:T(8,128)}, f32[32,128]{1,0:T(8,128)}, /*index=5*/f32[8,128]{1,0:T(8,128)S(1)}) custom-call(f32[32,128]{1,0:T(8,128)S(1)} %get-tuple-element.195.rec, ...), custom_call_target="tpu_custom_call", output_to_operand_aliasing={{0}: (4, {}), {1}: (5, {}), {2}: (6, {}), {3}: (7, {}), {5}... | custom-call | tf_op jit(solution)/shard_map/while/body/eval_jaxpr/pallas_call | solution.py:296
  148.7 7.1 %all-to-all-done = f32[32,1,128]{2,1,0:T(1,128)S(1)} async-done(((f32[32,1,128]{2,1,0:T(1,128)}), f32[32,1,128]{2,1,0:T(1,128)S(1)}, u32[]{:S(2)}, u32[]{:S(2)}) %all-to-all-start) | async-done | bytes 16416 | tf_op jit(solution)/shard_map/while/body/eval_jaxpr/all_to_all | solution.py:312
  155.8 10.4 %eval_jaxpr.1 = (f32[17,176,128]{2,1,0:T(8,128)}, f32[17,176,128]{2,1,0:T(8,128)}, f32[17,176,128]{2,1,0:T(8,128)}, f32[17,176,128]{2,1,0:T(8,128)}, f32[32,128]{1,0:T(8,128)}, /*index=5*/f32[8,128]{1,0:T(8,128)S(1)}) custom-call(f32[32,128]{1,0:T(8,128)S(1)} %get-tuple-element.195.rec, ...), custom_call_target="tpu_custom_call", output_to_operand_aliasing={{0}: (4, {}), {1}: (5, {}), {2}: (6, {}), {3}: (7, {}), {5}... | custom-call | tf_op jit(solution)/shard_map/while/body/eval_jaxpr/pallas_call | solution.py:296
  168.8 7.1 %all-to-all-done = f32[32,1,128]{2,1,0:T(1,128)S(1)} async-done(((f32[32,1,128]{2,1,0:T(1,128)}), f32[32,1,128]{2,1,0:T(1,128)S(1)}, u32[]{:S(2)}, u32[]{:S(2)}) %all-to-all-start) | async-done | bytes 16416 | tf_op jit(solution)/shard_map/while/body/eval_jaxpr/all_to_all | solution.py:312
  175.9 10.4 %eval_jaxpr.1 = (f32[17,176,128]{2,1,0:T(8,128)}, f32[17,176,128]{2,1,0:T(8,128)}, f32[17,176,128]{2,1,0:T(8,128)}, f32[17,176,128]{2,1,0:T(8,128)}, f32[32,128]{1,0:T(8,128)}, /*index=5*/f32[8,128]{1,0:T(8,128)S(1)}) custom-call(f32[32,128]{1,0:T(8,128)S(1)} %get-tuple-element.195.rec, ...), custom_call_target="tpu_custom_call", output_to_operand_aliasing={{0}: (4, {}), {1}: (5, {}), {2}: (6, {}), {3}: (7, {}), {5}... | custom-call | tf_op jit(solution)/shard_map/while/body/eval_jaxpr/pallas_call | solution.py:296
  188.9 7.1 %all-to-all-done = f32[32,1,128]{2,1,0:T(1,128)S(1)} async-done(((f32[32,1,128]{2,1,0:T(1,128)}), f32[32,1,128]{2,1,0:T(1,128)S(1)}, u32[]{:S(2)}, u32[]{:S(2)}) %all-to-all-start) | async-done | bytes 16416 | tf_op jit(solution)/shard_map/while/body/eval_jaxpr/all_to_all | solution.py:312
  196.0 10.4 %eval_jaxpr.1 = (f32[17,176,128]{2,1,0:T(8,128)}, f32[17,176,128]{2,1,0:T(8,128)}, f32[17,176,128]{2,1,0:T(8,128)}, f32[17,176,128]{2,1,0:T(8,128)}, f32[32,128]{1,0:T(8,128)}, /*index=5*/f32[8,128]{1,0:T(8,128)S(1)}) custom-call(f32[32,128]{1,0:T(8,128)S(1)} %get-tuple-element.195.rec, ...), custom_call_target="tpu_custom_call", output_to_operand_aliasing={{0}: (4, {}), {1}: (5, {}), {2}: (6, {}), {3}: (7, {}), {5}... | custom-call | tf_op jit(solution)/shard_map/while/body/eval_jaxpr/pallas_call | solution.py:296
  209.0 7.1 %all-to-all-done = f32[32,1,128]{2,1,0:T(1,128)S(1)} async-done(((f32[32,1,128]{2,1,0:T(1,128)}), f32[32,1,128]{2,1,0:T(1,128)S(1)}, u32[]{:S(2)}, u32[]{:S(2)}) %all-to-all-start) | async-done | bytes 16416 | tf_op jit(solution)/shard_map/while/body/eval_jaxpr/all_to_all | solution.py:312
  216.1 10.4 %eval_jaxpr.1 = (f32[17,176,128]{2,1,0:T(8,128)}, f32[17,176,128]{2,1,0:T(8,128)}, f32[17,176,128]{2,1,0:T(8,128)}, f32[17,176,128]{2,1,0:T(8,128)}, f32[32,128]{1,0:T(8,128)}, /*index=5*/f32[8,128]{1,0:T(8,128)S(1)}) custom-call(f32[32,128]{1,0:T(8,128)S(1)} %get-tuple-element.195.rec, ...), custom_call_target="tpu_custom_call", output_to_operand_aliasing={{0}: (4, {}), {1}: (5, {}), {2}: (6, {}), {3}: (7, {}), {5}... | custom-call | tf_op jit(solution)/shard_map/while/body/eval_jaxpr/pallas_call | solution.py:296
  236.2 10.4 %eval_jaxpr.1 = (f32[17,176,128]{2,1,0:T(8,128)}, f32[17,176,128]{2,1,0:T(8,128)}, f32[17,176,128]{2,1,0:T(8,128)}, f32[17,176,128]{2,1,0:T(8,128)}, f32[32,128]{1,0:T(8,128)}, /*index=5*/f32[8,128]{1,0:T(8,128)S(1)}) custom-call(f32[32,128]{1,0:T(8,128)S(1)} %get-tuple-element.195.rec, ...), custom_call_target="tpu_custom_call", output_to_operand_aliasing={{0}: (4, {}), {1}: (5, {}), {2}: (6, {}), {3}: (7, {}), {5}... | custom-call | tf_op jit(solution)/shard_map/while/body/eval_jaxpr/pallas_call | solution.py:296
  256.2 10.4 %eval_jaxpr.1 = (f32[17,176,128]{2,1,0:T(8,128)}, f32[17,176,128]{2,1,0:T(8,128)}, f32[17,176,128]{2,1,0:T(8,128)}, f32[17,176,128]{2,1,0:T(8,128)}, f32[32,128]{1,0:T(8,128)}, /*index=5*/f32[8,128]{1,0:T(8,128)S(1)}) custom-call(f32[32,128]{1,0:T(8,128)S(1)} %get-tuple-element.195.rec, ...), custom_call_target="tpu_custom_call", output_to_operand_aliasing={{0}: (4, {}), {1}: (5, {}), {2}: (6, {}), {3}: (7, {}), {5}... | custom-call | tf_op jit(solution)/shard_map/while/body/eval_jaxpr/pallas_call | solution.py:296
  276.3 7.6 %shard_map.69 = (f32[2,4,128,512]{3,2,1,0:T(8,128)}, f32[4,128,512]{2,1,0:T(8,128)}, f32[32,128]{1,0:T(8,128)S(1)}) custom-call(f32[32,128]{1,0:T(8,128)S(1)} %get-tuple-element.84.recv, f32[8,128]{1,0:T(8,128)S(1)} %get-tuple-element.85.rates, f32[5,176,128]{2,1,0:T(8,128)} %get-tuple-element.215, f32[17,176,128]{2,1,0:T(8,128)} %get-tuple-element.214, ...), custom_call_target="tpu_custom_call" | custom-call | tf_op jit(solution)/shard_map/pallas_call | solution.py:296
  283.9 8.9 %all_to_all.20 = f32[32,1,128]{2,1,0:T(1,128)S(1)} all-to-all(f32[32,1,128]{2,1,0:T(1,128)S(1)} %bitcast.11), channel_id=1, replica_groups=mesh['gy'=8,'gx'=4] {'gy','gx'}, dimensions={0} | all-to-all | bytes 32768 | tf_op jit(solution)/shard_map/all_to_all | solution.py:312
  (48 shorter events, 86.9 us)
Async XLA Ops:
  0.6 1.6 copy-start
  2.2 1.2 copy-start.2
  3.4 1.2 copy-start.4
  4.7 0.9 copy-start.6
  5.6 37.7 %copy-start.1 = (f32[2,4,128,512]{3,2,1,0:T(8,128)S(1)}, f32[2,4,128,512]{3,2,1,0:T(8,128)}, u32[]{:S(2)}) copy-start(f32[2,4,128,512]{3,2,1,0:T(8,128)} %flow.3) | copy-start | bytes 6291460
  7.1 36.2 %copy-start.3 = (f32[4,128,512]{2,1,0:T(8,128)S(1)}, f32[4,128,512]{2,1,0:T(8,128)}, u32[]{:S(2)}) copy-start(f32[4,128,512]{2,1,0:T(8,128)} %imb.3) | copy-start | bytes 3145732
  7.1 11.5 %collective-permute-start.2 = (f32[5,128,128]{2,1,0:T(8,128)S(1)}, f32[5,128,128]{2,1,0:T(8,128)S(1)}, u32[]{:S(2)}, u32[]{:S(2)}) collective-permute-start(f32[5,128,128]{2,1,0:T(8,128)S(1)} %get-tuple-element.76), channel_id=1, source_target_pairs={{1,0},{2,1},{3,2},{5,4},{6,5},{7,6},{9,8},{10,9},{11,10},{13,12},{... | collective-permute-start | bytes 983048 | tf_op jit(solution)/shard_map/ppermute | solution.py:25
  8.5 10.1 %collective-permute-start.3 = (f32[5,128,128]{2,1,0:T(8,128)S(1)}, f32[5,128,128]{2,1,0:T(8,128)S(1)}, u32[]{:S(2)}, u32[]{:S(2)}) collective-permute-start(f32[5,128,128]{2,1,0:T(8,128)S(1)} %get-tuple-element.77), channel_id=1, source_target_pairs={{0,1},{1,2},{2,3},{4,5},{5,6},{6,7},{8,9},{9,10},{10,11},{12,13},{... | collective-permute-start | bytes 983048 | tf_op jit(solution)/shard_map/ppermute | solution.py:25
  11.6 31.7 %collective-permute-start = (f32[17,16,512]{2,1,0:T(8,128)}, f32[17,16,512]{2,1,0:T(8,128)}, u32[]{:S(2)}, u32[]{:S(2)}) collective-permute-start(f32[17,16,512]{2,1,0:T(8,128)} %get-tuple-element.74), channel_id=1, source_target_pairs={{0,4},{4,8},{8,12},{12,16},{16,20},{20,24},{24,28},{1,5},{5,9},{9,... | collective-permute-start | bytes 1671176 | tf_op jit(solution)/shard_map/ppermute | solution.py:25
  17.3 26.0 %collective-permute-start.1 = (f32[17,16,512]{2,1,0:T(8,128)}, f32[17,16,512]{2,1,0:T(8,128)}, u32[]{:S(2)}, u32[]{:S(2)}) collective-permute-start(f32[17,16,512]{2,1,0:T(8,128)} %get-tuple-element.75), channel_id=1, source_target_pairs={{4,0},{8,4},{12,8},{16,12},{20,16},{24,20},{28,24},{5,1},{9,5},{13... | collective-permute-start | bytes 1671176 | tf_op jit(solution)/shard_map/ppermute | solution.py:25
  19.3 16.4 %collective-permute-start.5 = (f32[5,16,128]{2,1,0:T(8,128)}, f32[5,16,128]{2,1,0:T(8,128)S(1)}, u32[]{:S(2)}, u32[]{:S(2)}) collective-permute-start(f32[5,16,128]{2,1,0:T(8,128)} %get-tuple-element.111), channel_id=1, source_target_pairs={{4,0},{8,4},{12,8},{16,12},{20,16},{24,20},{28,24},{5,1},{9,5},{13... | collective-permute-start | bytes 122888 | tf_op jit(solution)/shard_map/ppermute | solution.py:25
  20.6 22.7 %collective-permute-start.4 = (f32[5,16,128]{2,1,0:T(8,128)}, f32[5,16,128]{2,1,0:T(8,128)S(1)}, u32[]{:S(2)}, u32[]{:S(2)}) collective-permute-start(f32[5,16,128]{2,1,0:T(8,128)} %get-tuple-element.112), channel_id=1, source_target_pairs={{0,4},{4,8},{8,12},{12,16},{16,20},{20,24},{24,28},{1,5},{5,9},{9,... | collective-permute-start | bytes 122888 | tf_op jit(solution)/shard_map/ppermute | solution.py:25
  43.4 1.2 copy-start.5
  62.4 13.0 %all-to-all-start = ((f32[32,1,128]{2,1,0:T(1,128)}), f32[32,1,128]{2,1,0:T(1,128)S(1)}, u32[]{:S(2)}, u32[]{:S(2)}) async-start(f32[32,1,128]{2,1,0:T(1,128)} %bitcast.9), calls=%async_computation | async-start | bytes 32768 | tf_op jit(solution)/shard_map/while/body/eval_jaxpr/all_to_all | solution.py:312
  85.8 9.7 %all-to-all-start = ((f32[32,1,128]{2,1,0:T(1,128)}), f32[32,1,128]{2,1,0:T(1,128)S(1)}, u32[]{:S(2)}, u32[]{:S(2)}) async-start(f32[32,1,128]{2,1,0:T(1,128)} %bitcast.9), calls=%async_computation | async-start | bytes 32768 | tf_op jit(solution)/shard_map/while/body/eval_jaxpr/all_to_all | solution.py:312
  105.9 9.7 %all-to-all-start = ((f32[32,1,128]{2,1,0:T(1,128)}), f32[32,1,128]{2,1,0:T(1,128)S(1)}, u32[]{:S(2)}, u32[]{:S(2)}) async-start(f32[32,1,128]{2,1,0:T(1,128)} %bitcast.9), calls=%async_computation | async-start | bytes 32768 | tf_op jit(solution)/shard_map/while/body/eval_jaxpr/all_to_all | solution.py:312
  126.0 9.7 %all-to-all-start = ((f32[32,1,128]{2,1,0:T(1,128)}), f32[32,1,128]{2,1,0:T(1,128)S(1)}, u32[]{:S(2)}, u32[]{:S(2)}) async-start(f32[32,1,128]{2,1,0:T(1,128)} %bitcast.9), calls=%async_computation | async-start | bytes 32768 | tf_op jit(solution)/shard_map/while/body/eval_jaxpr/all_to_all | solution.py:312
  146.1 9.7 %all-to-all-start = ((f32[32,1,128]{2,1,0:T(1,128)}), f32[32,1,128]{2,1,0:T(1,128)S(1)}, u32[]{:S(2)}, u32[]{:S(2)}) async-start(f32[32,1,128]{2,1,0:T(1,128)} %bitcast.9), calls=%async_computation | async-start | bytes 32768 | tf_op jit(solution)/shard_map/while/body/eval_jaxpr/all_to_all | solution.py:312
  166.2 9.7 %all-to-all-start = ((f32[32,1,128]{2,1,0:T(1,128)}), f32[32,1,128]{2,1,0:T(1,128)S(1)}, u32[]{:S(2)}, u32[]{:S(2)}) async-start(f32[32,1,128]{2,1,0:T(1,128)} %bitcast.9), calls=%async_computation | async-start | bytes 32768 | tf_op jit(solution)/shard_map/while/body/eval_jaxpr/all_to_all | solution.py:312
  186.3 9.7 %all-to-all-start = ((f32[32,1,128]{2,1,0:T(1,128)}), f32[32,1,128]{2,1,0:T(1,128)S(1)}, u32[]{:S(2)}, u32[]{:S(2)}) async-start(f32[32,1,128]{2,1,0:T(1,128)} %bitcast.9), calls=%async_computation | async-start | bytes 32768 | tf_op jit(solution)/shard_map/while/body/eval_jaxpr/all_to_all | solution.py:312
  206.4 9.7 %all-to-all-start = ((f32[32,1,128]{2,1,0:T(1,128)}), f32[32,1,128]{2,1,0:T(1,128)S(1)}, u32[]{:S(2)}, u32[]{:S(2)}) async-start(f32[32,1,128]{2,1,0:T(1,128)} %bitcast.9), calls=%async_computation | async-start | bytes 32768 | tf_op jit(solution)/shard_map/while/body/eval_jaxpr/all_to_all | solution.py:312
  226.5 9.7 %all-to-all-start = ((f32[32,1,128]{2,1,0:T(1,128)}), f32[32,1,128]{2,1,0:T(1,128)S(1)}, u32[]{:S(2)}, u32[]{:S(2)}) async-start(f32[32,1,128]{2,1,0:T(1,128)} %bitcast.9), calls=%async_computation | async-start | bytes 32768 | tf_op jit(solution)/shard_map/while/body/eval_jaxpr/all_to_all | solution.py:312
  246.6 9.7 %all-to-all-start = ((f32[32,1,128]{2,1,0:T(1,128)}), f32[32,1,128]{2,1,0:T(1,128)S(1)}, u32[]{:S(2)}, u32[]{:S(2)}) async-start(f32[32,1,128]{2,1,0:T(1,128)} %bitcast.9), calls=%async_computation | async-start | bytes 32768 | tf_op jit(solution)/shard_map/while/body/eval_jaxpr/all_to_all | solution.py:312
  266.7 9.7 %all-to-all-start = ((f32[32,1,128]{2,1,0:T(1,128)}), f32[32,1,128]{2,1,0:T(1,128)S(1)}, u32[]{:S(2)}, u32[]{:S(2)}) async-start(f32[32,1,128]{2,1,0:T(1,128)} %bitcast.9), calls=%async_computation | async-start | bytes 32768 | tf_op jit(solution)/shard_map/while/body/eval_jaxpr/all_to_all | solution.py:312
  (1 other events, 0.9 us)

commit v2 on v1

v2 whole, which is shorter than its diff:
```python
import functools

import jax
import jax.numpy as jnp
from jax import lax
from jax.experimental import pallas as pl
from jax.experimental.pallas import tpu as pltpu
from jax.sharding import PartitionSpec as P

ITERS = 12
initial_step = 0.35
epsilon = 1e-06

DEPTH = 4
SIDE = ITERS
SLAB = 8
PAD = 8
TOP = PAD + SLAB
LANES = 128
CHUNK = 16
AXES = ("gy", "gx")


def neighbour(value, axis, steps):
    count = lax.axis_size(axis)
    leading, last = (max(0, -steps), min(count, count - steps))
    return lax.ppermute(value, axis, [(source, source + steps) for source in range(leading, last)])


def rolled(value, shift):
    shift = shift % LANES
    return pltpu.roll(value, shift, 1) if shift else value


def pack_kernel(pairs, imb, flow, pot, cost, up, down, left, right, top, bottom, first, last, sems):
    rows, cols = cost.shape
    per, group = cols // LANES, LANES // pairs
    tiles = pairs * per
    fields = [pot, flow.at[0], flow.at[1], imb]
    copies = []

    def fetch(source, target):
        copies.append(pltpu.make_async_copy(source, target, sems.at[len(copies)]))

    for k, field in enumerate(fields):
        fetch(field.at[:, 0:SLAB, :], top.at[pl.ds(k * pairs, pairs)])
        fetch(field.at[:, rows - SLAB : rows, :], bottom.at[pl.ds(k * pairs, pairs)])
    fetch(cost.at[0:SLAB, :], top.at[4 * pairs])
    fetch(cost.at[rows - SLAB : rows, :], bottom.at[4 * pairs])
    slabs = len(copies)
    for k, field in enumerate(fields):
        fetch(field.at[:, :, 0:LANES], first.at[pl.ds(k * pairs, pairs)])
        fetch(field.at[:, :, cols - LANES : cols], last.at[pl.ds(k * pairs, pairs)])
    fetch(cost.at[:, 0:LANES], first.at[4 * pairs])
    fetch(cost.at[:, cols - LANES : cols], last.at[4 * pairs])
    for copy in copies:
        copy.start()
    for copy in copies[:slabs]:
        copy.wait()
    for n in range(4 * pairs + 1):
        for c in range(per):
            span = slice(c * LANES, (c + 1) * LANES)
            up[n * per + c] = top[n, 0:DEPTH, span]
            down[n * per + c] = bottom[n, SLAB - DEPTH : SLAB, span]
    for copy in copies[slabs:]:
        copy.wait()
    count = 32
    lane = lax.broadcasted_iota(jnp.int32, (count, LANES), 1)
    inner, which = lane % group, lane // group
    for k in range(5):
        for start in range(0, rows, count):
            span = slice(start, start + count)
            head = jnp.zeros((count, LANES), jnp.float32)
            tail = jnp.zeros((count, LANES), jnp.float32)
            for p in range(pairs):
                n = min(k * pairs + p, 4 * pairs)
                head = jnp.where((which == p) & (inner < SIDE), rolled(first[n, span, :], group * p), head)
                tail = jnp.where((which == p) & (inner >= group - SIDE), rolled(last[n, span, :], group * (p + 1)), tail)
            left[k, span, :] = head
            right[k, span, :] = tail


def own_masks(pairs):
    gy, gx = lax.axis_index("gy"), lax.axis_index("gx")
    above = jnp.where(gy > 0, 1.0, 0.0).astype(jnp.float32)
    below = jnp.where(gy < lax.axis_size("gy") - 1, 1.0, 0.0).astype(jnp.float32)
    inner = lax.broadcasted_iota(jnp.int32, (1, LANES), 1) % (LANES // pairs)
    to_right = (inner < SIDE) & (gx < lax.axis_size("gx") - 1)
    to_left = (inner >= LANES // pairs - SIDE) & (gx > 0)
    sides = jnp.where(to_right | to_left, 1.0, 0.0).astype(jnp.float32)
    return above, below, sides


def assemble_kernel(
    pairs, imb, flow, pot, cost, top, bottom, side, side_top, side_bottom, u, a, b, q, source, price
):
    rows, cols = cost.shape
    per = cols // LANES
    tiles = pairs * per
    end = TOP + rows
    fields = [(u, pot), (a, flow.at[0]), (b, flow.at[1]), (source, imb)]
    for k, (into, field) in enumerate(fields):
        into[:, 0 : TOP - DEPTH, :] = jnp.zeros((tiles + 1, TOP - DEPTH, LANES), jnp.float32)
        into[:, end + DEPTH :, :] = jnp.zeros((tiles + 1, TOP - DEPTH, LANES), jnp.float32)
        into[0:tiles, TOP - DEPTH : TOP, :] = top[k * tiles : (k + 1) * tiles]
        into[0:tiles, end : end + DEPTH, :] = bottom[k * tiles : (k + 1) * tiles]
        for p in range(pairs):
            for c in range(per):
                into[p * per + c, TOP:end, :] = field[p, :, c * LANES : (c + 1) * LANES]
        into[tiles, TOP - DEPTH : TOP, :] = side_top[k]
        into[tiles, TOP:end, :] = side[k]
        into[tiles, end : end + DEPTH, :] = side_bottom[k]
    above, below, sides = own_masks(pairs)
    price[:, 0 : TOP - DEPTH, :] = jnp.ones((per + 1, TOP - DEPTH, LANES), jnp.float32)
    price[:, end + DEPTH :, :] = jnp.ones((per + 1, TOP - DEPTH, LANES), jnp.float32)
    price[0:per, TOP - DEPTH : TOP, :] = top[4 * tiles :] + (1.0 - above)
    price[0:per, end : end + DEPTH, :] = bottom[4 * tiles :] + (1.0 - below)
    for c in range(per):
        price[c, TOP:end, :] = cost[:, c * LANES : (c + 1) * LANES]
    price[per, TOP - DEPTH : TOP, :] = jnp.where(sides * above > 0.0, side_top[4], 1.0)
    price[per, TOP:end, :] = jnp.where(sides > 0.0, side[4], 1.0)
    price[per, end : end + DEPTH, :] = jnp.where(sides * below > 0.0, side_bottom[4], 1.0)
    q[:, 0:PAD, :] = jnp.zeros((tiles + 1, PAD, LANES), jnp.float32)
    q[:, end + SLAB :, :] = jnp.zeros((tiles + 1, PAD, LANES), jnp.float32)

    def divergence(start, count):
        span, earlier = pl.ds(start, count), pl.ds(start - 1, count)

        def cell(t, p, here, left):
            q[t, span, :] = a[t, span, :] - a[t, earlier, :] + (here - left)

        from_left(pairs, per, b, start, count, cell)

    for start, count in ((PAD, SLAB), (end, SLAB)):
        divergence(start, count)

    def turn(k, carried):
        divergence(TOP + k * CHUNK, CHUNK)
        return carried

    lax.fori_loop(0, rows // CHUNK, turn, 0)


def from_left(pairs, per, b, start, count, cell, closing=False):
    group, tiles = LANES // pairs, pairs * per
    span = pl.ds(start, count)
    lane = lax.broadcasted_iota(jnp.int32, (count, LANES), 1)
    side = b[tiles, span, :]
    moved_side = rolled(side, 1)
    for p in range(pairs):
        before = rolled(side, -(group * p + group - 1))
        for c in range(per):
            here = b[p * per + c, span, :]
            moved = rolled(here, 1)
            cell(p * per + c, p, here, jnp.where(lane == 0, before, moved))
            before = moved
        if not closing:
            moved_side = jnp.where(lane == group * p, rolled(before, group * p), moved_side)
    if not closing:
        cell(tiles, None, side, moved_side)


def from_right(pairs, per, u, start, count, cell):
    group, tiles = LANES // pairs, pairs * per
    span = pl.ds(start, count)
    lane = lax.broadcasted_iota(jnp.int32, (count, LANES), 1)
    side = u[tiles, span, :]
    moved_side = rolled(side, -1)
    for p in range(pairs):
        after = rolled(side, -1 - group * p)
        for c in reversed(range(per)):
            here = u[p * per + c, span, :]
            moved = rolled(here, -1)
            cell(p * per + c, p, here, jnp.where(lane == LANES - 1, after, moved))
            after = moved
        moved_side = jnp.where(lane == group * p + group - 1, rolled(after, group * p + group), moved_side)
    cell(tiles, None, side, moved_side)


def folded(value):
    return jnp.sum(value.reshape(-1, 8, LANES), axis=0)


def next_rates(recv, rates):
    total = jnp.sum(recv[...], axis=0, keepdims=True)
    primal = total + epsilon
    dual = pltpu.roll(jnp.broadcast_to(total, (8, LANES)), LANES // 2, 1)[0:1] + epsilon
    rescale = jnp.sqrt(jnp.sqrt(primal / dual))
    return rates[0:1, :] / rescale, rates[1:2, :] * rescale


def spread_rates(pairs, values):
    lane = lax.broadcasted_iota(jnp.int32, (1, LANES), 1)
    each = [jnp.sum(jnp.where(lane == p, values, 0.0)) for p in range(pairs)]
    side = jnp.zeros((1, LANES), jnp.float32)
    for p in range(pairs):
        side = jnp.where(lane // (LANES // pairs) == p, each[p], side)
    return each, side


def lanes_of(parts):
    row = lax.broadcasted_iota(jnp.int32, (8, LANES), 0)
    lane = lax.broadcasted_iota(jnp.int32, (8, LANES), 1)
    matrix = jnp.zeros((8, LANES), jnp.float32)
    where = jnp.zeros((8, LANES), jnp.int32)
    for k, (place, part) in enumerate(parts.items()):
        matrix = jnp.where(row == k, jnp.sum(part, axis=0, keepdims=True), matrix)
        where = jnp.where(row == k, place, where)
    sums = jnp.sum(matrix, axis=1, keepdims=True)
    used = row < len(parts)
    return jnp.sum(jnp.where((lane == where) & used, sums, 0.0), axis=0, keepdims=True)


def primal_rows(pairs, per, start, count, taus, tau_side, row_mask, sides, price, u, a, b, a_out, b_out, sums):
    span, later = pl.ds(start, count), pl.ds(start + 1, count)
    sums = list(sums)
    side_rate = tau_side * sides if row_mask is None else tau_side * sides * row_mask
    masked = taus if row_mask is None else [tau * row_mask for tau in taus]

    def cell(t, p, here, right):
        rate, grad_rate = (tau_side, side_rate) if p is None else (taus[p], masked[p])
        cost = price[per if p is None else t % per, span, :]
        old_down, old_right = a[t, span, :], b[t, span, :]
        down = old_down + grad_rate * (u[t, later, :] - here)
        across = old_right + grad_rate * (right - here)
        square = down * down + across * across
        factor = jnp.maximum(1.0 - (rate * cost) * lax.rsqrt(square), 0.0)
        new_down, new_right = factor * down, factor * across
        a_out[t, span, :] = new_down
        b_out[t, span, :] = new_right
        if sums and p is not None:
            change_down, change_right = new_down - old_down, new_right - old_right
            sums[p] = sums[p] + folded(change_down * change_down + change_right * change_right)

    from_right(pairs, per, u, start, count, cell)
    return sums


def dual_rows(pairs, per, start, count, sigmas, sigma_side, source, a, b, q, u, q_out, u_out, sums):
    span, earlier = pl.ds(start, count), pl.ds(start - 1, count)
    sums = list(sums)

    def cell(t, p, here, left):
        spread = a[t, span, :] - a[t, earlier, :] + (here - left)
        change = (sigma_side if p is None else sigmas[p]) * (2.0 * spread - q[t, span, :] - source[t, span, :])
        q_out[t, span, :] = spread
        u_out[t, span, :] = u[t, span, :] + change
        if sums and p is not None:
            sums[p] = sums[p] + folded(change * change)

    from_left(pairs, per, b, start, count, cell)
    return sums


def iterate_kernel(pairs, rows, sending, recv, rates, price, source, u, a, b, q, u_out, a_out, b_out, q_out, send, rates_out, *slabs):
    per = price.shape[0] - 1
    tiles = pairs * per
    end, last = TOP + rows, rows // CHUNK - 1
    tau, sigma = next_rates(recv, rates)
    rates_out[0:1, :] = tau
    rates_out[1:2, :] = sigma
    taus, tau_side = spread_rates(pairs, tau)
    sigmas, sigma_side = spread_rates(pairs, sigma)
    above, below, sides = own_masks(pairs)
    for out in (u_out, a_out, b_out, q_out):
        out[:, 0:PAD, :] = jnp.zeros((tiles + 1, PAD, LANES), jnp.float32)
        out[:, end + SLAB :, :] = jnp.zeros((tiles + 1, PAD, LANES), jnp.float32)

    def primal(start, count, mask, sums):
        return primal_rows(pairs, per, start, count, taus, tau_side, mask, sides, price, u, a, b, a_out, b_out, sums)

    def dual(start, count, mask, sums):
        now = sigmas if mask is None else [sigma * mask for sigma in sigmas]
        side_now = sigma_side * sides if mask is None else sigma_side * sides * mask
        return dual_rows(pairs, per, start, count, now, side_now, source, a_out, b_out, q, u, q_out, u_out, sums)

    zeros = [jnp.zeros((8, LANES), jnp.float32)] * pairs
    primal(PAD, SLAB, above, ())
    dual(PAD, SLAB, above, ())
    primals = primal(TOP, CHUNK, None, zeros)

    def turn(k, carried):
        primals, duals = carried
        start = TOP + k * CHUNK
        primals = primal(start, CHUNK, None, primals)
        duals = dual(start - CHUNK, CHUNK, None, duals)
        return tuple(primals), tuple(duals)

    primals, duals = lax.fori_loop(1, last + 1, turn, (tuple(primals), tuple(zeros)))
    primal(end, SLAB, below, ())
    duals = dual(TOP + last * CHUNK, CHUNK, None, duals)
    dual(end, SLAB, below, ())
    parts = {p: primals[p] for p in range(pairs)} | {LANES // 2 + p: duals[p] for p in range(pairs)}
    send[...] = jnp.broadcast_to(lanes_of(parts), send.shape)
    if sending:
        up, down = slabs
        for k, out in enumerate((u_out, a_out, b_out, q_out)):
            up[k] = out[:, TOP : TOP + DEPTH, :]
            down[k] = out[:, end - DEPTH : end, :]


def merge_kernel(rows, recv, top, bottom, u, a, b, q, u_out, a_out, b_out, q_out):
    for k, out in enumerate((u_out, a_out, b_out, q_out)):
        out[:, TOP - DEPTH : TOP, :] = top[k]
        out[:, TOP + rows : TOP + rows + DEPTH, :] = bottom[k]


def closing_kernel(pairs, recv, rates, price, source, u, a, b, q, flow_out, pot_out, send, a_new, b_new):
    per = price.shape[0] - 1
    rows = pot_out.shape[1]
    tau, sigma = next_rates(recv, rates)
    taus, tau_side = spread_rates(pairs, tau)
    sigmas, _ = spread_rates(pairs, sigma)
    above, _, sides = own_masks(pairs)

    def primal(start, count, mask):
        primal_rows(pairs, per, start, count, taus, tau_side, mask, sides, price, u, a, b, a_new, b_new, ())

    def close(k, sums):
        sums = list(sums)
        start = TOP + k * CHUNK
        span, earlier, own = pl.ds(start, CHUNK), pl.ds(start - 1, CHUNK), pl.ds(k * CHUNK, CHUNK)

        def cell(t, p, new_right, left):
            new_down = a_new[t, span, :]
            spread = new_down - a_new[t, earlier, :] + (new_right - left)
            imbalance = source[t, span, :]
            missing = spread - imbalance
            lanes = slice(t % per * LANES, (t % per + 1) * LANES)
            flow_out[0, p, own, lanes] = new_down
            flow_out[1, p, own, lanes] = new_right
            change = sigmas[p] * (2.0 * spread - q[t, span, :] - imbalance)
            pot_out[p, own, lanes] = u[t, span, :] + change
            sums[p] = sums[p] + folded(missing * missing)

        from_left(pairs, per, b_new, start, CHUNK, cell, closing=True)
        return tuple(sums)

    primal(PAD, SLAB, above)
    primal(TOP, CHUNK, None)

    def turn(k, sums):
        primal(TOP + k * CHUNK, CHUNK, None)
        return close(k - 1, sums)

    last = rows // CHUNK - 1
    short = lax.fori_loop(1, last + 1, turn, (jnp.zeros((8, LANES), jnp.float32),) * pairs)
    short = close(last, short)
    send[...] = jnp.broadcast_to(lanes_of({p: short[p] for p in range(pairs)}), send.shape)


def call(kernel, out_shape, operands, aliases=None, scratch=(), limit=8, space=pltpu.VMEM):
    vmem = pl.BlockSpec(memory_space=pltpu.VMEM)
    return pl.pallas_call(
        kernel,
        out_shape=out_shape,
        in_specs=[pl.BlockSpec(memory_space=space)] * len(operands),
        out_specs=[vmem] * len(out_shape),
        input_output_aliases=aliases or {},
        scratch_shapes=list(scratch),
        compiler_params=pltpu.CompilerParams(vmem_limit_bytes=limit << 20),
    )(*operands)


def kept(*dims):
    return pltpu.VMEM(dims, jnp.float32)


def exchange(send):
    return lax.all_to_all(send, AXES, 0, 0, tiled=True)


def local(imbalance, flow, potential, cost):
    pairs, rows, cols = imbalance.shape
    per = cols // LANES
    tiles = pairs * per
    height = rows + 2 * TOP
    devices = lax.axis_size("gy") * lax.axis_size("gx")

    slab, edge = kept(4 * tiles + per, DEPTH, LANES), kept(5, rows, LANES)
    arrays = 4 * pairs + 1
    up, down, left, right = call(
        functools.partial(pack_kernel, pairs),
        [slab, slab, edge, edge],
        [imbalance, flow, potential, cost],
        scratch=[
            kept(arrays, SLAB, cols),
            kept(arrays, SLAB, cols),
            kept(arrays, rows, LANES),
            kept(arrays, rows, LANES),
            pltpu.SemaphoreType.DMA((20,)),
        ],
        space=pltpu.MemorySpace.HBM,
    )
    side = neighbour(left, "gx", -1) + neighbour(right, "gx", 1)
    bottom, top = neighbour(up, "gy", -1), neighbour(down, "gy", 1)
    side_bottom = neighbour(side[:, :DEPTH], "gy", -1)
    side_top = neighbour(side[:, rows - DEPTH :], "gy", 1)

    field = kept(tiles + 1, height, LANES)
    u, a, b, q, source, price = call(
        functools.partial(assemble_kernel, pairs),
        [field] * 5 + [kept(per + 1, height, LANES)],
        [imbalance, flow, potential, cost, top, bottom, side, side_top, side_bottom],
        limit=16,
    )
    rates = jnp.full((8, LANES), initial_step, jnp.float32)
    recv = jnp.zeros((devices, LANES), jnp.float32)
    moving = kept(4, tiles + 1, DEPTH, LANES)
    for k in range(1, ITERS):
        sending = k % DEPTH == 0
        u, a, b, q, send, rates, *slabs = call(
            functools.partial(iterate_kernel, pairs, rows, sending),
            [field] * 4 + [kept(devices, LANES), kept(8, LANES)] + [moving] * 2 * sending,
            [recv, rates, price, source, u, a, b, q],
        )
        if sending:
            bottom, top = neighbour(slabs[0], "gy", -1), neighbour(slabs[1], "gy", 1)
        recv = exchange(send)
        if sending:
            u, a, b, q = call(
                functools.partial(merge_kernel, rows),
                [field] * 4,
                [recv, top, bottom, u, a, b, q],
                aliases={3: 0, 4: 1, 5: 2, 6: 3},
            )
    new = kept(tiles + 1, height, LANES)
    flow_out, pot_out, send = call(
        functools.partial(closing_kernel, pairs),
        [kept(2, pairs, rows, cols), kept(pairs, rows, cols), kept(devices, LANES)],
        [recv, rates, price, source, u, a, b, q],
        scratch=[new, new],
    )
    cells = rows * lax.axis_size("gy") * cols * lax.axis_size("gx")
    residual = jnp.sum(exchange(send), axis=0)[:pairs] / cells
    return flow_out, pot_out, residual


def solution(mesh):
    placed = (P(None, "gy", "gx"), P(None, None, "gy", "gx"), P(None, "gy", "gx"), P("gy", "gx"))
    return jax.shard_map(
        local,
        mesh=mesh,
        in_specs=placed,
        out_specs=(P(None, None, "gy", "gx"), P(None, "gy", "gx"), P()),
        check_vma=False,
    )
```

time: 294 us -> 184 us (0.63)
  blocking collectives: 8.85 us -> 108 us
  Pallas kernels: 130 us -> 33.5 us
  waiting for transfers between devices: 95.6 us -> 6.26 us
  starting transfers between devices: 49.3 us -> 27 us
    all_to_all x1 -> x11, blocking collectives: 8.85 us -> 108 us  [exchange(): return lax.all_to_all(send, AXES, 0, 0, tiled=True)]
    pallas_call x14 -> x16, Pallas kernels: 130 us -> 33.5 us  [call(): pl.pallas_call(kernel, out_shape=out_shape, in_specs=[pl.BlockSpec(memory...]
    all_to_all x11 -> x1, waiting for transfers between devices: 78.1 us -> 4.88 us  [exchange(): return lax.all_to_all(send, AXES, 0, 0, tiled=True)]
    all_to_all x11 -> x1, starting transfers between devices: 31.4 us -> 2.52 us  [exchange(): return lax.all_to_all(send, AXES, 0, 0, tiled=True)]
    ppermute x6 -> x10, waiting for transfers between devices: 17.5 us -> 1.37 us  [neighbour(): lax.ppermute(value, axis, [(source, source + steps) for source in range(l...]
    ppermute x6 -> x10, starting transfers between devices: 17.9 us -> 24.5 us  [neighbour(): lax.ppermute(value, axis, [(source, source + steps) for source in range(l...]
    unnamed x16 -> x18, local copies, waits for them, and re-layouts: 7.16 us -> 7.29 us
  transfers between devices with their start and end apart: 17 -> 11, of which waited for: 13 -> 4; matrix products, arithmetic and copies ran while one was open for 0% -> 1% of each run, Pallas kernels for 0% -> 0%
where the time goes in v2:
time: 184 us; the launch traced here: 183 us
  blocking collectives  108 us (59%)
  Pallas kernels  33.5 us (18%)
  starting transfers between devices  27 us (15%)
  local copies, waits for them, and re-layouts  7.3 us (4%)
  waiting for transfers between devices  6.26 us (3%)
    all_to_all x11, blocking collectives, exchange(): return lax.all_to_all(send, AXES, 0, 0, tiled=True)  108 us
    pallas_call x16, Pallas kernels, call(): pl.pallas_call(kernel, out_shape=out_shape, in_specs=[pl.BlockSpec(memory...  33.5 us
    ppermute x10, starting transfers between devices, neighbour(): lax.ppermute(value, axis, [(source, source + steps) for source in range(l...  24.5 us
    unnamed x18, local copies, waits for them, and re-layouts  7.29 us
    all_to_all x1, waiting for transfers between devices, exchange(): return lax.all_to_all(send, AXES, 0, 0, tiled=True)  4.88 us
  transfers between devices with their start and end apart: 11, of which 4 were waited for; matrix products, arithmetic and copies ran while one was open for 1% of the time, Pallas kernels for 0%

profile of v2, /device:TPU:0, one launch (start us, length us, event | category | flops | bytes accessed | tf_op | source)
XLA Modules:
  0.0 183.5 jit_solution(10350110229498671041)
XLA Ops:
  8.3 3.1 %collective-permute-start.3 = (f32[5,128,128]{2,1,0:T(8,128)S(1)}, f32[5,128,128]{2,1,0:T(8,128)S(1)}, u32[]{:S(2)}, u32[]{:S(2)}) collective-permute-start(f32[5,128,128]{2,1,0:T(8,128)S(1)} %get-tuple-element.97), channel_id=1, source_target_pairs={{0,1},{1,2},{2,3},{4,5},{5,6},{6,7},{8,9},{9,10},{10,11},{12,13},{... | collective-permute-start | bytes 983048 | tf_op jit(solution)/shard_map/ppermute | solution.py:27
  11.3 4.9 %collective-permute-start = (f32[68,4,128]{2,1,0:T(4,128)S(1)}, f32[68,4,128]{2,1,0:T(4,128)S(1)}, u32[]{:S(2)}, u32[]{:S(2)}) collective-permute-start(f32[68,4,128]{2,1,0:T(4,128)S(1)} %get-tuple-element.94), channel_id=1, source_target_pairs={{0,4},{4,8},{8,12},{12,16},{16,20},{20,24},{24,28},{1,5},{5,9},{9,... | collective-permute-start | bytes 417800 | tf_op jit(solution)/shard_map/ppermute | solution.py:27
  18.9 5.2 %collective-permute-start.4 = (f32[5,4,128]{2,1,0:T(4,128)S(1)}, f32[5,4,128]{2,1,0:T(4,128)S(1)}, u32[]{:S(2)}, u32[]{:S(2)}) collective-permute-start(f32[5,4,128]{2,1,0:T(4,128)S(1)} %get-tuple-element.186), channel_id=1, source_target_pairs={{0,4},{4,8},{8,12},{12,16},{16,20},{20,24},{24,28},{1,5},{5,9},{9,... | collective-permute-start | bytes 30728 | tf_op jit(solution)/shard_map/ppermute | solution.py:27
  27.2 2.5 %shard_map.69 = (f32[17,160,128]{2,1,0:T(8,128)S(1)}, f32[17,160,128]{2,1,0:T(8,128)S(1)}, f32[17,160,128]{2,1,0:T(8,128)S(1)}, f32[17,160,128]{2,1,0:T(8,128)S(...) custom-call(f32[32,128]{1,0:T(8,128)S(1)} %broadcast_in_dim.6.recv, f32[8,128]{1,0:T(8,128)S(1)} %broadcast_in_dim.7.rates, ...), custom_call_target="tpu_custom_call" | custom-call | tf_op jit(solution)/shard_map/pallas_call | solution.py:354
  29.6 15.1 %all_to_all.130 = f32[32,1,128]{2,1,0:T(1,128)S(1)} all-to-all(f32[32,1,128]{2,1,0:T(1,128)S(1)} %bitcast.62), channel_id=1, replica_groups=mesh['gy'=8,'gx'=4] {'gy','gx'}, dimensions={0} | all-to-all | bytes 32768 | tf_op jit(solution)/shard_map/all_to_all | solution.py:370
  47.1 8.9 %all_to_all.131 = f32[32,1,128]{2,1,0:T(1,128)S(1)} all-to-all(f32[32,1,128]{2,1,0:T(1,128)S(1)} %bitcast.63), channel_id=1, replica_groups=mesh['gy'=8,'gx'=4] {'gy','gx'}, dimensions={0} | all-to-all | bytes 32768 | tf_op jit(solution)/shard_map/all_to_all | solution.py:370
  56.0 2.5 %shard_map.71 = (f32[17,160,128]{2,1,0:T(8,128)S(1)}, f32[17,160,128]{2,1,0:T(8,128)S(1)}, f32[17,160,128]{2,1,0:T(8,128)S(1)}, f32[17,160,128]{2,1,0:T(8,128)S(...) custom-call(f32[32,128]{1,0:T(8,128)S(1)} %bitcast.54, f32[8,128]{1,0:T(8,128)S(1)} %get-tuple-element.111.rates, ...), custom_call_target="tpu_custom_call" | custom-call | tf_op jit(solution)/shard_map/pallas_call | solution.py:354
  58.5 8.9 %all_to_all.132 = f32[32,1,128]{2,1,0:T(1,128)S(1)} all-to-all(f32[32,1,128]{2,1,0:T(1,128)S(1)} %bitcast.64), channel_id=1, replica_groups=mesh['gy'=8,'gx'=4] {'gy','gx'}, dimensions={0} | all-to-all | bytes 32768 | tf_op jit(solution)/shard_map/all_to_all | solution.py:370
  67.4 2.5 %shard_map.72 = (f32[17,160,128]{2,1,0:T(8,128)S(1)}, f32[17,160,128]{2,1,0:T(8,128)S(1)}, f32[17,160,128]{2,1,0:T(8,128)S(1)}, f32[17,160,128]{2,1,0:T(8,128)S(...) custom-call(f32[32,128]{1,0:T(8,128)S(1)} %bitcast.51, ...), custom_call_target="tpu_custom_call" | custom-call | tf_op jit(solution)/shard_map/pallas_call | solution.py:354
  69.9 2.5 %collective-permute-start.6 = (f32[4,17,4,128]{3,2,1,0:T(4,128)S(1)}, f32[4,17,4,128]{3,2,1,0:T(4,128)S(1)}, u32[]{:S(2)}, u32[]{:S(2)}) collective-permute-start(f32[4,17,4,128]{3,2,1,0:T(4,128)S(1)} %get-tuple-element.124), channel_id=1, source_target_pairs={{0,4},{4,8},{8,12},{12,16},{16,20},{20,24},{24,28},{1,5},{5,9},{9,... | collective-permute-start | bytes 417800 | tf_op jit(solution)/shard_map/ppermute | solution.py:27
  73.7 10.9 %all_to_all.133 = f32[32,1,128]{2,1,0:T(1,128)S(1)} all-to-all(f32[32,1,128]{2,1,0:T(1,128)S(1)} %bitcast.60), channel_id=1, replica_groups=mesh['gy'=8,'gx'=4] {'gy','gx'}, dimensions={0} | all-to-all | bytes 32768 | tf_op jit(solution)/shard_map/all_to_all | solution.py:370
  87.1 8.9 %all_to_all.134 = f32[32,1,128]{2,1,0:T(1,128)S(1)} all-to-all(f32[32,1,128]{2,1,0:T(1,128)S(1)} %bitcast.65), channel_id=1, replica_groups=mesh['gy'=8,'gx'=4] {'gy','gx'}, dimensions={0} | all-to-all | bytes 32768 | tf_op jit(solution)/shard_map/all_to_all | solution.py:370
  98.4 8.9 %all_to_all.135 = f32[32,1,128]{2,1,0:T(1,128)S(1)} all-to-all(f32[32,1,128]{2,1,0:T(1,128)S(1)} %bitcast.66), channel_id=1, replica_groups=mesh['gy'=8,'gx'=4] {'gy','gx'}, dimensions={0} | all-to-all | bytes 32768 | tf_op jit(solution)/shard_map/all_to_all | solution.py:370
  107.3 2.5 %shard_map.76 = (f32[17,160,128]{2,1,0:T(8,128)S(1)}, f32[17,160,128]{2,1,0:T(8,128)S(1)}, f32[17,160,128]{2,1,0:T(8,128)S(1)}, f32[17,160,128]{2,1,0:T(8,128)S(...) custom-call(f32[32,128]{1,0:T(8,128)S(1)} %bitcast.56, f32[8,128]{1,0:T(8,128)S(1)} %get-tuple-element.141.rates, ...), custom_call_target="tpu_custom_call" | custom-call | tf_op jit(solution)/shard_map/pallas_call | solution.py:354
  109.8 8.9 %all_to_all.136 = f32[32,1,128]{2,1,0:T(1,128)S(1)} all-to-all(f32[32,1,128]{2,1,0:T(1,128)S(1)} %bitcast.67), channel_id=1, replica_groups=mesh['gy'=8,'gx'=4] {'gy','gx'}, dimensions={0} | all-to-all | bytes 32768 | tf_op jit(solution)/shard_map/all_to_all | solution.py:370
  118.7 2.5 %shard_map.77 = (f32[17,160,128]{2,1,0:T(8,128)S(1)}, f32[17,160,128]{2,1,0:T(8,128)S(1)}, f32[17,160,128]{2,1,0:T(8,128)S(1)}, f32[17,160,128]{2,1,0:T(8,128)S(...) custom-call(f32[32,128]{1,0:T(8,128)S(1)} %bitcast.52, ...), custom_call_target="tpu_custom_call" | custom-call | tf_op jit(solution)/shard_map/pallas_call | solution.py:354
  121.2 2.5 %collective-permute-start.8 = (f32[4,17,4,128]{3,2,1,0:T(4,128)S(1)}, f32[4,17,4,128]{3,2,1,0:T(4,128)S(1)}, u32[]{:S(2)}, u32[]{:S(2)}) collective-permute-start(f32[4,17,4,128]{3,2,1,0:T(4,128)S(1)} %get-tuple-element.154), channel_id=1, source_target_pairs={{0,4},{4,8},{8,12},{12,16},{16,20},{20,24},{24,28},{1,5},{5,9},{9,... | collective-permute-start | bytes 417800 | tf_op jit(solution)/shard_map/ppermute | solution.py:27
  125.0 10.9 %all_to_all.137 = f32[32,1,128]{2,1,0:T(1,128)S(1)} all-to-all(f32[32,1,128]{2,1,0:T(1,128)S(1)} %bitcast.61), channel_id=1, replica_groups=mesh['gy'=8,'gx'=4] {'gy','gx'}, dimensions={0} | all-to-all | bytes 32768 | tf_op jit(solution)/shard_map/all_to_all | solution.py:370
  138.4 8.9 %all_to_all.138 = f32[32,1,128]{2,1,0:T(1,128)S(1)} all-to-all(f32[32,1,128]{2,1,0:T(1,128)S(1)} %bitcast.68), channel_id=1, replica_groups=mesh['gy'=8,'gx'=4] {'gy','gx'}, dimensions={0} | all-to-all | bytes 32768 | tf_op jit(solution)/shard_map/all_to_all | solution.py:370
  149.7 8.9 %all_to_all.139 = f32[32,1,128]{2,1,0:T(1,128)S(1)} all-to-all(f32[32,1,128]{2,1,0:T(1,128)S(1)} %bitcast.69), channel_id=1, replica_groups=mesh['gy'=8,'gx'=4] {'gy','gx'}, dimensions={0} | all-to-all | bytes 32768 | tf_op jit(solution)/shard_map/all_to_all | solution.py:370
  161.0 8.9 %all_to_all.140 = f32[32,1,128]{2,1,0:T(1,128)S(1)} all-to-all(f32[32,1,128]{2,1,0:T(1,128)S(1)} %bitcast.70), channel_id=1, replica_groups=mesh['gy'=8,'gx'=4] {'gy','gx'}, dimensions={0} | all-to-all | bytes 32768 | tf_op jit(solution)/shard_map/all_to_all | solution.py:370
  169.9 3.3 %shard_map.82 = (f32[2,4,128,512]{3,2,1,0:T(8,128)S(1)}, f32[4,128,512]{2,1,0:T(8,128)S(1)}, f32[32,128]{1,0:T(8,128)}) custom-call(f32[32,128]{1,0:T(8,128)S(1)} %bitcast.59, f32[8,128]{1,0:T(8,128)S(1)} %get-tuple-element.177.rates, f32[5,160,128]{2,1,0:T(8,128)S(1)} %get-tuple-element.98.price, f32[17,160,128]{2,1,0:T(8,128)S(1)} %get-tuple-element.99.source, ...), custom_call_target="tpu_custom_call" | custom-call | tf_op jit(solution)/shard_map/pallas_call | solution.py:354
  173.2 2.5 %all-to-all-start.11 = ((f32[32,1,128]{2,1,0:T(1,128)}), f32[32,1,128]{2,1,0:T(1,128)S(1)}, u32[]{:S(2)}, u32[]{:S(2)}) async-start(f32[32,1,128]{2,1,0:T(1,128)} %bitcast.34), calls=%async_computation.11 | async-start | bytes 32768 | tf_op jit(solution)/shard_map/all_to_all | solution.py:370
  178.0 4.9 %all-to-all-done.11 = f32[32,1,128]{2,1,0:T(1,128)S(1)} async-done(((f32[32,1,128]{2,1,0:T(1,128)}), f32[32,1,128]{2,1,0:T(1,128)S(1)}, u32[]{:S(2)}, u32[]{:S(2)}) %all-to-all-start.11) | async-done | bytes 16416 | tf_op jit(solution)/shard_map/all_to_all | solution.py:370
  (49 shorter events, 33.4 us)
Async XLA Ops:
  0.6 1.6 copy-start
  2.2 1.2 copy-start.2
  3.4 1.2 copy-start.4
  4.7 0.9 copy-start.6
  5.6 19.8 %copy-start.1 = (f32[2,4,128,512]{3,2,1,0:T(8,128)S(1)}, f32[2,4,128,512]{3,2,1,0:T(8,128)}, u32[]{:S(2)}) copy-start(f32[2,4,128,512]{3,2,1,0:T(8,128)} %flow.3) | copy-start | bytes 6291460
  5.6 19.8 %copy-start.3 = (f32[4,128,512]{2,1,0:T(8,128)S(1)}, f32[4,128,512]{2,1,0:T(8,128)}, u32[]{:S(2)}) copy-start(f32[4,128,512]{2,1,0:T(8,128)} %imb.3) | copy-start | bytes 3145732
  5.6 19.8 %copy-start.5 = (f32[4,128,512]{2,1,0:T(8,128)S(1)}, f32[4,128,512]{2,1,0:T(8,128)}, u32[]{:S(2)}) copy-start(f32[4,128,512]{2,1,0:T(8,128)} %pot.3) | copy-start | bytes 3145732
  5.6 19.8 %copy-start.7 = (f32[128,512]{1,0:T(8,128)S(1)}, f32[128,512]{1,0:T(8,128)}, u32[]{:S(2)}) copy-start(f32[128,512]{1,0:T(8,128)} %cost.3) | copy-start | bytes 786436
  7.0 10.5 %collective-permute-start.2 = (f32[5,128,128]{2,1,0:T(8,128)S(1)}, f32[5,128,128]{2,1,0:T(8,128)S(1)}, u32[]{:S(2)}, u32[]{:S(2)}) collective-permute-start(f32[5,128,128]{2,1,0:T(8,128)S(1)} %get-tuple-element.96), channel_id=1, source_target_pairs={{1,0},{2,1},{3,2},{5,4},{6,5},{7,6},{9,8},{10,9},{11,10},{13,12},{... | collective-permute-start | bytes 983048 | tf_op jit(solution)/shard_map/ppermute | solution.py:27
  8.3 9.3 %collective-permute-start.3 = (f32[5,128,128]{2,1,0:T(8,128)S(1)}, f32[5,128,128]{2,1,0:T(8,128)S(1)}, u32[]{:S(2)}, u32[]{:S(2)}) collective-permute-start(f32[5,128,128]{2,1,0:T(8,128)S(1)} %get-tuple-element.97), channel_id=1, source_target_pairs={{0,1},{1,2},{2,3},{4,5},{5,6},{6,7},{8,9},{9,10},{10,11},{12,13},{... | collective-permute-start | bytes 983048 | tf_op jit(solution)/shard_map/ppermute | solution.py:27
  11.3 12.8 %collective-permute-start = (f32[68,4,128]{2,1,0:T(4,128)S(1)}, f32[68,4,128]{2,1,0:T(4,128)S(1)}, u32[]{:S(2)}, u32[]{:S(2)}) collective-permute-start(f32[68,4,128]{2,1,0:T(4,128)S(1)} %get-tuple-element.94), channel_id=1, source_target_pairs={{0,4},{4,8},{8,12},{12,16},{16,20},{20,24},{24,28},{1,5},{5,9},{9,... | collective-permute-start | bytes 417800 | tf_op jit(solution)/shard_map/ppermute | solution.py:27
  16.2 8.4 %collective-permute-start.1 = (f32[68,4,128]{2,1,0:T(4,128)S(1)}, f32[68,4,128]{2,1,0:T(4,128)S(1)}, u32[]{:S(2)}, u32[]{:S(2)}) collective-permute-start(f32[68,4,128]{2,1,0:T(4,128)S(1)} %get-tuple-element.95), channel_id=1, source_target_pairs={{4,0},{8,4},{12,8},{16,12},{20,16},{24,20},{28,24},{5,1},{9,5},{13... | collective-permute-start | bytes 417800 | tf_op jit(solution)/shard_map/ppermute | solution.py:27
  17.6 7.2 %collective-permute-start.5 = (f32[5,4,128]{2,1,0:T(4,128)S(1)}, f32[5,4,128]{2,1,0:T(4,128)S(1)}, u32[]{:S(2)}, u32[]{:S(2)}) collective-permute-start(f32[5,4,128]{2,1,0:T(4,128)S(1)} %get-tuple-element.185), channel_id=1, source_target_pairs={{4,0},{8,4},{12,8},{16,12},{20,16},{24,20},{28,24},{5,1},{9,5},{13... | collective-permute-start | bytes 30728 | tf_op jit(solution)/shard_map/ppermute | solution.py:27
  18.9 6.6 %collective-permute-start.4 = (f32[5,4,128]{2,1,0:T(4,128)S(1)}, f32[5,4,128]{2,1,0:T(4,128)S(1)}, u32[]{:S(2)}, u32[]{:S(2)}) collective-permute-start(f32[5,4,128]{2,1,0:T(4,128)S(1)} %get-tuple-element.186), channel_id=1, source_target_pairs={{0,4},{4,8},{8,12},{12,16},{16,20},{20,24},{24,28},{1,5},{5,9},{9,... | collective-permute-start | bytes 30728 | tf_op jit(solution)/shard_map/ppermute | solution.py:27
  69.9 14.7 %collective-permute-start.6 = (f32[4,17,4,128]{3,2,1,0:T(4,128)S(1)}, f32[4,17,4,128]{3,2,1,0:T(4,128)S(1)}, u32[]{:S(2)}, u32[]{:S(2)}) collective-permute-start(f32[4,17,4,128]{3,2,1,0:T(4,128)S(1)} %get-tuple-element.124), channel_id=1, source_target_pairs={{0,4},{4,8},{8,12},{12,16},{16,20},{20,24},{24,28},{1,5},{5,9},{9,... | collective-permute-start | bytes 417800 | tf_op jit(solution)/shard_map/ppermute | solution.py:27
  72.4 12.2 %collective-permute-start.7 = (f32[4,17,4,128]{3,2,1,0:T(4,128)S(1)}, f32[4,17,4,128]{3,2,1,0:T(4,128)S(1)}, u32[]{:S(2)}, u32[]{:S(2)}) collective-permute-start(f32[4,17,4,128]{3,2,1,0:T(4,128)S(1)} %get-tuple-element.125), channel_id=1, source_target_pairs={{4,0},{8,4},{12,8},{16,12},{20,16},{24,20},{28,24},{5,1},{9,5},{13... | collective-permute-start | bytes 417800 | tf_op jit(solution)/shard_map/ppermute | solution.py:27
  121.2 14.7 %collective-permute-start.8 = (f32[4,17,4,128]{3,2,1,0:T(4,128)S(1)}, f32[4,17,4,128]{3,2,1,0:T(4,128)S(1)}, u32[]{:S(2)}, u32[]{:S(2)}) collective-permute-start(f32[4,17,4,128]{3,2,1,0:T(4,128)S(1)} %get-tuple-element.154), channel_id=1, source_target_pairs={{0,4},{4,8},{8,12},{12,16},{16,20},{20,24},{24,28},{1,5},{5,9},{9,... | collective-permute-start | bytes 417800 | tf_op jit(solution)/shard_map/ppermute | solution.py:27
  123.7 12.2 %collective-permute-start.9 = (f32[4,17,4,128]{3,2,1,0:T(4,128)S(1)}, f32[4,17,4,128]{3,2,1,0:T(4,128)S(1)}, u32[]{:S(2)}, u32[]{:S(2)}) collective-permute-start(f32[4,17,4,128]{3,2,1,0:T(4,128)S(1)} %get-tuple-element.155), channel_id=1, source_target_pairs={{4,0},{8,4},{12,8},{16,12},{20,16},{24,20},{28,24},{5,1},{9,5},{13... | collective-permute-start | bytes 417800 | tf_op jit(solution)/shard_map/ppermute | solution.py:27
  173.2 9.7 %all-to-all-start.11 = ((f32[32,1,128]{2,1,0:T(1,128)}), f32[32,1,128]{2,1,0:T(1,128)S(1)}, u32[]{:S(2)}, u32[]{:S(2)}) async-start(f32[32,1,128]{2,1,0:T(1,128)} %bitcast.34), calls=%async_computation.11 | async-start | bytes 32768 | tf_op jit(solution)/shard_map/all_to_all | solution.py:370

commit v3 on v2

--- a/solution.py
+++ b/solution.py
@@ -17,7 +17,7 @@
 PAD = 8
 TOP = PAD + SLAB
 LANES = 128
-CHUNK = 16
+CHUNK = 32
 AXES = ("gy", "gx")
 
 
@@ -32,42 +32,34 @@
     return pltpu.roll(value, shift, 1) if shift else value
 
 
-def pack_kernel(pairs, imb, flow, pot, cost, up, down, left, right, top, bottom, first, last, sems):
+def edge_kernel(pairs, imb, flow, pot, cost, left, right, up, down, top, bottom, first, last, sems):
     rows, cols = cost.shape
     per, group = cols // LANES, LANES // pairs
-    tiles = pairs * per
     fields = [pot, flow.at[0], flow.at[1], imb]
     copies = []
 
     def fetch(source, target):
         copies.append(pltpu.make_async_copy(source, target, sems.at[len(copies)]))
 
+    for k, field in enumerate(fields):
+        fetch(field.at[:, :, 0:LANES], first.at[pl.ds(k * pairs, pairs)])
+        fetch(field.at[:, :, cols - LANES : cols], last.at[pl.ds(k * pairs, pairs)])
+    fetch(cost.at[:, 0:LANES], first.at[4 * pairs])
+    fetch(cost.at[:, cols - LANES : cols], last.at[4 * pairs])
+    sides = len(copies)
     for k, field in enumerate(fields):
         fetch(field.at[:, 0:SLAB, :], top.at[pl.ds(k * pairs, pairs)])
         fetch(field.at[:, rows - SLAB : rows, :], bottom.at[pl.ds(k * pairs, pairs)])
     fetch(cost.at[0:SLAB, :], top.at[4 * pairs])
     fetch(cost.at[rows - SLAB : rows, :], bottom.at[4 * pairs])
-    slabs = len(copies)
-    for k, field in enumerate(fields):
-        fetch(field.at[:, :, 0:LANES], first.at[pl.ds(k * pairs, pairs)])
-        fetch(field.at[:, :, cols - LANES : cols], last.at[pl.ds(k * pairs, pairs)])
-    fetch(cost.at[:, 0:LANES], first.at[4 * pairs])
-    fetch(cost.at[:, cols - LANES : cols], last.at[4 * pairs])
     for copy in copies:
         copy.start()
-    for copy in copies[:slabs]:
-        copy.wait()
-    for n in range(4 * pairs + 1):
-        for c in range(per):
-            span = slice(c * LANES, (c + 1) * LANES)
-            up[n * per + c] = top[n, 0:DEPTH, span]
-            down[n * per + c] = bottom[n, SLAB - DEPTH : SLAB, span]
-    for copy in copies[slabs:]:
-        copy.wait()
     count = 32
     lane = lax.broadcasted_iota(jnp.int32, (count, LANES), 1)
     inner, which = lane % group, lane // group
     for k in range(5):
+        for copy in copies[2 * k : 2 * k + 2]:
+            copy.wait()
         for start in range(0, rows, count):
             span = slice(start, start + count)
             head = jnp.zeros((count, LANES), jnp.float32)
@@ -78,6 +70,21 @@
                 tail = jnp.where((which == p) & (inner >= group - SIDE), rolled(last[n, span, :], group * (p + 1)), tail)
             left[k, span, :] = head
             right[k, span, :] = tail
+    for copy in copies[sides:]:
+        copy.wait()
+    for n in range(4 * pairs + 1):
+        for c in range(per):
+            span = slice(c * LANES, (c + 1) * LANES)
+            up[n * per + c] = top[n, 0:DEPTH, span]
+            down[n * per + c] = bottom[n, SLAB - DEPTH : SLAB, span]
+
+
+def slab_kernel(rows, left, right, own_up, own_down, up, down):
+    count = own_up.shape[0]
+    up[0:count] = own_up[...]
+    down[0:count] = own_down[...]
+    up[count : count + 5] = left[:, 0:DEPTH, :] + right[:, 0:DEPTH, :]
+    down[count : count + 5] = left[:, rows - DEPTH : rows, :] + right[:, rows - DEPTH : rows, :]
 
 
 def own_masks(pairs):
@@ -91,54 +98,59 @@
     return above, below, sides
 
 
-def assemble_kernel(
-    pairs, imb, flow, pot, cost, top, bottom, side, side_top, side_bottom, u, a, b, q, source, price
-):
+def assemble_kernel(pairs, imb, flow, pot, cost, left, right, u, a, b, q, source, price):
     rows, cols = cost.shape
     per = cols // LANES
     tiles = pairs * per
     end = TOP + rows
     fields = [(u, pot), (a, flow.at[0]), (b, flow.at[1]), (source, imb)]
+    blank = jnp.zeros((tiles + 1, TOP, LANES), jnp.float32)
     for k, (into, field) in enumerate(fields):
-        into[:, 0 : TOP - DEPTH, :] = jnp.zeros((tiles + 1, TOP - DEPTH, LANES), jnp.float32)
-        into[:, end + DEPTH :, :] = jnp.zeros((tiles + 1, TOP - DEPTH, LANES), jnp.float32)
-        into[0:tiles, TOP - DEPTH : TOP, :] = top[k * tiles : (k + 1) * tiles]
-        into[0:tiles, end : end + DEPTH, :] = bottom[k * tiles : (k + 1) * tiles]
+        into[:, 0:TOP, :] = blank
+        into[:, end : end + TOP, :] = blank
         for p in range(pairs):
             for c in range(per):
                 into[p * per + c, TOP:end, :] = field[p, :, c * LANES : (c + 1) * LANES]
-        into[tiles, TOP - DEPTH : TOP, :] = side_top[k]
-        into[tiles, TOP:end, :] = side[k]
-        into[tiles, end : end + DEPTH, :] = side_bottom[k]
-    above, below, sides = own_masks(pairs)
-    price[:, 0 : TOP - DEPTH, :] = jnp.ones((per + 1, TOP - DEPTH, LANES), jnp.float32)
-    price[:, end + DEPTH :, :] = jnp.ones((per + 1, TOP - DEPTH, LANES), jnp.float32)
-    price[0:per, TOP - DEPTH : TOP, :] = top[4 * tiles :] + (1.0 - above)
-    price[0:per, end : end + DEPTH, :] = bottom[4 * tiles :] + (1.0 - below)
+        into[tiles, TOP:end, :] = left[k] + right[k]
+    sides = own_masks(pairs)[2]
+    price[:, 0:TOP, :] = jnp.ones((per + 1, TOP, LANES), jnp.float32)
+    price[:, end : end + TOP, :] = jnp.ones((per + 1, TOP, LANES), jnp.float32)
     for c in range(per):
         price[c, TOP:end, :] = cost[:, c * LANES : (c + 1) * LANES]
-    price[per, TOP - DEPTH : TOP, :] = jnp.where(sides * above > 0.0, side_top[4], 1.0)
-    price[per, TOP:end, :] = jnp.where(sides > 0.0, side[4], 1.0)
-    price[per, end : end + DEPTH, :] = jnp.where(sides * below > 0.0, side_bottom[4], 1.0)
-    q[:, 0:PAD, :] = jnp.zeros((tiles + 1, PAD, LANES), jnp.float32)
-    q[:, end + SLAB :, :] = jnp.zeros((tiles + 1, PAD, LANES), jnp.float32)
-
-    def divergence(start, count):
-        span, earlier = pl.ds(start, count), pl.ds(start - 1, count)
-
-        def cell(t, p, here, left):
-            q[t, span, :] = a[t, span, :] - a[t, earlier, :] + (here - left)
-
-        from_left(pairs, per, b, start, count, cell)
-
-    for start, count in ((PAD, SLAB), (end, SLAB)):
-        divergence(start, count)
+    price[per, TOP:end, :] = jnp.where(sides > 0.0, left[4] + right[4], 1.0)
+    q[:, 0:TOP, :] = blank
+    q[:, end : end + TOP, :] = blank
 
     def turn(k, carried):
-        divergence(TOP + k * CHUNK, CHUNK)
+        start_rows(pairs, per, a, b, q, TOP + k * 16, 16)
         return carried
 
-    lax.fori_loop(0, rows // CHUNK, turn, 0)
+    lax.fori_loop(0, rows // 16, turn, 0)
+
+
+def start_rows(pairs, per, a, b, q, start, count):
+    span, earlier = pl.ds(start, count), pl.ds(start - 1, count)
+
+    def cell(t, p, here, left):
+        q[t, span, :] = a[t, span, :] - a[t, earlier, :] + (here - left)
+
+    from_left(pairs, per, b, start, count, cell)
+
+
+def adopt_kernel(pairs, top, bottom, u, a, b, q, source, price, u_out, a_out, b_out, q_out, source_out, price_out):
+    per = price.shape[0] - 1
+    tiles = pairs * per
+    height = u.shape[1]
+    above_rows, below_rows = slice(TOP - DEPTH, TOP), slice(height - TOP, height - TOP + DEPTH)
+    above, below, sides = own_masks(pairs)
+    for rows, slab, mask in ((above_rows, top, above), (below_rows, bottom, below)):
+        for k, out in enumerate((u_out, a_out, b_out, source_out)):
+            out[0:tiles, rows, :] = slab[k * tiles : (k + 1) * tiles]
+            out[tiles, rows, :] = slab[4 * tiles + per + k]
+        price_out[0:per, rows, :] = slab[4 * tiles : 4 * tiles + per] + (1.0 - mask)
+        price_out[per, rows, :] = jnp.where(sides * mask > 0.0, slab[4 * tiles + per + 4], 1.0)
+    for start in (PAD, TOP, height - TOP):
+        start_rows(pairs, per, a_out, b_out, q_out, start, SLAB)
 
 
 def from_left(pairs, per, b, start, count, cell, closing=False):
@@ -349,7 +361,7 @@
     send[...] = jnp.broadcast_to(lanes_of({p: short[p] for p in range(pairs)}), send.shape)
 
 
-def call(kernel, out_shape, operands, aliases=None, scratch=(), limit=8, space=pltpu.VMEM):
+def call(kernel, out_shape, operands, aliases=None, scratch=(), limit=8, space=pltpu.VMEM, flops=0):
     vmem = pl.BlockSpec(memory_space=pltpu.VMEM)
     return pl.pallas_call(
         kernel,
@@ -358,6 +370,7 @@
         out_specs=[vmem] * len(out_shape),
         input_output_aliases=aliases or {},
         scratch_shapes=list(scratch),
+        cost_estimate=pl.CostEstimate(flops=flops, bytes_accessed=0, transcendentals=0) if flops else None,
         compiler_params=pltpu.CompilerParams(vmem_limit_bytes=limit << 20),
     )(*operands)
 
@@ -377,32 +390,28 @@
     height = rows + 2 * TOP
     devices = lax.axis_size("gy") * lax.axis_size("gx")
 
-    slab, edge = kept(4 * tiles + per, DEPTH, LANES), kept(5, rows, LANES)
-    arrays = 4 * pairs + 1
-    up, down, left, right = call(
-        functools.partial(pack_kernel, pairs),
-        [slab, slab, edge, edge],
-        [imbalance, flow, potential, cost],
-        scratch=[
-            kept(arrays, SLAB, cols),
-            kept(arrays, SLAB, cols),
-            kept(arrays, rows, LANES),
-            kept(arrays, rows, LANES),
-            pltpu.SemaphoreType.DMA((20,)),
-        ],
+    arrays, strips = 4 * pairs + 1, 4 * tiles + per
+    edge, slab, moving = kept(5, rows, LANES), kept(strips, DEPTH, LANES), kept(strips + 5, DEPTH, LANES)
+    inputs = [imbalance, flow, potential, cost]
+    left, right, own_up, own_down = call(
+        functools.partial(edge_kernel, pairs),
+        [edge, edge, slab, slab],
+        [pltpu.with_memory_space_constraint(x, pltpu.MemorySpace.HBM) for x in inputs],
+        scratch=[kept(arrays, SLAB, cols)] * 2 + [kept(arrays, rows, LANES)] * 2 + [pltpu.SemaphoreType.DMA((20,))],
         space=pltpu.MemorySpace.HBM,
     )
-    side = neighbour(left, "gx", -1) + neighbour(right, "gx", 1)
+    left, right = neighbour(left, "gx", -1), neighbour(right, "gx", 1)
+    up, down = call(functools.partial(slab_kernel, rows), [moving] * 2, [left, right, own_up, own_down])
     bottom, top = neighbour(up, "gy", -1), neighbour(down, "gy", 1)
-    side_bottom = neighbour(side[:, :DEPTH], "gy", -1)
-    side_top = neighbour(side[:, rows - DEPTH :], "gy", 1)
 
     field = kept(tiles + 1, height, LANES)
+    fields = [field] * 5 + [kept(per + 1, height, LANES)]
+    started = call(functools.partial(assemble_kernel, pairs), fields, inputs + [left, right], flops=40_000_000)
     u, a, b, q, source, price = call(
-        functools.partial(assemble_kernel, pairs),
-        [field] * 5 + [kept(per + 1, height, LANES)],
-        [imbalance, flow, potential, cost, top, bottom, side, side_top, side_bottom],
-        limit=16,
+        functools.partial(adopt_kernel, pairs),
+        fields,
+        [top, bottom, *started],
+        aliases={k + 2: k for k in range(6)},
     )
     rates = jnp.full((8, LANES), initial_step, jnp.float32)
     recv = jnp.zeros((devices, LANES), jnp.float32)

time: 184 us -> 177 us (0.962)
  starting transfers between devices: 27 us -> 20.6 us
  local copies, waits for them, and re-layouts: 7.3 us -> 2.31 us
  waiting for transfers between devices: 6.26 us -> 10.2 us
  blocking collectives: 108 us -> 110 us
    ppermute x10 -> x8, starting transfers between devices: 24.5 us -> 18 us  [neighbour(): lax.ppermute(value, axis, [(source, source + steps) for source in range(l...]
    unnamed x18 -> x10, local copies, waits for them, and re-layouts: 7.29 us -> 2.31 us
    ppermute x10 -> x8, waiting for transfers between devices: 1.37 us -> 5.36 us  [neighbour(): lax.ppermute(value, axis, [(source, source + steps) for source in range(l...]
    all_to_all x11, blocking collectives: 108 us -> 110 us  [exchange(): return lax.all_to_all(send, AXES, 0, 0, tiled=True)]
    pallas_call x16 -> x18, Pallas kernels: 33.5 us -> 32 us  [call(): pl.pallas_call(kernel, out_shape=out_shape, in_specs=[pl.BlockSpec(memory...]
  transfers between devices with their start and end apart: 11 -> 9, of which waited for: 4 -> 3; matrix products, arithmetic and copies ran while one was open for 1% -> 1% of each run, Pallas kernels for 0% -> 1%
where the time goes in v3:
time: 177 us
  blocking collectives  110 us (62%)
  Pallas kernels  32 us (18%)
  starting transfers between devices  20.6 us (12%)
  waiting for transfers between devices  10.2 us (6%)
  local copies, waits for them, and re-layouts  2.31 us (1%)
    all_to_all x11, blocking collectives, exchange(): return lax.all_to_all(send, AXES, 0, 0, tiled=True)  110 us
    pallas_call x18, Pallas kernels, call(): pl.pallas_call(kernel, out_shape=out_shape, in_specs=[pl.BlockSpec(memory...  32 us
    ppermute x8, starting transfers between devices, neighbour(): lax.ppermute(value, axis, [(source, source + steps) for source in range(l...  18 us
    ppermute x8, waiting for transfers between devices, neighbour(): lax.ppermute(value, axis, [(source, source + steps) for source in range(l...  5.36 us
    all_to_all x1, waiting for transfers between devices, exchange(): return lax.all_to_all(send, AXES, 0, 0, tiled=True)  4.89 us
  transfers between devices with their start and end apart: 9, of which 3 were waited for; matrix products, arithmetic and copies ran while one was open for 1% of the time, Pallas kernels for 1%

profile of v3, /device:TPU:0, one launch (start us, length us, event | category | flops | bytes accessed | tf_op | source)
XLA Modules:
  0.0 176.9 jit_solution(14402589367171082688)
XLA Ops:
  4.3 3.1 %collective-permute-start.1 = (f32[5,128,128]{2,1,0:T(8,128)S(1)}, f32[5,128,128]{2,1,0:T(8,128)S(1)}, u32[]{:S(2)}, u32[]{:S(2)}) collective-permute-start(f32[5,128,128]{2,1,0:T(8,128)S(1)} %get-tuple-element.103), channel_id=1, source_target_pairs={{0,1},{1,2},{2,3},{4,5},{5,6},{6,7},{8,9},{9,10},{10,11},{12,13},{... | collective-permute-start | bytes 983048 | tf_op jit(solution)/shard_map/ppermute | solution.py:27
  8.6 4.9 %collective-permute-start.2 = (f32[73,4,128]{2,1,0:T(4,128)S(1)}, f32[73,4,128]{2,1,0:T(4,128)S(1)}, u32[]{:S(2)}, u32[]{:S(2)}) collective-permute-start(f32[73,4,128]{2,1,0:T(4,128)S(1)} %get-tuple-element.106), channel_id=1, source_target_pairs={{0,4},{4,8},{8,12},{12,16},{16,20},{20,24},{24,28},{1,5},{5,9},{9,... | collective-permute-start | bytes 448520 | tf_op jit(solution)/shard_map/ppermute | solution.py:27
  16.4 4.1 %collective-permute-done.3.bottom = f32[73,4,128]{2,1,0:T(4,128)S(1)} collective-permute-done((f32[73,4,128]{2,1,0:T(4,128)S(1)}, f32[73,4,128]{2,1,0:T(4,128)S(1)}, u32[]{:S(2)}, u32[]{:S(2)}) %collective-permute-start.3) | collective-permute-done | bytes 149536 | tf_op jit(solution)/shard_map/ppermute | solution.py:27
  20.7 2.3 %shard_map.71 = (f32[17,160,128]{2,1,0:T(8,128)S(1)}, f32[17,160,128]{2,1,0:T(8,128)S(1)}, f32[17,160,128]{2,1,0:T(8,128)S(1)}, f32[17,160,128]{2,1,0:T(8,128)S(...) custom-call(f32[32,128]{1,0:T(8,128)S(1)} %broadcast_in_dim.6.recv, f32[8,128]{1,0:T(8,128)S(1)} %broadcast_in_dim.7.rates, ...), custom_call_target="tpu_custom_call" | custom-call | tf_op jit(solution)/shard_map/pallas_call | solution.py:366
  23.0 17.5 %all_to_all.130 = f32[32,1,128]{2,1,0:T(1,128)S(1)} all-to-all(f32[32,1,128]{2,1,0:T(1,128)S(1)} %bitcast.62), channel_id=1, replica_groups=mesh['gy'=8,'gx'=4] {'gy','gx'}, dimensions={0} | all-to-all | bytes 32768 | tf_op jit(solution)/shard_map/all_to_all | solution.py:383
  42.8 8.9 %all_to_all.131 = f32[32,1,128]{2,1,0:T(1,128)S(1)} all-to-all(f32[32,1,128]{2,1,0:T(1,128)S(1)} %bitcast.63), channel_id=1, replica_groups=mesh['gy'=8,'gx'=4] {'gy','gx'}, dimensions={0} | all-to-all | bytes 32768 | tf_op jit(solution)/shard_map/all_to_all | solution.py:383
  51.6 2.3 %shard_map.73 = (f32[17,160,128]{2,1,0:T(8,128)S(1)}, f32[17,160,128]{2,1,0:T(8,128)S(1)}, f32[17,160,128]{2,1,0:T(8,128)S(1)}, f32[17,160,128]{2,1,0:T(8,128)S(...) custom-call(f32[32,128]{1,0:T(8,128)S(1)} %bitcast.54, f32[8,128]{1,0:T(8,128)S(1)} %get-tuple-element.127.rates, ...), custom_call_target="tpu_custom_call" | custom-call | tf_op jit(solution)/shard_map/pallas_call | solution.py:366
  54.0 8.9 %all_to_all.132 = f32[32,1,128]{2,1,0:T(1,128)S(1)} all-to-all(f32[32,1,128]{2,1,0:T(1,128)S(1)} %bitcast.64), channel_id=1, replica_groups=mesh['gy'=8,'gx'=4] {'gy','gx'}, dimensions={0} | all-to-all | bytes 32768 | tf_op jit(solution)/shard_map/all_to_all | solution.py:383
  62.8 2.3 %shard_map.74 = (f32[17,160,128]{2,1,0:T(8,128)S(1)}, f32[17,160,128]{2,1,0:T(8,128)S(1)}, f32[17,160,128]{2,1,0:T(8,128)S(1)}, f32[17,160,128]{2,1,0:T(8,128)S(...) custom-call(f32[32,128]{1,0:T(8,128)S(1)} %bitcast.51, ...), custom_call_target="tpu_custom_call" | custom-call | tf_op jit(solution)/shard_map/pallas_call | solution.py:366
  65.2 2.5 %collective-permute-start.4 = (f32[4,17,4,128]{3,2,1,0:T(4,128)S(1)}, f32[4,17,4,128]{3,2,1,0:T(4,128)S(1)}, u32[]{:S(2)}, u32[]{:S(2)}) collective-permute-start(f32[4,17,4,128]{3,2,1,0:T(4,128)S(1)} %get-tuple-element.140), channel_id=1, source_target_pairs={{0,4},{4,8},{8,12},{12,16},{16,20},{20,24},{24,28},{1,5},{5,9},{9,... | collective-permute-start | bytes 417800 | tf_op jit(solution)/shard_map/ppermute | solution.py:27
  68.9 10.9 %all_to_all.133 = f32[32,1,128]{2,1,0:T(1,128)S(1)} all-to-all(f32[32,1,128]{2,1,0:T(1,128)S(1)} %bitcast.60), channel_id=1, replica_groups=mesh['gy'=8,'gx'=4] {'gy','gx'}, dimensions={0} | all-to-all | bytes 32768 | tf_op jit(solution)/shard_map/all_to_all | solution.py:383
  82.2 8.9 %all_to_all.134 = f32[32,1,128]{2,1,0:T(1,128)S(1)} all-to-all(f32[32,1,128]{2,1,0:T(1,128)S(1)} %bitcast.65), channel_id=1, replica_groups=mesh['gy'=8,'gx'=4] {'gy','gx'}, dimensions={0} | all-to-all | bytes 32768 | tf_op jit(solution)/shard_map/all_to_all | solution.py:383
  93.3 8.9 %all_to_all.135 = f32[32,1,128]{2,1,0:T(1,128)S(1)} all-to-all(f32[32,1,128]{2,1,0:T(1,128)S(1)} %bitcast.66), channel_id=1, replica_groups=mesh['gy'=8,'gx'=4] {'gy','gx'}, dimensions={0} | all-to-all | bytes 32768 | tf_op jit(solution)/shard_map/all_to_all | solution.py:383
  102.2 2.3 %shard_map.78 = (f32[17,160,128]{2,1,0:T(8,128)S(1)}, f32[17,160,128]{2,1,0:T(8,128)S(1)}, f32[17,160,128]{2,1,0:T(8,128)S(1)}, f32[17,160,128]{2,1,0:T(8,128)S(...) custom-call(f32[32,128]{1,0:T(8,128)S(1)} %bitcast.56, f32[8,128]{1,0:T(8,128)S(1)} %get-tuple-element.157.rates, ...), custom_call_target="tpu_custom_call" | custom-call | tf_op jit(solution)/shard_map/pallas_call | solution.py:366
  104.5 8.9 %all_to_all.136 = f32[32,1,128]{2,1,0:T(1,128)S(1)} all-to-all(f32[32,1,128]{2,1,0:T(1,128)S(1)} %bitcast.67), channel_id=1, replica_groups=mesh['gy'=8,'gx'=4] {'gy','gx'}, dimensions={0} | all-to-all | bytes 32768 | tf_op jit(solution)/shard_map/all_to_all | solution.py:383
  113.4 2.3 %shard_map.79 = (f32[17,160,128]{2,1,0:T(8,128)S(1)}, f32[17,160,128]{2,1,0:T(8,128)S(1)}, f32[17,160,128]{2,1,0:T(8,128)S(1)}, f32[17,160,128]{2,1,0:T(8,128)S(...) custom-call(f32[32,128]{1,0:T(8,128)S(1)} %bitcast.52, ...), custom_call_target="tpu_custom_call" | custom-call | tf_op jit(solution)/shard_map/pallas_call | solution.py:366
  115.7 2.5 %collective-permute-start.6 = (f32[4,17,4,128]{3,2,1,0:T(4,128)S(1)}, f32[4,17,4,128]{3,2,1,0:T(4,128)S(1)}, u32[]{:S(2)}, u32[]{:S(2)}) collective-permute-start(f32[4,17,4,128]{3,2,1,0:T(4,128)S(1)} %get-tuple-element.170), channel_id=1, source_target_pairs={{0,4},{4,8},{8,12},{12,16},{16,20},{20,24},{24,28},{1,5},{5,9},{9,... | collective-permute-start | bytes 417800 | tf_op jit(solution)/shard_map/ppermute | solution.py:27
  119.5 10.9 %all_to_all.137 = f32[32,1,128]{2,1,0:T(1,128)S(1)} all-to-all(f32[32,1,128]{2,1,0:T(1,128)S(1)} %bitcast.61), channel_id=1, replica_groups=mesh['gy'=8,'gx'=4] {'gy','gx'}, dimensions={0} | all-to-all | bytes 32768 | tf_op jit(solution)/shard_map/all_to_all | solution.py:383
  132.8 8.9 %all_to_all.138 = f32[32,1,128]{2,1,0:T(1,128)S(1)} all-to-all(f32[32,1,128]{2,1,0:T(1,128)S(1)} %bitcast.68), channel_id=1, replica_groups=mesh['gy'=8,'gx'=4] {'gy','gx'}, dimensions={0} | all-to-all | bytes 32768 | tf_op jit(solution)/shard_map/all_to_all | solution.py:383
  143.9 8.9 %all_to_all.139 = f32[32,1,128]{2,1,0:T(1,128)S(1)} all-to-all(f32[32,1,128]{2,1,0:T(1,128)S(1)} %bitcast.69), channel_id=1, replica_groups=mesh['gy'=8,'gx'=4] {'gy','gx'}, dimensions={0} | all-to-all | bytes 32768 | tf_op jit(solution)/shard_map/all_to_all | solution.py:383
  155.0 8.9 %all_to_all.140 = f32[32,1,128]{2,1,0:T(1,128)S(1)} all-to-all(f32[32,1,128]{2,1,0:T(1,128)S(1)} %bitcast.70), channel_id=1, replica_groups=mesh['gy'=8,'gx'=4] {'gy','gx'}, dimensions={0} | all-to-all | bytes 32768 | tf_op jit(solution)/shard_map/all_to_all | solution.py:383
  163.9 2.8 %shard_map.84 = (f32[2,4,128,512]{3,2,1,0:T(8,128)S(1)}, f32[4,128,512]{2,1,0:T(8,128)S(1)}, f32[32,128]{1,0:T(8,128)}) custom-call(f32[32,128]{1,0:T(8,128)S(1)} %bitcast.59, f32[8,128]{1,0:T(8,128)S(1)} %get-tuple-element.193.rates, f32[5,160,128]{2,1,0:T(8,128)S(1)} %get-tuple-element.114.price, f32[17,160,128]{2,1,0:T(8,128)S(1)} %get-tuple-element.115.source, ...), custom_call_target="tpu_custom_call" | custom-call | tf_op jit(solution)/shard_map/pallas_call | solution.py:366
  166.7 2.5 %all-to-all-start.11 = ((f32[32,1,128]{2,1,0:T(1,128)}), f32[32,1,128]{2,1,0:T(1,128)S(1)}, u32[]{:S(2)}, u32[]{:S(2)}) async-start(f32[32,1,128]{2,1,0:T(1,128)} %bitcast.34), calls=%async_computation.11 | async-start | bytes 32768 | tf_op jit(solution)/shard_map/all_to_all | solution.py:383
  171.5 4.9 %all-to-all-done.11 = f32[32,1,128]{2,1,0:T(1,128)S(1)} async-done(((f32[32,1,128]{2,1,0:T(1,128)}), f32[32,1,128]{2,1,0:T(1,128)S(1)}, u32[]{:S(2)}, u32[]{:S(2)}) %all-to-all-start.11) | async-done | bytes 16416 | tf_op jit(solution)/shard_map/all_to_all | solution.py:383
  (37 shorter events, 26.9 us)
Async XLA Ops:
  0.6 14.1 %copy-start = (f32[2,4,128,512]{3,2,1,0:T(8,128)S(1)}, f32[2,4,128,512]{3,2,1,0:T(8,128)}, u32[]{:S(2)}) copy-start(f32[2,4,128,512]{3,2,1,0:T(8,128)} %flow.3) | copy-start | bytes 6291460
  0.6 14.1 %copy-start.1 = (f32[4,128,512]{2,1,0:T(8,128)S(1)}, f32[4,128,512]{2,1,0:T(8,128)}, u32[]{:S(2)}) copy-start(f32[4,128,512]{2,1,0:T(8,128)} %imb.3) | copy-start | bytes 3145732
  0.7 14.1 %copy-start.2 = (f32[4,128,512]{2,1,0:T(8,128)S(1)}, f32[4,128,512]{2,1,0:T(8,128)}, u32[]{:S(2)}) copy-start(f32[4,128,512]{2,1,0:T(8,128)} %pot.3) | copy-start | bytes 3145732
  0.7 14.1 %copy-start.3 = (f32[128,512]{1,0:T(8,128)S(1)}, f32[128,512]{1,0:T(8,128)}, u32[]{:S(2)}) copy-start(f32[128,512]{1,0:T(8,128)} %cost.3) | copy-start | bytes 786436
  3.0 4.4 %collective-permute-start = (f32[5,128,128]{2,1,0:T(8,128)S(1)}, f32[5,128,128]{2,1,0:T(8,128)S(1)}, u32[]{:S(2)}, u32[]{:S(2)}) collective-permute-start(f32[5,128,128]{2,1,0:T(8,128)S(1)} %get-tuple-element.102), channel_id=1, source_target_pairs={{1,0},{2,1},{3,2},{5,4},{6,5},{7,6},{9,8},{10,9},{11,10},{13,12},{... | collective-permute-start | bytes 983048 | tf_op jit(solution)/shard_map/ppermute | solution.py:27
  4.3 4.3 %collective-permute-start.1 = (f32[5,128,128]{2,1,0:T(8,128)S(1)}, f32[5,128,128]{2,1,0:T(8,128)S(1)}, u32[]{:S(2)}, u32[]{:S(2)}) collective-permute-start(f32[5,128,128]{2,1,0:T(8,128)S(1)} %get-tuple-element.103), channel_id=1, source_target_pairs={{0,1},{1,2},{2,3},{4,5},{5,6},{6,7},{8,9},{9,10},{10,11},{12,13},{... | collective-permute-start | bytes 983048 | tf_op jit(solution)/shard_map/ppermute | solution.py:27
  8.6 7.8 %collective-permute-start.2 = (f32[73,4,128]{2,1,0:T(4,128)S(1)}, f32[73,4,128]{2,1,0:T(4,128)S(1)}, u32[]{:S(2)}, u32[]{:S(2)}) collective-permute-start(f32[73,4,128]{2,1,0:T(4,128)S(1)} %get-tuple-element.106), channel_id=1, source_target_pairs={{0,4},{4,8},{8,12},{12,16},{16,20},{20,24},{24,28},{1,5},{5,9},{9,... | collective-permute-start | bytes 448520 | tf_op jit(solution)/shard_map/ppermute | solution.py:27
  13.4 7.1 %collective-permute-start.3 = (f32[73,4,128]{2,1,0:T(4,128)S(1)}, f32[73,4,128]{2,1,0:T(4,128)S(1)}, u32[]{:S(2)}, u32[]{:S(2)}) collective-permute-start(f32[73,4,128]{2,1,0:T(4,128)S(1)} %get-tuple-element.107), channel_id=1, source_target_pairs={{4,0},{8,4},{12,8},{16,12},{20,16},{24,20},{28,24},{5,1},{9,5},{13... | collective-permute-start | bytes 448520 | tf_op jit(solution)/shard_map/ppermute | solution.py:27
  65.2 14.7 %collective-permute-start.4 = (f32[4,17,4,128]{3,2,1,0:T(4,128)S(1)}, f32[4,17,4,128]{3,2,1,0:T(4,128)S(1)}, u32[]{:S(2)}, u32[]{:S(2)}) collective-permute-start(f32[4,17,4,128]{3,2,1,0:T(4,128)S(1)} %get-tuple-element.140), channel_id=1, source_target_pairs={{0,4},{4,8},{8,12},{12,16},{16,20},{20,24},{24,28},{1,5},{5,9},{9,... | collective-permute-start | bytes 417800 | tf_op jit(solution)/shard_map/ppermute | solution.py:27
  67.6 12.2 %collective-permute-start.5 = (f32[4,17,4,128]{3,2,1,0:T(4,128)S(1)}, f32[4,17,4,128]{3,2,1,0:T(4,128)S(1)}, u32[]{:S(2)}, u32[]{:S(2)}) collective-permute-start(f32[4,17,4,128]{3,2,1,0:T(4,128)S(1)} %get-tuple-element.141), channel_id=1, source_target_pairs={{4,0},{8,4},{12,8},{16,12},{20,16},{24,20},{28,24},{5,1},{9,5},{13... | collective-permute-start | bytes 417800 | tf_op jit(solution)/shard_map/ppermute | solution.py:27
  115.7 14.7 %collective-permute-start.6 = (f32[4,17,4,128]{3,2,1,0:T(4,128)S(1)}, f32[4,17,4,128]{3,2,1,0:T(4,128)S(1)}, u32[]{:S(2)}, u32[]{:S(2)}) collective-permute-start(f32[4,17,4,128]{3,2,1,0:T(4,128)S(1)} %get-tuple-element.170), channel_id=1, source_target_pairs={{0,4},{4,8},{8,12},{12,16},{16,20},{20,24},{24,28},{1,5},{5,9},{9,... | collective-permute-start | bytes 417800 | tf_op jit(solution)/shard_map/ppermute | solution.py:27
  118.2 12.2 %collective-permute-start.7 = (f32[4,17,4,128]{3,2,1,0:T(4,128)S(1)}, f32[4,17,4,128]{3,2,1,0:T(4,128)S(1)}, u32[]{:S(2)}, u32[]{:S(2)}) collective-permute-start(f32[4,17,4,128]{3,2,1,0:T(4,128)S(1)} %get-tuple-element.171), channel_id=1, source_target_pairs={{4,0},{8,4},{12,8},{16,12},{20,16},{24,20},{28,24},{5,1},{9,5},{13... | collective-permute-start | bytes 417800 | tf_op jit(solution)/shard_map/ppermute | solution.py:27
  166.7 9.7 %all-to-all-start.11 = ((f32[32,1,128]{2,1,0:T(1,128)}), f32[32,1,128]{2,1,0:T(1,128)S(1)}, u32[]{:S(2)}, u32[]{:S(2)}) async-start(f32[32,1,128]{2,1,0:T(1,128)} %bitcast.34), calls=%async_computation.11 | async-start | bytes 32768 | tf_op jit(solution)/shard_map/all_to_all | solution.py:383

commit v4 on v3

v4 whole, which is shorter than its diff:
```python
import functools

import jax
import jax.numpy as jnp
from jax import lax
from jax.experimental import pallas as pl
from jax.experimental.pallas import tpu as pltpu
from jax.sharding import PartitionSpec as P

ITERS = 12
initial_step = 0.35
epsilon = 1e-06

DEPTH = 6
SIDE = ITERS
SLAB = 8
PAD = 8
TOP = PAD + SLAB
LANES = 128
CHUNK = 32
AXES = ("gy", "gx")


def neighbour(value, axis, steps):
    count = lax.axis_size(axis)
    leading, last = (max(0, -steps), min(count, count - steps))
    return lax.ppermute(value, axis, [(source, source + steps) for source in range(leading, last)])


def rolled(value, shift):
    shift = shift % LANES
    return pltpu.roll(value, shift, 1) if shift else value


def edge_kernel(pairs, imb, flow, pot, cost, left, right, up, down, top, bottom, first, last, sems):
    rows, cols = cost.shape
    per, group = cols // LANES, LANES // pairs
    fields = [pot, flow.at[0], flow.at[1], imb]
    copies = []

    def fetch(source, target):
        copies.append(pltpu.make_async_copy(source, target, sems.at[len(copies)]))

    for k, field in enumerate(fields):
        fetch(field.at[:, :, 0:LANES], first.at[pl.ds(k * pairs, pairs)])
        fetch(field.at[:, :, cols - LANES : cols], last.at[pl.ds(k * pairs, pairs)])
    fetch(cost.at[:, 0:LANES], first.at[4 * pairs])
    fetch(cost.at[:, cols - LANES : cols], last.at[4 * pairs])
    sides = len(copies)
    for k, field in enumerate(fields):
        fetch(field.at[:, 0:SLAB, :], top.at[pl.ds(k * pairs, pairs)])
        fetch(field.at[:, rows - SLAB : rows, :], bottom.at[pl.ds(k * pairs, pairs)])
    fetch(cost.at[0:SLAB, :], top.at[4 * pairs])
    fetch(cost.at[rows - SLAB : rows, :], bottom.at[4 * pairs])
    for copy in copies:
        copy.start()
    count = 32
    lane = lax.broadcasted_iota(jnp.int32, (count, LANES), 1)
    inner, which = lane % group, lane // group
    for k in range(5):
        for copy in copies[2 * k : 2 * k + 2]:
            copy.wait()
        for start in range(0, rows, count):
            span = slice(start, start + count)
            head = jnp.zeros((count, LANES), jnp.float32)
            tail = jnp.zeros((count, LANES), jnp.float32)
            for p in range(pairs):
                n = min(k * pairs + p, 4 * pairs)
                head = jnp.where((which == p) & (inner < SIDE), rolled(first[n, span, :], group * p), head)
                tail = jnp.where((which == p) & (inner >= group - SIDE), rolled(last[n, span, :], group * (p + 1)), tail)
            left[k, span, :] = head
            right[k, span, :] = tail
    for copy in copies[sides:]:
        copy.wait()
    for n in range(4 * pairs + 1):
        for c in range(per):
            span = slice(c * LANES, (c + 1) * LANES)
            up[strip(n * per + c), :] = top[n, 0:DEPTH, span]
            down[strip(n * per + c), :] = bottom[n, SLAB - DEPTH : SLAB, span]


def strip(n):
    return slice(n * DEPTH, (n + 1) * DEPTH)


def strips(count):
    return kept(-(-count * DEPTH // 8) * 8, LANES)


def slab_kernel(rows, count, left, right, own_up, own_down, up, down):
    up[0 : count * DEPTH, :] = own_up[0 : count * DEPTH, :]
    down[0 : count * DEPTH, :] = own_down[0 : count * DEPTH, :]
    for k in range(5):
        up[strip(count + k), :] = left[k, 0:DEPTH, :] + right[k, 0:DEPTH, :]
        down[strip(count + k), :] = left[k, rows - DEPTH : rows, :] + right[k, rows - DEPTH : rows, :]


def own_masks(pairs):
    gy, gx = lax.axis_index("gy"), lax.axis_index("gx")
    above = jnp.where(gy > 0, 1.0, 0.0).astype(jnp.float32)
    below = jnp.where(gy < lax.axis_size("gy") - 1, 1.0, 0.0).astype(jnp.float32)
    inner = lax.broadcasted_iota(jnp.int32, (1, LANES), 1) % (LANES // pairs)
    to_right = (inner < SIDE) & (gx < lax.axis_size("gx") - 1)
    to_left = (inner >= LANES // pairs - SIDE) & (gx > 0)
    sides = jnp.where(to_right | to_left, 1.0, 0.0).astype(jnp.float32)
    return above, below, sides


def assemble_kernel(pairs, imb, flow, pot, cost, left, right, u, a, b, source, price):
    rows, cols = cost.shape
    per = cols // LANES
    tiles = pairs * per
    end = TOP + rows
    fields = [(u, pot), (a, flow.at[0]), (b, flow.at[1]), (source, imb)]
    blank = jnp.zeros((tiles + 1, TOP, LANES), jnp.float32)
    for k, (into, field) in enumerate(fields):
        into[:, 0:TOP, :] = blank
        into[:, end : end + TOP, :] = blank
        for p in range(pairs):
            for c in range(per):
                into[p * per + c, TOP:end, :] = field[p, :, c * LANES : (c + 1) * LANES]
        into[tiles, TOP:end, :] = left[k] + right[k]
    sides = own_masks(pairs)[2]
    price[:, 0:TOP, :] = jnp.ones((per + 1, TOP, LANES), jnp.float32)
    price[:, end : end + TOP, :] = jnp.ones((per + 1, TOP, LANES), jnp.float32)
    for c in range(per):
        price[c, TOP:end, :] = cost[:, c * LANES : (c + 1) * LANES]
    price[per, TOP:end, :] = jnp.where(sides > 0.0, left[4] + right[4], 1.0)


def adopt_kernel(pairs, rows, top, bottom, u, a, b, source, price, u_out, a_out, b_out, source_out, price_out):
    per = price.shape[0] - 1
    tiles = pairs * per
    end, count = TOP + rows, 4 * tiles + per
    above, below, sides = own_masks(pairs)
    for span, slab, mask in ((slice(TOP - DEPTH, TOP), top, above), (slice(end, end + DEPTH), bottom, below)):
        for k, out in enumerate((u_out, a_out, b_out, source_out)):
            for t in range(tiles):
                out[t, span, :] = slab[strip(k * tiles + t), :]
            out[tiles, span, :] = slab[strip(count + k), :]
        for c in range(per):
            price_out[c, span, :] = slab[strip(4 * tiles + c), :] + (1.0 - mask)
        price_out[per, span, :] = jnp.where(sides * mask > 0.0, slab[strip(count + 4), :], 1.0)


def from_left(pairs, per, b, start, count, cell, closing=False):
    group, tiles = LANES // pairs, pairs * per
    span = pl.ds(start, count)
    lane = lax.broadcasted_iota(jnp.int32, (count, LANES), 1)
    side = b[tiles, span, :]
    moved_side = rolled(side, 1)
    for p in range(pairs):
        before = rolled(side, -(group * p + group - 1))
        for c in range(per):
            here = b[p * per + c, span, :]
            moved = rolled(here, 1)
            cell(p * per + c, p, here, jnp.where(lane == 0, before, moved))
            before = moved
        if not closing:
            moved_side = jnp.where(lane == group * p, rolled(before, group * p), moved_side)
    if not closing:
        cell(tiles, None, side, moved_side)


def from_right(pairs, per, u, start, count, cell):
    group, tiles = LANES // pairs, pairs * per
    span = pl.ds(start, count)
    lane = lax.broadcasted_iota(jnp.int32, (count, LANES), 1)
    side = u[tiles, span, :]
    moved_side = rolled(side, -1)
    for p in range(pairs):
        after = rolled(side, -1 - group * p)
        for c in reversed(range(per)):
            here = u[p * per + c, span, :]
            moved = rolled(here, -1)
            cell(p * per + c, p, here, jnp.where(lane == LANES - 1, after, moved))
            after = moved
        moved_side = jnp.where(lane == group * p + group - 1, rolled(after, group * p + group), moved_side)
    cell(tiles, None, side, moved_side)


def folded(value):
    return jnp.sum(value.reshape(-1, 8, LANES), axis=0)


def same_parity(value):
    value = value + pltpu.roll(value, 2, 0)
    return value + pltpu.roll(value, 4, 0)


def next_rates(recv, rates):
    total = same_parity(folded(recv[...])) + epsilon
    ratio = total / pltpu.roll(total, 1, 0)
    return rates[...] * lax.rsqrt(lax.rsqrt(ratio))


def spread_rates(pairs, rates):
    group = lax.broadcasted_iota(jnp.int32, (8, LANES), 1) // (LANES // pairs)
    each = [jnp.max(jnp.where(group == p, rates, 0.0), axis=1, keepdims=True) for p in range(pairs)]
    each = [jnp.broadcast_to(value, (8, LANES)) for value in each]
    return [v[1:2] for v in each], rates[1:2], [v[0:1] for v in each], rates[0:1]


def sums_to_send(pairs, even, odd):
    row = lax.broadcasted_iota(jnp.int32, (8, LANES), 0)
    group = lax.broadcasted_iota(jnp.int32, (8, LANES), 1) // (LANES // pairs)
    matrix = jnp.zeros((8, LANES), jnp.float32)
    for p in range(pairs):
        for k, part in ((2 * p, even[p]), (2 * p + 1, odd[p])):
            if part is not None:
                matrix = jnp.where(row == k, jnp.sum(part, axis=0, keepdims=True), matrix)
    sums = jnp.sum(matrix, axis=1, keepdims=True)
    return same_parity(jnp.where(group == row // 2, sums, 0.0))


def put_sums(send, sums):
    for start in range(0, send.shape[0], 8):
        send[start : start + 8, :] = sums


def primal_rows(pairs, per, start, count, taus, tau_side, row_mask, sides, price, u, a, b, a_out, b_out, a_far, b_far, sums):
    span, later = pl.ds(start, count), pl.ds(start + 1, count)
    sums = list(sums)
    side_rate = tau_side * sides if row_mask is None else tau_side * sides * row_mask
    masked = taus if row_mask is None else [tau * row_mask for tau in taus]

    def cell(t, p, here, right):
        rate, grad_rate = (tau_side, side_rate) if p is None else (taus[p], masked[p])
        cost = price[per if p is None else t % per, span, :]
        old_down, old_right = a[t, span, :], b[t, span, :]
        down = old_down + grad_rate * (u[t, later, :] - here)
        across = old_right + grad_rate * (right - here)
        square = down * down + across * across
        factor = jnp.maximum(1.0 - (rate * cost) * lax.rsqrt(square), 0.0)
        new_down, new_right = factor * down, factor * across
        a_out[t, span, :] = new_down
        b_out[t, span, :] = new_right
        change_down, change_right = new_down - old_down, new_right - old_right
        a_far[t, span, :] = new_down + change_down
        b_far[t, span, :] = new_right + change_right
        if sums and p is not None:
            sums[p] = sums[p] + folded(change_down * change_down + change_right * change_right)

    from_right(pairs, per, u, start, count, cell)
    return sums


def dual_rows(pairs, per, start, count, sigmas, sigma_side, source, a_far, b_far, u, u_out, sums):
    span, earlier = pl.ds(start, count), pl.ds(start - 1, count)
    sums = list(sums)

    def cell(t, p, here, left):
        spread = a_far[t, span, :] - a_far[t, earlier, :] + (here - left)
        change = (sigma_side if p is None else sigmas[p]) * (spread - source[t, span, :])
        u_out[t, span, :] = u[t, span, :] + change
        if sums and p is not None:
            sums[p] = sums[p] + folded(change * change)

    from_left(pairs, per, b_far, start, count, cell)
    return sums


def iterate_kernel(pairs, rows, sending, recv, rates, price, source, u, a, b, u_out, a_out, b_out, send, rates_out, *rest):
    slabs, (a_far, b_far) = rest[:-2], rest[-2:]
    per = price.shape[0] - 1
    tiles = pairs * per
    end, last = TOP + rows, rows // CHUNK - 1
    rates_now = next_rates(recv, rates)
    rates_out[...] = rates_now
    taus, tau_side, sigmas, sigma_side = spread_rates(pairs, rates_now)
    above, below, sides = own_masks(pairs)
    a_far[:, 0:PAD, :] = jnp.zeros((tiles + 1, PAD, LANES), jnp.float32)
    u_out[:, end + SLAB : end + TOP, :] = jnp.zeros((tiles + 1, PAD, LANES), jnp.float32)

    def primal(start, count, mask, sums):
        return primal_rows(
            pairs, per, start, count, taus, tau_side, mask, sides, price, u, a, b, a_out, b_out, a_far, b_far, sums
        )

    def dual(start, count, mask, sums):
        now = sigmas if mask is None else [sigma * mask for sigma in sigmas]
        side_now = sigma_side * sides if mask is None else sigma_side * sides * mask
        return dual_rows(pairs, per, start, count, now, side_now, source, a_far, b_far, u, u_out, sums)

    zeros = [jnp.zeros((8, LANES), jnp.float32)] * pairs
    primal(PAD, SLAB, above, ())
    dual(PAD, SLAB, above, ())
    primals = primal(TOP, CHUNK, None, zeros)

    def turn(k, carried):
        primals, duals = carried
        start = TOP + k * CHUNK
        primals = primal(start, CHUNK, None, primals)
        duals = dual(start - CHUNK, CHUNK, None, duals)
        return tuple(primals), tuple(duals)

    primals, duals = lax.fori_loop(1, last + 1, turn, (tuple(primals), tuple(zeros)))
    primal(end, SLAB, below, ())
    duals = dual(TOP + last * CHUNK, CHUNK, None, duals)
    dual(end, SLAB, below, ())
    put_sums(send, sums_to_send(pairs, primals, duals))
    if sending:
        up, down = slabs
        for k, out in enumerate((u_out, a_out, b_out)):
            for t in range(tiles + 1):
                up[strip(k * (tiles + 1) + t), :] = out[t, TOP : TOP + DEPTH, :]
                down[strip(k * (tiles + 1) + t), :] = out[t, end - DEPTH : end, :]


def merge_kernel(rows, recv, top, bottom, u, a, b, u_out, a_out, b_out):
    tiles = u.shape[0]
    for k, out in enumerate((u_out, a_out, b_out)):
        for t in range(tiles):
            out[t, TOP - DEPTH : TOP, :] = top[strip(k * tiles + t), :]
            out[t, TOP + rows : TOP + rows + DEPTH, :] = bottom[strip(k * tiles + t), :]


def closing_kernel(
    pairs, recv, rates, price, source, u, a, b, flow_out, pot_out, send, a_new, b_new, a_far, b_far
):
    per = price.shape[0] - 1
    rows = pot_out.shape[1]
    taus, tau_side, sigmas, _ = spread_rates(pairs, next_rates(recv, rates))
    above, _, sides = own_masks(pairs)

    def primal(start, count, mask):
        primal_rows(
            pairs, per, start, count, taus, tau_side, mask, sides, price, u, a, b, a_new, b_new, a_far, b_far, ()
        )

    def close(k, sums):
        sums = list(sums)
        start = TOP + k * CHUNK
        span, earlier, own = pl.ds(start, CHUNK), pl.ds(start - 1, CHUNK), pl.ds(k * CHUNK, CHUNK)

        def lanes(t):
            return slice(t % per * LANES, (t % per + 1) * LANES)

        def shortfall(t, p, here, left):
            down = a_new[t, span, :]
            missing = down - a_new[t, earlier, :] + (here - left) - source[t, span, :]
            flow_out[0, p, own, lanes(t)] = down
            flow_out[1, p, own, lanes(t)] = here
            sums[p] = sums[p] + folded(missing * missing)

        def rise(t, p, here, left):
            spread = a_far[t, span, :] - a_far[t, earlier, :] + (here - left)
            pot_out[p, own, lanes(t)] = u[t, span, :] + sigmas[p] * (spread - source[t, span, :])

        from_left(pairs, per, b_new, start, CHUNK, shortfall, closing=True)
        from_left(pairs, per, b_far, start, CHUNK, rise, closing=True)
        return tuple(sums)

    primal(PAD, SLAB, above)
    primal(TOP, CHUNK, None)

    def turn(k, sums):
        primal(TOP + k * CHUNK, CHUNK, None)
        return close(k - 1, sums)

    last = rows // CHUNK - 1
    short = lax.fori_loop(1, last + 1, turn, (jnp.zeros((8, LANES), jnp.float32),) * pairs)
    short = close(last, short)
    put_sums(send, sums_to_send(pairs, short, [None] * pairs))


def call(kernel, out_shape, operands, aliases=None, scratch=(), limit=8, space=pltpu.VMEM, flops=0):
    vmem = pl.BlockSpec(memory_space=pltpu.VMEM)
    return pl.pallas_call(
        kernel,
        out_shape=out_shape,
        in_specs=[pl.BlockSpec(memory_space=space)] * len(operands),
        out_specs=[vmem] * len(out_shape),
        input_output_aliases=aliases or {},
        scratch_shapes=list(scratch),
        cost_estimate=pl.CostEstimate(flops=flops, bytes_accessed=0, transcendentals=0) if flops else None,
        compiler_params=pltpu.CompilerParams(vmem_limit_bytes=limit << 20),
    )(*operands)


def kept(*dims):
    return pltpu.VMEM(dims, jnp.float32)


def exchange(send):
    return lax.all_to_all(send, AXES, 0, 0, tiled=True)


def local(imbalance, flow, potential, cost):
    pairs, rows, cols = imbalance.shape
    per = cols // LANES
    tiles = pairs * per
    height = rows + 2 * TOP
    devices = lax.axis_size("gy") * lax.axis_size("gx")

    arrays, count = 4 * pairs + 1, 4 * tiles + per
    edge = kept(5, rows, LANES)
    inputs = [imbalance, flow, potential, cost]
    left, right, own_up, own_down = call(
        functools.partial(edge_kernel, pairs),
        [edge, edge, strips(count), strips(count)],
        [pltpu.with_memory_space_constraint(x, pltpu.MemorySpace.HBM) for x in inputs],
        scratch=[kept(arrays, SLAB, cols)] * 2 + [kept(arrays, rows, LANES)] * 2 + [pltpu.SemaphoreType.DMA((20,))],
        space=pltpu.MemorySpace.HBM,
    )
    left, right = neighbour(left, "gx", -1), neighbour(right, "gx", 1)
    up, down = call(
        functools.partial(slab_kernel, rows, count), [strips(count + 5)] * 2, [left, right, own_up, own_down]
    )
    bottom, top = neighbour(up, "gy", -1), neighbour(down, "gy", 1)

    field = kept(tiles + 1, height, LANES)
    fields = [field] * 4 + [kept(per + 1, height, LANES)]
    started = call(functools.partial(assemble_kernel, pairs), fields, inputs + [left, right], flops=40_000_000)
    u, a, b, source, price = call(
        functools.partial(adopt_kernel, pairs, rows),
        fields,
        [top, bottom, *started],
        aliases={k + 2: k for k in range(5)},
    )
    rates = jnp.full((8, LANES), initial_step, jnp.float32)
    recv = jnp.zeros((2 * devices, LANES), jnp.float32)
    for k in range(1, ITERS):
        sending = k % DEPTH == 0
        u, a, b, send, rates, *slabs = call(
            functools.partial(iterate_kernel, pairs, rows, sending),
            [field] * 3 + [kept(2 * devices, LANES), kept(8, LANES)] + [strips(3 * (tiles + 1))] * 2 * sending,
            [recv, rates, price, source, u, a, b],
            scratch=[field] * 2,
        )
        if sending:
            bottom, top = neighbour(slabs[0], "gy", -1), neighbour(slabs[1], "gy", 1)
        recv = exchange(send)
        if sending:
            u, a, b = call(
                functools.partial(merge_kernel, rows),
                [field] * 3,
                [recv, top, bottom, u, a, b],
                aliases={3: 0, 4: 1, 5: 2},
            )
    flow_out, pot_out, send = call(
        functools.partial(closing_kernel, pairs),
        [kept(2, pairs, rows, cols), kept(pairs, rows, cols), kept(2 * devices, LANES)],
        [recv, rates, price, source, u, a, b],
        scratch=[field] * 4,
        limit=12,
    )
    cells = rows * lax.axis_size("gy") * cols * lax.axis_size("gx")
    residual = jnp.sum(exchange(send), axis=0)[:: LANES // pairs] / cells
    return flow_out, pot_out, residual


def solution(mesh):
    placed = (P(None, "gy", "gx"), P(None, None, "gy", "gx"), P(None, "gy", "gx"), P("gy", "gx"))
    return jax.shard_map(
        local,
        mesh=mesh,
        in_specs=placed,
        out_specs=(P(None, None, "gy", "gx"), P(None, "gy", "gx"), P()),
        check_vma=False,
    )
```

time: 177 us -> 170 us (0.960)
  Pallas kernels: 32 us -> 27.2 us
  starting transfers between devices: 20.6 us -> 17 us
  waiting for transfers between devices: 10.2 us -> 12.3 us
    pallas_call x18 -> x17, Pallas kernels: 32 us -> 27.2 us  [call(): pl.pallas_call(kernel, out_shape=out_shape, in_specs=[pl.BlockSpec(memory...]
    ppermute x8 -> x6, starting transfers between devices: 18 us -> 14.4 us  [neighbour(): lax.ppermute(value, axis, [(source, source + steps) for source in range(l...]
    ppermute x8 -> x6, waiting for transfers between devices: 5.36 us -> 7.35 us  [neighbour(): lax.ppermute(value, axis, [(source, source + steps) for source in range(l...]
  transfers between devices with their start and end apart: 9 -> 7, of which waited for: 3 -> 4; matrix products, arithmetic and copies ran while one was open for 1% -> 1% of each run, Pallas kernels for 1% -> 0%
where the time goes in v4:
time: 170 us
  blocking collectives  109 us (64%)
  Pallas kernels  27.2 us (16%)
  starting transfers between devices  17 us (10%)
  waiting for transfers between devices  12.3 us (7%)
  local copies, waits for them, and re-layouts  2.41 us (1%)
    all_to_all x11, blocking collectives, exchange(): return lax.all_to_all(send, AXES, 0, 0, tiled=True)  109 us
    pallas_call x17, Pallas kernels, call(): pl.pallas_call(kernel, out_shape=out_shape, in_specs=[pl.BlockSpec(memory...  27.2 us
    ppermute x6, starting transfers between devices, neighbour(): lax.ppermute(value, axis, [(source, source + steps) for source in range(l...  14.4 us
    ppermute x6, waiting for transfers between devices, neighbour(): lax.ppermute(value, axis, [(source, source + steps) for source in range(l...  7.35 us
    all_to_all x1, waiting for transfers between devices, exchange(): return lax.all_to_all(send, AXES, 0, 0, tiled=True)  4.96 us
  transfers between devices with their start and end apart: 7, of which 4 were waited for; matrix products, arithmetic and copies ran while one was open for 1% of the time, Pallas kernels for 0%

profile of v4, /device:TPU:0, one launch (start us, length us, event | category | flops | bytes accessed | tf_op | source)
XLA Modules:
  0.0 169.7 jit_solution(2075633388156784088)
XLA Ops:
  0.7 2.3 %shard_map.67 = (f32[5,128,128]{2,1,0:T(8,128)S(1)}, f32[5,128,128]{2,1,0:T(8,128)S(1)}, f32[408,128]{1,0:T(8,128)S(1)}, f32[408,128]{1,0:T(8,128)S(1)}) custom-call(f32[4,128,512]{2,1,0:T(8,128)} %imb.3, f32[2,4,128,512]{3,2,1,0:T(8,128)} %flow.3, f32[4,128,512]{2,1,0:T(8,128)} %pot.3, f32[128,512]{1,0:T(8,128)} %cost.3), custom_call_target="tpu_custom_call" | custom-call | tf_op jit(solution)/shard_map/pallas_call | solution.py:369
  4.4 3.1 %collective-permute-start.1 = (f32[5,128,128]{2,1,0:T(8,128)S(1)}, f32[5,128,128]{2,1,0:T(8,128)S(1)}, u32[]{:S(2)}, u32[]{:S(2)}) collective-permute-start(f32[5,128,128]{2,1,0:T(8,128)S(1)} %get-tuple-element.83), channel_id=1, source_target_pairs={{0,1},{1,2},{2,3},{4,5},{5,6},{6,7},{8,9},{9,10},{10,11},{12,13},{... | collective-permute-start | bytes 983048 | tf_op jit(solution)/shard_map/ppermute | solution.py:27
  8.7 4.9 %collective-permute-start.2 = (f32[440,128]{1,0:T(8,128)S(1)}, f32[440,128]{1,0:T(8,128)S(1)}, u32[]{:S(2)}, u32[]{:S(2)}) collective-permute-start(f32[440,128]{1,0:T(8,128)S(1)} %get-tuple-element.86), channel_id=1, source_target_pairs={{0,4},{4,8},{8,12},{12,16},{16,20},{20,24},{24,28},{1,5},{5,9},{9,... | collective-permute-start | bytes 675848 | tf_op jit(solution)/shard_map/ppermute | solution.py:27
  17.1 4.4 %collective-permute-done.3.bottom = f32[440,128]{1,0:T(8,128)S(1)} collective-permute-done((f32[440,128]{1,0:T(8,128)S(1)}, f32[440,128]{1,0:T(8,128)S(1)}, u32[]{:S(2)}, u32[]{:S(2)}) %collective-permute-start.3) | collective-permute-done | bytes 225312 | tf_op jit(solution)/shard_map/ppermute | solution.py:27
  21.6 1.9 %shard_map.71 = (f32[17,160,128]{2,1,0:T(8,128)S(1)}, f32[17,160,128]{2,1,0:T(8,128)S(1)}, f32[17,160,128]{2,1,0:T(8,128)S(1)}, f32[64,128]{1,0:T(8,128)S(1)}, f32[8,128]{1,0:T(8,128)S(1)}) custom-call(f32[64,128]{1,0:T(8,128)S(1)} %broadcast_in_dim.6.recv, f32[8,128]{1,0:T(8,128)S(1)} %broadcast_in_dim.7.rates, f32[5,160,128]{2,1,0:T(8,128)S(1)} %get-tuple-element.93.price, ...), custom_call_target="tpu_custom_call" | custom-call | tf_op jit(solution)/shard_map/pallas_call | solution.py:369
  23.5 17.6 %all_to_all.130 = f32[32,2,128]{2,1,0:T(2,128)S(1)} all-to-all(f32[32,2,128]{2,1,0:T(2,128)S(1)} %bitcast.36), channel_id=1, replica_groups=mesh['gy'=8,'gx'=4] {'gy','gx'}, dimensions={0} | all-to-all | bytes 65536 | tf_op jit(solution)/shard_map/all_to_all | solution.py:386
  43.1 9.0 %all_to_all.131 = f32[32,2,128]{2,1,0:T(2,128)S(1)} all-to-all(f32[32,2,128]{2,1,0:T(2,128)S(1)} %bitcast.37), channel_id=1, replica_groups=mesh['gy'=8,'gx'=4] {'gy','gx'}, dimensions={0} | all-to-all | bytes 65536 | tf_op jit(solution)/shard_map/all_to_all | solution.py:386
  54.0 9.0 %all_to_all.132 = f32[32,2,128]{2,1,0:T(2,128)S(1)} all-to-all(f32[32,2,128]{2,1,0:T(2,128)S(1)} %bitcast.38), channel_id=1, replica_groups=mesh['gy'=8,'gx'=4] {'gy','gx'}, dimensions={0} | all-to-all | bytes 65536 | tf_op jit(solution)/shard_map/all_to_all | solution.py:386
  64.9 9.0 %all_to_all.133 = f32[32,2,128]{2,1,0:T(2,128)S(1)} all-to-all(f32[32,2,128]{2,1,0:T(2,128)S(1)} %bitcast.39), channel_id=1, replica_groups=mesh['gy'=8,'gx'=4] {'gy','gx'}, dimensions={0} | all-to-all | bytes 65536 | tf_op jit(solution)/shard_map/all_to_all | solution.py:386
  75.7 9.0 %all_to_all.134 = f32[32,2,128]{2,1,0:T(2,128)S(1)} all-to-all(f32[32,2,128]{2,1,0:T(2,128)S(1)} %bitcast.40), channel_id=1, replica_groups=mesh['gy'=8,'gx'=4] {'gy','gx'}, dimensions={0} | all-to-all | bytes 65536 | tf_op jit(solution)/shard_map/all_to_all | solution.py:386
  84.7 2.1 %shard_map.76 = (f32[17,160,128]{2,1,0:T(8,128)S(1)}, f32[17,160,128]{2,1,0:T(8,128)S(1)}, f32[17,160,128]{2,1,0:T(8,128)S(1)}, f32[64,128]{1,0:T(8,128)S(1)}, f...) custom-call(f32[64,128]{1,0:T(8,128)S(1)} %bitcast.25, ...), custom_call_target="tpu_custom_call" | custom-call | tf_op jit(solution)/shard_map/pallas_call | solution.py:369
  86.8 2.5 %collective-permute-start.4 = (f32[312,128]{1,0:T(8,128)S(1)}, f32[312,128]{1,0:T(8,128)S(1)}, u32[]{:S(2)}, u32[]{:S(2)}) collective-permute-start(f32[312,128]{1,0:T(8,128)S(1)} %get-tuple-element.125), channel_id=1, source_target_pairs={{0,4},{4,8},{8,12},{12,16},{16,20},{20,24},{24,28},{1,5},{5,9},{9,... | collective-permute-start | bytes 479240 | tf_op jit(solution)/shard_map/ppermute | solution.py:27
  90.6 11.0 %all_to_all.135 = f32[32,2,128]{2,1,0:T(2,128)S(1)} all-to-all(f32[32,2,128]{2,1,0:T(2,128)S(1)} %bitcast.35), channel_id=1, replica_groups=mesh['gy'=8,'gx'=4] {'gy','gx'}, dimensions={0} | all-to-all | bytes 65536 | tf_op jit(solution)/shard_map/all_to_all | solution.py:386
  101.7 1.9 %shard_map.78 = (f32[17,160,128]{2,1,0:T(8,128)S(1)}, f32[17,160,128]{2,1,0:T(8,128)S(1)}, f32[17,160,128]{2,1,0:T(8,128)S(1)}, f32[64,128]{1,0:T(8,128)S(1)}, f32[8,128]{1,0:T(8,128)S(1)}) custom-call(f32[64,128]{1,0:T(8,128)S(1)} %bitcast.24, f32[8,128]{1,0:T(8,128)S(1)} %get-tuple-element.124.rates, f32[5,160,128]{2,1,0:T(8,128)S(1)} %get-tuple-element.93.price, ...), custom_call_target="tpu_custom_call" | custom-call | tf_op jit(solution)/shard_map/pallas_call | solution.py:369
  103.6 9.0 %all_to_all.136 = f32[32,2,128]{2,1,0:T(2,128)S(1)} all-to-all(f32[32,2,128]{2,1,0:T(2,128)S(1)} %bitcast.41), channel_id=1, replica_groups=mesh['gy'=8,'gx'=4] {'gy','gx'}, dimensions={0} | all-to-all | bytes 65536 | tf_op jit(solution)/shard_map/all_to_all | solution.py:386
  112.6 1.9 %shard_map.79 = (f32[17,160,128]{2,1,0:T(8,128)S(1)}, f32[17,160,128]{2,1,0:T(8,128)S(1)}, f32[17,160,128]{2,1,0:T(8,128)S(1)}, f32[64,128]{1,0:T(8,128)S(1)}, f32[8,128]{1,0:T(8,128)S(1)}) custom-call(f32[64,128]{1,0:T(8,128)S(1)} %bitcast.30, f32[8,128]{1,0:T(8,128)S(1)} %get-tuple-element.134.rates, f32[5,160,128]{2,1,0:T(8,128)S(1)} %get-tuple-element.93.price, ...), custom_call_target="tpu_custom_call" | custom-call | tf_op jit(solution)/shard_map/pallas_call | solution.py:369
  114.5 9.1 %all_to_all.137 = f32[32,2,128]{2,1,0:T(2,128)S(1)} all-to-all(f32[32,2,128]{2,1,0:T(2,128)S(1)} %bitcast.42), channel_id=1, replica_groups=mesh['gy'=8,'gx'=4] {'gy','gx'}, dimensions={0} | all-to-all | bytes 65536 | tf_op jit(solution)/shard_map/all_to_all | solution.py:386
  125.6 9.0 %all_to_all.138 = f32[32,2,128]{2,1,0:T(2,128)S(1)} all-to-all(f32[32,2,128]{2,1,0:T(2,128)S(1)} %bitcast.43), channel_id=1, replica_groups=mesh['gy'=8,'gx'=4] {'gy','gx'}, dimensions={0} | all-to-all | bytes 65536 | tf_op jit(solution)/shard_map/all_to_all | solution.py:386
  134.5 1.9 %shard_map.81 = (f32[17,160,128]{2,1,0:T(8,128)S(1)}, f32[17,160,128]{2,1,0:T(8,128)S(1)}, f32[17,160,128]{2,1,0:T(8,128)S(1)}, f32[64,128]{1,0:T(8,128)S(1)}, f32[8,128]{1,0:T(8,128)S(1)}) custom-call(f32[64,128]{1,0:T(8,128)S(1)} %bitcast.32, f32[8,128]{1,0:T(8,128)S(1)} %get-tuple-element.144.rates, f32[5,160,128]{2,1,0:T(8,128)S(1)} %get-tuple-element.93.price, ...), custom_call_target="tpu_custom_call" | custom-call | tf_op jit(solution)/shard_map/pallas_call | solution.py:369
  136.5 9.0 %all_to_all.139 = f32[32,2,128]{2,1,0:T(2,128)S(1)} all-to-all(f32[32,2,128]{2,1,0:T(2,128)S(1)} %bitcast.44), channel_id=1, replica_groups=mesh['gy'=8,'gx'=4] {'gy','gx'}, dimensions={0} | all-to-all | bytes 65536 | tf_op jit(solution)/shard_map/all_to_all | solution.py:386
  147.4 9.0 %all_to_all.140 = f32[32,2,128]{2,1,0:T(2,128)S(1)} all-to-all(f32[32,2,128]{2,1,0:T(2,128)S(1)} %bitcast.45), channel_id=1, replica_groups=mesh['gy'=8,'gx'=4] {'gy','gx'}, dimensions={0} | all-to-all | bytes 65536 | tf_op jit(solution)/shard_map/all_to_all | solution.py:386
  156.3 2.9 %shard_map.83 = (f32[2,4,128,512]{3,2,1,0:T(8,128)S(1)}, f32[4,128,512]{2,1,0:T(8,128)S(1)}, f32[64,128]{1,0:T(8,128)}) custom-call(f32[64,128]{1,0:T(8,128)S(1)} %bitcast.34, f32[8,128]{1,0:T(8,128)S(1)} %get-tuple-element.154.rates, f32[5,160,128]{2,1,0:T(8,128)S(1)} %get-tuple-element.93.price, f32[17,160,128]{2,1,0:T(8,128)S(1)} %get-tuple-element.94.source, ...), custom_call_target="tpu_custom_call" | custom-call | tf_op jit(solution)/shard_map/pallas_call | solution.py:369
  159.2 2.5 %all-to-all-start.11 = ((f32[32,2,128]{2,1,0:T(2,128)}), f32[32,2,128]{2,1,0:T(2,128)S(1)}, u32[]{:S(2)}, u32[]{:S(2)}) async-start(f32[32,2,128]{2,1,0:T(2,128)} %bitcast.22), calls=%async_computation.11 | async-start | bytes 65536 | tf_op jit(solution)/shard_map/all_to_all | solution.py:386
  164.0 5.0 %all-to-all-done.11 = f32[32,2,128]{2,1,0:T(2,128)S(1)} async-done(((f32[32,2,128]{2,1,0:T(2,128)}), f32[32,2,128]{2,1,0:T(2,128)S(1)}, u32[]{:S(2)}, u32[]{:S(2)}) %all-to-all-start.11) | async-done | bytes 32800 | tf_op jit(solution)/shard_map/all_to_all | solution.py:386
  (33 shorter events, 22.1 us)
Async XLA Ops:
  0.6 14.3 %copy-start = (f32[2,4,128,512]{3,2,1,0:T(8,128)S(1)}, f32[2,4,128,512]{3,2,1,0:T(8,128)}, u32[]{:S(2)}) copy-start(f32[2,4,128,512]{3,2,1,0:T(8,128)} %flow.3) | copy-start | bytes 6291460
  0.6 14.3 %copy-start.2 = (f32[4,128,512]{2,1,0:T(8,128)S(1)}, f32[4,128,512]{2,1,0:T(8,128)}, u32[]{:S(2)}) copy-start(f32[4,128,512]{2,1,0:T(8,128)} %pot.3) | copy-start | bytes 3145732
  0.7 14.3 %copy-start.3 = (f32[128,512]{1,0:T(8,128)S(1)}, f32[128,512]{1,0:T(8,128)}, u32[]{:S(2)}) copy-start(f32[128,512]{1,0:T(8,128)} %cost.3) | copy-start | bytes 786436
  2.9 12.0 %copy-start.1 = (f32[4,128,512]{2,1,0:T(8,128)S(1)}, f32[4,128,512]{2,1,0:T(8,128)}, u32[]{:S(2)}) copy-start(f32[4,128,512]{2,1,0:T(8,128)} %imb.3) | copy-start | bytes 3145732
  3.0 4.5 %collective-permute-start = (f32[5,128,128]{2,1,0:T(8,128)S(1)}, f32[5,128,128]{2,1,0:T(8,128)S(1)}, u32[]{:S(2)}, u32[]{:S(2)}) collective-permute-start(f32[5,128,128]{2,1,0:T(8,128)S(1)} %get-tuple-element.82), channel_id=1, source_target_pairs={{1,0},{2,1},{3,2},{5,4},{6,5},{7,6},{9,8},{10,9},{11,10},{13,12},{... | collective-permute-start | bytes 983048 | tf_op jit(solution)/shard_map/ppermute | solution.py:27
  4.4 4.3 %collective-permute-start.1 = (f32[5,128,128]{2,1,0:T(8,128)S(1)}, f32[5,128,128]{2,1,0:T(8,128)S(1)}, u32[]{:S(2)}, u32[]{:S(2)}) collective-permute-start(f32[5,128,128]{2,1,0:T(8,128)S(1)} %get-tuple-element.83), channel_id=1, source_target_pairs={{0,1},{1,2},{2,3},{4,5},{5,6},{6,7},{8,9},{9,10},{10,11},{12,13},{... | collective-permute-start | bytes 983048 | tf_op jit(solution)/shard_map/ppermute | solution.py:27
  8.7 8.4 %collective-permute-start.2 = (f32[440,128]{1,0:T(8,128)S(1)}, f32[440,128]{1,0:T(8,128)S(1)}, u32[]{:S(2)}, u32[]{:S(2)}) collective-permute-start(f32[440,128]{1,0:T(8,128)S(1)} %get-tuple-element.86), channel_id=1, source_target_pairs={{0,4},{4,8},{8,12},{12,16},{16,20},{20,24},{24,28},{1,5},{5,9},{9,... | collective-permute-start | bytes 675848 | tf_op jit(solution)/shard_map/ppermute | solution.py:27
  13.6 7.9 %collective-permute-start.3 = (f32[440,128]{1,0:T(8,128)S(1)}, f32[440,128]{1,0:T(8,128)S(1)}, u32[]{:S(2)}, u32[]{:S(2)}) collective-permute-start(f32[440,128]{1,0:T(8,128)S(1)} %get-tuple-element.87), channel_id=1, source_target_pairs={{4,0},{8,4},{12,8},{16,12},{20,16},{24,20},{28,24},{5,1},{9,5},{13... | collective-permute-start | bytes 675848 | tf_op jit(solution)/shard_map/ppermute | solution.py:27
  86.8 14.8 %collective-permute-start.4 = (f32[312,128]{1,0:T(8,128)S(1)}, f32[312,128]{1,0:T(8,128)S(1)}, u32[]{:S(2)}, u32[]{:S(2)}) collective-permute-start(f32[312,128]{1,0:T(8,128)S(1)} %get-tuple-element.125), channel_id=1, source_target_pairs={{0,4},{4,8},{8,12},{12,16},{16,20},{20,24},{24,28},{1,5},{5,9},{9,... | collective-permute-start | bytes 479240 | tf_op jit(solution)/shard_map/ppermute | solution.py:27
  89.3 12.3 %collective-permute-start.5 = (f32[312,128]{1,0:T(8,128)S(1)}, f32[312,128]{1,0:T(8,128)S(1)}, u32[]{:S(2)}, u32[]{:S(2)}) collective-permute-start(f32[312,128]{1,0:T(8,128)S(1)} %get-tuple-element.126), channel_id=1, source_target_pairs={{4,0},{8,4},{12,8},{16,12},{20,16},{24,20},{28,24},{5,1},{9,5},{13... | collective-permute-start | bytes 479240 | tf_op jit(solution)/shard_map/ppermute | solution.py:27
  159.2 9.8 %all-to-all-start.11 = ((f32[32,2,128]{2,1,0:T(2,128)}), f32[32,2,128]{2,1,0:T(2,128)S(1)}, u32[]{:S(2)}, u32[]{:S(2)}) async-start(f32[32,2,128]{2,1,0:T(2,128)} %bitcast.22), calls=%async_computation.11 | async-start | bytes 65536 | tf_op jit(solution)/shard_map/all_to_all | solution.py:386

commit v5 on v4

--- a/solution.py
+++ b/solution.py
@@ -17,6 +17,7 @@
 PAD = 8
 TOP = PAD + SLAB
 LANES = 128
+CLOSING_CHUNK = 64
 CHUNK = 32
 AXES = ("gy", "gx")
 
@@ -32,9 +33,9 @@
     return pltpu.roll(value, shift, 1) if shift else value
 
 
-def edge_kernel(pairs, imb, flow, pot, cost, left, right, up, down, top, bottom, first, last, sems):
+def edge_columns_kernel(pairs, imb, flow, pot, cost, left, right, first, last, sems):
     rows, cols = cost.shape
-    per, group = cols // LANES, LANES // pairs
+    group = LANES // pairs
     fields = [pot, flow.at[0], flow.at[1], imb]
     copies = []
 
@@ -46,12 +47,6 @@
         fetch(field.at[:, :, cols - LANES : cols], last.at[pl.ds(k * pairs, pairs)])
     fetch(cost.at[:, 0:LANES], first.at[4 * pairs])
     fetch(cost.at[:, cols - LANES : cols], last.at[4 * pairs])
-    sides = len(copies)
-    for k, field in enumerate(fields):
-        fetch(field.at[:, 0:SLAB, :], top.at[pl.ds(k * pairs, pairs)])
-        fetch(field.at[:, rows - SLAB : rows, :], bottom.at[pl.ds(k * pairs, pairs)])
-    fetch(cost.at[0:SLAB, :], top.at[4 * pairs])
-    fetch(cost.at[rows - SLAB : rows, :], bottom.at[4 * pairs])
     for copy in copies:
         copy.start()
     count = 32
@@ -70,7 +65,24 @@
                 tail = jnp.where((which == p) & (inner >= group - SIDE), rolled(last[n, span, :], group * (p + 1)), tail)
             left[k, span, :] = head
             right[k, span, :] = tail
-    for copy in copies[sides:]:
+
+
+def edge_rows_kernel(pairs, imb, flow, pot, cost, up, down, top, bottom, sems):
+    rows, cols = cost.shape
+    per = cols // LANES
+    copies = []
+
+    def fetch(source, target):
+        copies.append(pltpu.make_async_copy(source, target, sems.at[len(copies)]))
+
+    for k, field in enumerate([pot, flow.at[0], flow.at[1], imb]):
+        fetch(field.at[:, 0:SLAB, :], top.at[pl.ds(k * pairs, pairs)])
+        fetch(field.at[:, rows - SLAB : rows, :], bottom.at[pl.ds(k * pairs, pairs)])
+    fetch(cost.at[0:SLAB, :], top.at[4 * pairs])
+    fetch(cost.at[rows - SLAB : rows, :], bottom.at[4 * pairs])
+    for copy in copies:
+        copy.start()
+    for copy in copies:
         copy.wait()
     for n in range(4 * pairs + 1):
         for c in range(per):
@@ -128,7 +140,7 @@
     price[per, TOP:end, :] = jnp.where(sides > 0.0, left[4] + right[4], 1.0)
 
 
-def adopt_kernel(pairs, rows, top, bottom, u, a, b, source, price, u_out, a_out, b_out, source_out, price_out):
+def adopt_kernel(pairs, rows, early_sums, top, bottom, u, a, b, source, price, u_out, a_out, b_out, source_out, price_out):
     per = price.shape[0] - 1
     tiles = pairs * per
     end, count = TOP + rows, 4 * tiles + per
@@ -307,6 +319,62 @@
                 down[strip(k * (tiles + 1) + t), :] = out[t, end - DEPTH : end, :]
 
 
+def largest_chunk(rows):
+    return max(size for size in range(8, 65, 8) if rows % size == 0)
+
+
+def early_kernel(pairs, rows, price, source, u, a, b, u_out, a_out, b_out, a_far, b_far, sums_out):
+    per = price.shape[0] - 1
+    tiles, end = pairs * per, TOP + rows
+    rates, side = [initial_step] * pairs, jnp.full((1, LANES), initial_step, jnp.float32)
+    sides = own_masks(pairs)[2]
+    a_far[:, 0:PAD, :] = jnp.zeros((tiles + 1, PAD, LANES), jnp.float32)
+    u_out[:, end + SLAB : end + TOP, :] = jnp.zeros((tiles + 1, PAD, LANES), jnp.float32)
+    zeros = (jnp.zeros((8, LANES), jnp.float32),) * pairs
+    size = largest_chunk(rows - 8)
+
+    def primal_turn(k, sums):
+        start = TOP + k * size
+        out = (a_out, b_out, a_far, b_far)
+        return tuple(primal_rows(pairs, per, start, size, rates, side, None, sides, price, u, a, b, *out, sums))
+
+    primals = lax.fori_loop(0, (rows - 8) // size, primal_turn, zeros)
+    step = largest_chunk(rows - 16)
+
+    def dual_turn(k, sums):
+        start = TOP + 8 + k * step
+        return tuple(dual_rows(pairs, per, start, step, rates, side * sides, source, a_far, b_far, u, u_out, sums))
+
+    duals = lax.fori_loop(0, (rows - 16) // step, dual_turn, zeros)
+    for p in range(pairs):
+        sums_out[p] = primals[p]
+        sums_out[pairs + p] = duals[p]
+
+
+def late_kernel(pairs, rows, price, source, u, a, b, sums, *refs):
+    u_out, a_out, b_out, a_far, b_far, send = refs[5:]
+    per, end = price.shape[0] - 1, TOP + rows
+    rates, side = [initial_step] * pairs, jnp.full((1, LANES), initial_step, jnp.float32)
+    above, below, sides = own_masks(pairs)
+
+    def primal(start, mask, sums):
+        out = (a_out, b_out, a_far, b_far)
+        return primal_rows(pairs, per, start, 8, rates, side, mask, sides, price, u, a, b, *out, sums)
+
+    def dual(start, mask, sums):
+        now, side_now = (rates, side * sides) if mask is None else ([mask * r for r in rates], side * sides * mask)
+        return dual_rows(pairs, per, start, 8, now, side_now, source, a_far, b_far, u, u_out, sums)
+
+    primal(PAD, above, ())
+    primals = primal(end - 8, None, [sums[p] for p in range(pairs)])
+    primal(end, below, ())
+    duals = dual(TOP, None, [sums[pairs + p] for p in range(pairs)])
+    duals = dual(end - 8, None, duals)
+    dual(PAD, above, ())
+    dual(end, below, ())
+    put_sums(send, sums_to_send(pairs, primals, duals))
+
+
 def merge_kernel(rows, recv, top, bottom, u, a, b, u_out, a_out, b_out):
     tiles = u.shape[0]
     for k, out in enumerate((u_out, a_out, b_out)):
@@ -330,8 +398,8 @@
 
     def close(k, sums):
         sums = list(sums)
-        start = TOP + k * CHUNK
-        span, earlier, own = pl.ds(start, CHUNK), pl.ds(start - 1, CHUNK), pl.ds(k * CHUNK, CHUNK)
+        start = TOP + k * CLOSING_CHUNK
+        span, earlier, own = pl.ds(start, CLOSING_CHUNK), pl.ds(start - 1, CLOSING_CHUNK), pl.ds(k * CLOSING_CHUNK, CLOSING_CHUNK)
 
         def lanes(t):
             return slice(t % per * LANES, (t % per + 1) * LANES)
@@ -347,18 +415,18 @@
             spread = a_far[t, span, :] - a_far[t, earlier, :] + (here - left)
             pot_out[p, own, lanes(t)] = u[t, span, :] + sigmas[p] * (spread - source[t, span, :])
 
-        from_left(pairs, per, b_new, start, CHUNK, shortfall, closing=True)
-        from_left(pairs, per, b_far, start, CHUNK, rise, closing=True)
+        from_left(pairs, per, b_new, start, CLOSING_CHUNK, shortfall, closing=True)
+        from_left(pairs, per, b_far, start, CLOSING_CHUNK, rise, closing=True)
         return tuple(sums)
 
     primal(PAD, SLAB, above)
-    primal(TOP, CHUNK, None)
+    primal(TOP, CLOSING_CHUNK, None)
 
     def turn(k, sums):
-        primal(TOP + k * CHUNK, CHUNK, None)
+        primal(TOP + k * CLOSING_CHUNK, CLOSING_CHUNK, None)
         return close(k - 1, sums)
 
-    last = rows // CHUNK - 1
+    last = rows // CLOSING_CHUNK - 1
     short = lax.fori_loop(1, last + 1, turn, (jnp.zeros((8, LANES), jnp.float32),) * pairs)
     short = close(last, short)
     put_sums(send, sums_to_send(pairs, short, [None] * pairs))
@@ -396,12 +464,22 @@
     arrays, count = 4 * pairs + 1, 4 * tiles + per
     edge = kept(5, rows, LANES)
     inputs = [imbalance, flow, potential, cost]
-    left, right, own_up, own_down = call(
-        functools.partial(edge_kernel, pairs),
-        [edge, edge, strips(count), strips(count)],
-        [pltpu.with_memory_space_constraint(x, pltpu.MemorySpace.HBM) for x in inputs],
-        scratch=[kept(arrays, SLAB, cols)] * 2 + [kept(arrays, rows, LANES)] * 2 + [pltpu.SemaphoreType.DMA((20,))],
+    held = [pltpu.with_memory_space_constraint(x, pltpu.MemorySpace.HBM) for x in inputs]
+    sems = pltpu.SemaphoreType.DMA((10,))
+    left, right = call(
+        functools.partial(edge_columns_kernel, pairs),
+        [edge, edge],
+        held,
+        scratch=[kept(arrays, rows, LANES)] * 2 + [sems],
         space=pltpu.MemorySpace.HBM,
+    )
+    own_up, own_down = call(
+        functools.partial(edge_rows_kernel, pairs),
+        [strips(count), strips(count)],
+        held,
+        scratch=[kept(arrays, SLAB, cols)] * 2 + [sems],
+        space=pltpu.MemorySpace.HBM,
+        flops=20_000_000,
     )
     left, right = neighbour(left, "gx", -1), neighbour(right, "gx", 1)
     up, down = call(
@@ -412,15 +490,28 @@
     field = kept(tiles + 1, height, LANES)
     fields = [field] * 4 + [kept(per + 1, height, LANES)]
     started = call(functools.partial(assemble_kernel, pairs), fields, inputs + [left, right], flops=40_000_000)
+    u, a, b, source, price = started
+    *early, early_sums = call(
+        functools.partial(early_kernel, pairs, rows),
+        [field] * 5 + [kept(2 * pairs, 8, LANES)],
+        [price, source, u, a, b],
+        flops=100_000_000,
+    )
     u, a, b, source, price = call(
         functools.partial(adopt_kernel, pairs, rows),
         fields,
-        [top, bottom, *started],
-        aliases={k + 2: k for k in range(5)},
-    )
+        [early_sums, top, bottom, *started],
+        aliases={k + 3: k for k in range(5)},
+    )
+    u, a, b, _, _, send = call(
+        functools.partial(late_kernel, pairs, rows),
+        [field] * 5 + [kept(2 * devices, LANES)],
+        [price, source, u, a, b, early_sums, *early],
+        aliases={k + 6: k for k in range(5)},
+    )
+    recv = exchange(send)
     rates = jnp.full((8, LANES), initial_step, jnp.float32)
-    recv = jnp.zeros((2 * devices, LANES), jnp.float32)
-    for k in range(1, ITERS):
+    for k in range(2, ITERS):
         sending = k % DEPTH == 0
         u, a, b, send, rates, *slabs = call(
             functools.partial(iterate_kernel, pairs, rows, sending),

time: 170 us -> 168 us (0.988)
  waiting for transfers between devices: 12.3 us -> 9.37 us
    ppermute x6, waiting for transfers between devices: 7.35 us -> 4.41 us  [neighbour(): lax.ppermute(value, axis, [(source, source + steps) for source in range(l...]
    pallas_call x17 -> x19, Pallas kernels: 27.2 us -> 28.4 us  [call(): pl.pallas_call(kernel, out_shape=out_shape, in_specs=[pl.BlockSpec(memory...]
  transfers between devices with their start and end apart: 7 -> 7, of which waited for: 4 -> 2; matrix products, arithmetic and copies ran while one was open for 1% -> 1% of each run, Pallas kernels for 0% -> 2%
where the time goes in v5:
time: 168 us
  blocking collectives  109 us (65%)
  Pallas kernels  28.4 us (17%)
  starting transfers between devices  17.1 us (10%)
  waiting for transfers between devices  9.37 us (6%)
  local copies, waits for them, and re-layouts  2.41 us (1%)
    all_to_all x11, blocking collectives, exchange(): return lax.all_to_all(send, AXES, 0, 0, tiled=True)  109 us
    pallas_call x19, Pallas kernels, call(): pl.pallas_call(kernel, out_shape=out_shape, in_specs=[pl.BlockSpec(memory...  28.4 us
    ppermute x6, starting transfers between devices, neighbour(): lax.ppermute(value, axis, [(source, source + steps) for source in range(l...  14.6 us
    all_to_all x1, waiting for transfers between devices, exchange(): return lax.all_to_all(send, AXES, 0, 0, tiled=True)  4.96 us
    ppermute x6, waiting for transfers between devices, neighbour(): lax.ppermute(value, axis, [(source, source + steps) for source in range(l...  4.41 us
  transfers between devices with their start and end apart: 7, of which 2 were waited for; matrix products, arithmetic and copies ran while one was open for 1% of the time, Pallas kernels for 2%

profile of v5, /device:TPU:0, one launch (start us, length us, event | category | flops | bytes accessed | tf_op | source)
XLA Modules:
  0.0 167.6 jit_solution(1312848336877376856)
XLA Ops:
  0.6 2.0 %shard_map.67 = (f32[5,128,128]{2,1,0:T(8,128)S(1)}, f32[5,128,128]{2,1,0:T(8,128)S(1)}) custom-call(f32[4,128,512]{2,1,0:T(8,128)} %imb.5, f32[2,4,128,512]{3,2,1,0:T(8,128)} %flow.5, f32[4,128,512]{2,1,0:T(8,128)} %pot.5, f32[128,512]{1,0:T(8,128)} %cost.5), custom_call_target="tpu_custom_call" | custom-call | tf_op jit(solution)/shard_map/pallas_call | solution.py:437
  4.0 3.2 %collective-permute-start.1 = (f32[5,128,128]{2,1,0:T(8,128)S(1)}, f32[5,128,128]{2,1,0:T(8,128)S(1)}, u32[]{:S(2)}, u32[]{:S(2)}) collective-permute-start(f32[5,128,128]{2,1,0:T(8,128)S(1)} %get-tuple-element.88), channel_id=1, source_target_pairs={{0,1},{1,2},{2,3},{4,5},{5,6},{6,7},{8,9},{9,10},{10,11},{12,13},{... | collective-permute-start | bytes 983048 | tf_op jit(solution)/shard_map/ppermute | solution.py:28
  8.6 5.0 %collective-permute-start.2 = (f32[440,128]{1,0:T(8,128)S(1)}, f32[440,128]{1,0:T(8,128)S(1)}, u32[]{:S(2)}, u32[]{:S(2)}) collective-permute-start(f32[440,128]{1,0:T(8,128)S(1)} %get-tuple-element.97), channel_id=1, source_target_pairs={{0,4},{4,8},{8,12},{12,16},{16,20},{20,24},{24,28},{1,5},{5,9},{9,... | collective-permute-start | bytes 675848 | tf_op jit(solution)/shard_map/ppermute | solution.py:28
  17.2 4.4 %collective-permute-done.3.bottom = f32[440,128]{1,0:T(8,128)S(1)} collective-permute-done((f32[440,128]{1,0:T(8,128)S(1)}, f32[440,128]{1,0:T(8,128)S(1)}, u32[]{:S(2)}, u32[]{:S(2)}) %collective-permute-start.3) | collective-permute-done | bytes 225312 | tf_op jit(solution)/shard_map/ppermute | solution.py:28
  22.1 17.1 %all_to_all.130 = f32[32,2,128]{2,1,0:T(2,128)S(1)} all-to-all(f32[32,2,128]{2,1,0:T(2,128)S(1)} %bitcast.36), channel_id=1, replica_groups=mesh['gy'=8,'gx'=4] {'gy','gx'}, dimensions={0} | all-to-all | bytes 65536 | tf_op jit(solution)/shard_map/all_to_all | solution.py:454
  39.3 1.9 %shard_map.74 = (f32[17,160,128]{2,1,0:T(8,128)S(1)}, f32[17,160,128]{2,1,0:T(8,128)S(1)}, f32[17,160,128]{2,1,0:T(8,128)S(1)}, f32[64,128]{1,0:T(8,128)S(1)}, f32[8,128]{1,0:T(8,128)S(1)}) custom-call(f32[64,128]{1,0:T(8,128)S(1)} %bitcast.26, f32[8,128]{1,0:T(8,128)S(1)} %broadcast_in_dim.3.rates, f32[5,160,128]{2,1,0:T(8,128)S(1)} %get-tuple-element.99.price, ...), custom_call_target="tpu_custom_call" | custom-call | tf_op jit(solution)/shard_map/pallas_call | solution.py:437
  41.2 9.0 %all_to_all.131 = f32[32,2,128]{2,1,0:T(2,128)S(1)} all-to-all(f32[32,2,128]{2,1,0:T(2,128)S(1)} %bitcast.37), channel_id=1, replica_groups=mesh['gy'=8,'gx'=4] {'gy','gx'}, dimensions={0} | all-to-all | bytes 65536 | tf_op jit(solution)/shard_map/all_to_all | solution.py:454
  50.2 2.0 %shard_map.75 = (f32[17,160,128]{2,1,0:T(8,128)S(1)}, f32[17,160,128]{2,1,0:T(8,128)S(1)}, f32[17,160,128]{2,1,0:T(8,128)S(1)}, f32[64,128]{1,0:T(8,128)S(1)}, f32[8,128]{1,0:T(8,128)S(1)}) custom-call(f32[64,128]{1,0:T(8,128)S(1)} %bitcast.27, f32[8,128]{1,0:T(8,128)S(1)} %get-tuple-element.114.rates, f32[5,160,128]{2,1,0:T(8,128)S(1)} %get-tuple-element.99.price, ...), custom_call_target="tpu_custom_call" | custom-call | tf_op jit(solution)/shard_map/pallas_call | solution.py:437
  52.2 9.0 %all_to_all.132 = f32[32,2,128]{2,1,0:T(2,128)S(1)} all-to-all(f32[32,2,128]{2,1,0:T(2,128)S(1)} %bitcast.38), channel_id=1, replica_groups=mesh['gy'=8,'gx'=4] {'gy','gx'}, dimensions={0} | all-to-all | bytes 65536 | tf_op jit(solution)/shard_map/all_to_all | solution.py:454
  63.1 9.0 %all_to_all.133 = f32[32,2,128]{2,1,0:T(2,128)S(1)} all-to-all(f32[32,2,128]{2,1,0:T(2,128)S(1)} %bitcast.39), channel_id=1, replica_groups=mesh['gy'=8,'gx'=4] {'gy','gx'}, dimensions={0} | all-to-all | bytes 65536 | tf_op jit(solution)/shard_map/all_to_all | solution.py:454
  74.0 9.0 %all_to_all.134 = f32[32,2,128]{2,1,0:T(2,128)S(1)} all-to-all(f32[32,2,128]{2,1,0:T(2,128)S(1)} %bitcast.40), channel_id=1, replica_groups=mesh['gy'=8,'gx'=4] {'gy','gx'}, dimensions={0} | all-to-all | bytes 65536 | tf_op jit(solution)/shard_map/all_to_all | solution.py:454
  83.0 2.1 %shard_map.78 = (f32[17,160,128]{2,1,0:T(8,128)S(1)}, f32[17,160,128]{2,1,0:T(8,128)S(1)}, f32[17,160,128]{2,1,0:T(8,128)S(1)}, f32[64,128]{1,0:T(8,128)S(1)}, f...) custom-call(f32[64,128]{1,0:T(8,128)S(1)} %bitcast.25, ...), custom_call_target="tpu_custom_call" | custom-call | tf_op jit(solution)/shard_map/pallas_call | solution.py:437
  85.1 2.5 %collective-permute-start.4 = (f32[312,128]{1,0:T(8,128)S(1)}, f32[312,128]{1,0:T(8,128)S(1)}, u32[]{:S(2)}, u32[]{:S(2)}) collective-permute-start(f32[312,128]{1,0:T(8,128)S(1)} %get-tuple-element.135), channel_id=1, source_target_pairs={{0,4},{4,8},{8,12},{12,16},{16,20},{20,24},{24,28},{1,5},{5,9},{9,... | collective-permute-start | bytes 479240 | tf_op jit(solution)/shard_map/ppermute | solution.py:28
  88.9 11.0 %all_to_all.135 = f32[32,2,128]{2,1,0:T(2,128)S(1)} all-to-all(f32[32,2,128]{2,1,0:T(2,128)S(1)} %bitcast.35), channel_id=1, replica_groups=mesh['gy'=8,'gx'=4] {'gy','gx'}, dimensions={0} | all-to-all | bytes 65536 | tf_op jit(solution)/shard_map/all_to_all | solution.py:454
  101.9 9.0 %all_to_all.136 = f32[32,2,128]{2,1,0:T(2,128)S(1)} all-to-all(f32[32,2,128]{2,1,0:T(2,128)S(1)} %bitcast.41), channel_id=1, replica_groups=mesh['gy'=8,'gx'=4] {'gy','gx'}, dimensions={0} | all-to-all | bytes 65536 | tf_op jit(solution)/shard_map/all_to_all | solution.py:454
  112.8 9.1 %all_to_all.137 = f32[32,2,128]{2,1,0:T(2,128)S(1)} all-to-all(f32[32,2,128]{2,1,0:T(2,128)S(1)} %bitcast.42), channel_id=1, replica_groups=mesh['gy'=8,'gx'=4] {'gy','gx'}, dimensions={0} | all-to-all | bytes 65536 | tf_op jit(solution)/shard_map/all_to_all | solution.py:454
  121.9 2.0 %shard_map.82 = (f32[17,160,128]{2,1,0:T(8,128)S(1)}, f32[17,160,128]{2,1,0:T(8,128)S(1)}, f32[17,160,128]{2,1,0:T(8,128)S(1)}, f32[64,128]{1,0:T(8,128)S(1)}, f32[8,128]{1,0:T(8,128)S(1)}) custom-call(f32[64,128]{1,0:T(8,128)S(1)} %bitcast.31, f32[8,128]{1,0:T(8,128)S(1)} %get-tuple-element.149.rates, f32[5,160,128]{2,1,0:T(8,128)S(1)} %get-tuple-element.99.price, ...), custom_call_target="tpu_custom_call" | custom-call | tf_op jit(solution)/shard_map/pallas_call | solution.py:437
  123.9 9.0 %all_to_all.138 = f32[32,2,128]{2,1,0:T(2,128)S(1)} all-to-all(f32[32,2,128]{2,1,0:T(2,128)S(1)} %bitcast.43), channel_id=1, replica_groups=mesh['gy'=8,'gx'=4] {'gy','gx'}, dimensions={0} | all-to-all | bytes 65536 | tf_op jit(solution)/shard_map/all_to_all | solution.py:454
  134.8 9.0 %all_to_all.139 = f32[32,2,128]{2,1,0:T(2,128)S(1)} all-to-all(f32[32,2,128]{2,1,0:T(2,128)S(1)} %bitcast.44), channel_id=1, replica_groups=mesh['gy'=8,'gx'=4] {'gy','gx'}, dimensions={0} | all-to-all | bytes 65536 | tf_op jit(solution)/shard_map/all_to_all | solution.py:454
  143.7 2.0 %shard_map.84 = (f32[17,160,128]{2,1,0:T(8,128)S(1)}, f32[17,160,128]{2,1,0:T(8,128)S(1)}, f32[17,160,128]{2,1,0:T(8,128)S(1)}, f32[64,128]{1,0:T(8,128)S(1)}, f32[8,128]{1,0:T(8,128)S(1)}) custom-call(f32[64,128]{1,0:T(8,128)S(1)} %bitcast.33, f32[8,128]{1,0:T(8,128)S(1)} %get-tuple-element.159.rates, f32[5,160,128]{2,1,0:T(8,128)S(1)} %get-tuple-element.99.price, ...), custom_call_target="tpu_custom_call" | custom-call | tf_op jit(solution)/shard_map/pallas_call | solution.py:437
  145.7 9.0 %all_to_all.140 = f32[32,2,128]{2,1,0:T(2,128)S(1)} all-to-all(f32[32,2,128]{2,1,0:T(2,128)S(1)} %bitcast.45), channel_id=1, replica_groups=mesh['gy'=8,'gx'=4] {'gy','gx'}, dimensions={0} | all-to-all | bytes 65536 | tf_op jit(solution)/shard_map/all_to_all | solution.py:454
  154.7 2.5 %shard_map.85 = (f32[2,4,128,512]{3,2,1,0:T(8,128)S(1)}, f32[4,128,512]{2,1,0:T(8,128)S(1)}, f32[64,128]{1,0:T(8,128)}) custom-call(f32[64,128]{1,0:T(8,128)S(1)} %bitcast.34, f32[8,128]{1,0:T(8,128)S(1)} %get-tuple-element.164.rates, f32[5,160,128]{2,1,0:T(8,128)S(1)} %get-tuple-element.99.price, f32[17,160,128]{2,1,0:T(8,128)S(1)} %get-tuple-element.100.source, ...), custom_call_target="tpu_custom_call" | custom-call | tf_op jit(solution)/shard_map/pallas_call | solution.py:437
  157.2 2.6 %all-to-all-start.11 = ((f32[32,2,128]{2,1,0:T(2,128)}), f32[32,2,128]{2,1,0:T(2,128)S(1)}, u32[]{:S(2)}, u32[]{:S(2)}) async-start(f32[32,2,128]{2,1,0:T(2,128)} %bitcast.22), calls=%async_computation.11 | async-start | bytes 65536 | tf_op jit(solution)/shard_map/all_to_all | solution.py:454
  162.0 5.0 %all-to-all-done.11 = f32[32,2,128]{2,1,0:T(2,128)S(1)} async-done(((f32[32,2,128]{2,1,0:T(2,128)}), f32[32,2,128]{2,1,0:T(2,128)S(1)}, u32[]{:S(2)}, u32[]{:S(2)}) %all-to-all-start.11) | async-done | bytes 32800 | tf_op jit(solution)/shard_map/all_to_all | solution.py:454
  (34 shorter events, 20.7 us)
Async XLA Ops:
  2.6 5.9 %collective-permute-start = (f32[5,128,128]{2,1,0:T(8,128)S(1)}, f32[5,128,128]{2,1,0:T(8,128)S(1)}, u32[]{:S(2)}, u32[]{:S(2)}) collective-permute-start(f32[5,128,128]{2,1,0:T(8,128)S(1)} %get-tuple-element.87), channel_id=1, source_target_pairs={{1,0},{2,1},{3,2},{5,4},{6,5},{7,6},{9,8},{10,9},{11,10},{13,12},{... | collective-permute-start | bytes 983048 | tf_op jit(solution)/shard_map/ppermute | solution.py:28
  3.9 11.0 %copy-start.3 = (f32[128,512]{1,0:T(8,128)S(1)}, f32[128,512]{1,0:T(8,128)}, u32[]{:S(2)}) copy-start(f32[128,512]{1,0:T(8,128)} %cost.5) | copy-start | bytes 786436
  4.0 4.6 %collective-permute-start.1 = (f32[5,128,128]{2,1,0:T(8,128)S(1)}, f32[5,128,128]{2,1,0:T(8,128)S(1)}, u32[]{:S(2)}, u32[]{:S(2)}) collective-permute-start(f32[5,128,128]{2,1,0:T(8,128)S(1)} %get-tuple-element.88), channel_id=1, source_target_pairs={{0,1},{1,2},{2,3},{4,5},{5,6},{6,7},{8,9},{9,10},{10,11},{12,13},{... | collective-permute-start | bytes 983048 | tf_op jit(solution)/shard_map/ppermute | solution.py:28
  7.1 7.8 %copy-start = (f32[2,4,128,512]{3,2,1,0:T(8,128)S(1)}, f32[2,4,128,512]{3,2,1,0:T(8,128)}, u32[]{:S(2)}) copy-start(f32[2,4,128,512]{3,2,1,0:T(8,128)} %flow.5) | copy-start | bytes 6291460
  7.2 7.8 %copy-start.2 = (f32[4,128,512]{2,1,0:T(8,128)S(1)}, f32[4,128,512]{2,1,0:T(8,128)}, u32[]{:S(2)}) copy-start(f32[4,128,512]{2,1,0:T(8,128)} %pot.5) | copy-start | bytes 3145732
  8.5 6.4 %copy-start.1 = (f32[4,128,512]{2,1,0:T(8,128)S(1)}, f32[4,128,512]{2,1,0:T(8,128)}, u32[]{:S(2)}) copy-start(f32[4,128,512]{2,1,0:T(8,128)} %imb.5) | copy-start | bytes 3145732
  8.6 8.6 %collective-permute-start.2 = (f32[440,128]{1,0:T(8,128)S(1)}, f32[440,128]{1,0:T(8,128)S(1)}, u32[]{:S(2)}, u32[]{:S(2)}) collective-permute-start(f32[440,128]{1,0:T(8,128)S(1)} %get-tuple-element.97), channel_id=1, source_target_pairs={{0,4},{4,8},{8,12},{12,16},{16,20},{20,24},{24,28},{1,5},{5,9},{9,... | collective-permute-start | bytes 675848 | tf_op jit(solution)/shard_map/ppermute | solution.py:28
  13.6 8.0 %collective-permute-start.3 = (f32[440,128]{1,0:T(8,128)S(1)}, f32[440,128]{1,0:T(8,128)S(1)}, u32[]{:S(2)}, u32[]{:S(2)}) collective-permute-start(f32[440,128]{1,0:T(8,128)S(1)} %get-tuple-element.98), channel_id=1, source_target_pairs={{4,0},{8,4},{12,8},{16,12},{20,16},{24,20},{28,24},{5,1},{9,5},{13... | collective-permute-start | bytes 675848 | tf_op jit(solution)/shard_map/ppermute | solution.py:28
  85.1 14.8 %collective-permute-start.4 = (f32[312,128]{1,0:T(8,128)S(1)}, f32[312,128]{1,0:T(8,128)S(1)}, u32[]{:S(2)}, u32[]{:S(2)}) collective-permute-start(f32[312,128]{1,0:T(8,128)S(1)} %get-tuple-element.135), channel_id=1, source_target_pairs={{0,4},{4,8},{8,12},{12,16},{16,20},{20,24},{24,28},{1,5},{5,9},{9,... | collective-permute-start | bytes 479240 | tf_op jit(solution)/shard_map/ppermute | solution.py:28
  87.6 12.3 %collective-permute-start.5 = (f32[312,128]{1,0:T(8,128)S(1)}, f32[312,128]{1,0:T(8,128)S(1)}, u32[]{:S(2)}, u32[]{:S(2)}) collective-permute-start(f32[312,128]{1,0:T(8,128)S(1)} %get-tuple-element.136), channel_id=1, source_target_pairs={{4,0},{8,4},{12,8},{16,12},{20,16},{24,20},{28,24},{5,1},{9,5},{13... | collective-permute-start | bytes 479240 | tf_op jit(solution)/shard_map/ppermute | solution.py:28
  157.2 9.8 %all-to-all-start.11 = ((f32[32,2,128]{2,1,0:T(2,128)}), f32[32,2,128]{2,1,0:T(2,128)S(1)}, u32[]{:S(2)}, u32[]{:S(2)}) async-start(f32[32,2,128]{2,1,0:T(2,128)} %bitcast.22), calls=%async_computation.11 | async-start | bytes 65536 | tf_op jit(solution)/shard_map/all_to_all | solution.py:454

commit v6 on v5

--- a/solution.py
+++ b/solution.py
@@ -195,34 +195,38 @@
     return jnp.sum(value.reshape(-1, 8, LANES), axis=0)
 
 
-def same_parity(value):
-    value = value + pltpu.roll(value, 2, 0)
-    return value + pltpu.roll(value, 4, 0)
-
-
-def next_rates(recv, rates):
-    total = same_parity(folded(recv[...])) + epsilon
-    ratio = total / pltpu.roll(total, 1, 0)
-    return rates[...] * lax.rsqrt(lax.rsqrt(ratio))
+def row_lanes(pairs):
+    assert 2 * pairs == 8
+    return lax.broadcasted_iota(jnp.int32, (8, LANES), 0) == lax.broadcasted_iota(jnp.int32, (8, LANES), 1)
+
+
+def next_rates(pairs, recv, rates):
+    total = jnp.sum(folded(recv[...]), axis=0, keepdims=True)
+    each = jnp.sum(jnp.where(row_lanes(pairs), total, 0.0), axis=1, keepdims=True) + epsilon
+    each = jnp.broadcast_to(each, (8, LANES))
+    return rates[...] * lax.rsqrt(lax.rsqrt(each / pltpu.roll(each, pairs, 0)))
 
 
 def spread_rates(pairs, rates):
-    group = lax.broadcasted_iota(jnp.int32, (8, LANES), 1) // (LANES // pairs)
-    each = [jnp.max(jnp.where(group == p, rates, 0.0), axis=1, keepdims=True) for p in range(pairs)]
-    each = [jnp.broadcast_to(value, (8, LANES)) for value in each]
-    return [v[1:2] for v in each], rates[1:2], [v[0:1] for v in each], rates[0:1]
-
-
-def sums_to_send(pairs, even, odd):
+    group = lax.broadcasted_iota(jnp.int32, (1, LANES), 1) // (LANES // pairs)
+    out = []
+    for first in (pairs, 0):
+        each = [rates[first + p : first + p + 1] for p in range(pairs)]
+        side = each[0]
+        for p in range(1, pairs):
+            side = jnp.where(group == p, each[p], side)
+        out += [each, side]
+    return out
+
+
+def sums_to_send(pairs, primals, duals):
     row = lax.broadcasted_iota(jnp.int32, (8, LANES), 0)
-    group = lax.broadcasted_iota(jnp.int32, (8, LANES), 1) // (LANES // pairs)
     matrix = jnp.zeros((8, LANES), jnp.float32)
-    for p in range(pairs):
-        for k, part in ((2 * p, even[p]), (2 * p + 1, odd[p])):
-            if part is not None:
-                matrix = jnp.where(row == k, jnp.sum(part, axis=0, keepdims=True), matrix)
+    for k, part in enumerate([*primals, *duals]):
+        matrix = jnp.where(row == k, jnp.sum(part, axis=0, keepdims=True), matrix)
     sums = jnp.sum(matrix, axis=1, keepdims=True)
-    return same_parity(jnp.where(group == row // 2, sums, 0.0))
+    line = jnp.sum(jnp.where(row_lanes(pairs), sums, 0.0), axis=0, keepdims=True)
+    return jnp.broadcast_to(line, (8, LANES))
 
 
 def put_sums(send, sums):
@@ -277,7 +281,7 @@
     per = price.shape[0] - 1
     tiles = pairs * per
     end, last = TOP + rows, rows // CHUNK - 1
-    rates_now = next_rates(recv, rates)
+    rates_now = next_rates(pairs, recv, rates)
     rates_out[...] = rates_now
     taus, tau_side, sigmas, sigma_side = spread_rates(pairs, rates_now)
     above, below, sides = own_masks(pairs)
@@ -388,7 +392,7 @@
 ):
     per = price.shape[0] - 1
     rows = pot_out.shape[1]
-    taus, tau_side, sigmas, _ = spread_rates(pairs, next_rates(recv, rates))
+    taus, tau_side, sigmas, _ = spread_rates(pairs, next_rates(pairs, recv, rates))
     above, _, sides = own_masks(pairs)
 
     def primal(start, count, mask):
@@ -429,7 +433,7 @@
     last = rows // CLOSING_CHUNK - 1
     short = lax.fori_loop(1, last + 1, turn, (jnp.zeros((8, LANES), jnp.float32),) * pairs)
     short = close(last, short)
-    put_sums(send, sums_to_send(pairs, short, [None] * pairs))
+    put_sums(send, sums_to_send(pairs, short, ()))
 
 
 def call(kernel, out_shape, operands, aliases=None, scratch=(), limit=8, space=pltpu.VMEM, flops=0):
@@ -505,7 +509,7 @@
     )
     u, a, b, _, _, send = call(
         functools.partial(late_kernel, pairs, rows),
-        [field] * 5 + [kept(2 * devices, LANES)],
+        [field] * 5 + [kept(devices, LANES)],
         [price, source, u, a, b, early_sums, *early],
         aliases={k + 6: k for k in range(5)},
     )
@@ -515,7 +519,7 @@
         sending = k % DEPTH == 0
         u, a, b, send, rates, *slabs = call(
             functools.partial(iterate_kernel, pairs, rows, sending),
-            [field] * 3 + [kept(2 * devices, LANES), kept(8, LANES)] + [strips(3 * (tiles + 1))] * 2 * sending,
+            [field] * 3 + [kept(devices, LANES), kept(8, LANES)] + [strips(3 * (tiles + 1))] * 2 * sending,
             [recv, rates, price, source, u, a, b],
             scratch=[field] * 2,
         )
@@ -531,13 +535,13 @@
             )
     flow_out, pot_out, send = call(
         functools.partial(closing_kernel, pairs),
-        [kept(2, pairs, rows, cols), kept(pairs, rows, cols), kept(2 * devices, LANES)],
+        [kept(2, pairs, rows, cols), kept(pairs, rows, cols), kept(devices, LANES)],
         [recv, rates, price, source, u, a, b],
         scratch=[field] * 4,
         limit=12,
     )
     cells = rows * lax.axis_size("gy") * cols * lax.axis_size("gx")
-    residual = jnp.sum(exchange(send), axis=0)[:: LANES // pairs] / cells
+    residual = jnp.sum(exchange(send), axis=0)[:pairs] / cells
     return flow_out, pot_out, residual
 
 

time: 168 us -> 167 us (level)
  no operation moved by 1% of the time
where the time goes in v6:
time: 167 us
  blocking collectives  108 us (65%)
  Pallas kernels  28.4 us (17%)
  starting transfers between devices  17.1 us (10%)
  waiting for transfers between devices  9.29 us (6%)
  local copies, waits for them, and re-layouts  2.32 us (1%)
    all_to_all x11, blocking collectives, exchange(): return lax.all_to_all(send, AXES, 0, 0, tiled=True)  108 us
    pallas_call x19, Pallas kernels, call(): pl.pallas_call(kernel, out_shape=out_shape, in_specs=[pl.BlockSpec(memory...  28.4 us
    ppermute x6, starting transfers between devices, neighbour(): lax.ppermute(value, axis, [(source, source + steps) for source in range(l...  14.6 us
    all_to_all x1, waiting for transfers between devices, exchange(): return lax.all_to_all(send, AXES, 0, 0, tiled=True)  4.88 us
    ppermute x6, waiting for transfers between devices, neighbour(): lax.ppermute(value, axis, [(source, source + steps) for source in range(l...  4.41 us
  transfers between devices with their start and end apart: 7, of which 2 were waited for; matrix products, arithmetic and copies ran while one was open for 1% of the time, Pallas kernels for 2%

profile of v6, /device:TPU:0, one launch (start us, length us, event | category | flops | bytes accessed | tf_op | source)
XLA Modules:
  0.0 166.6 jit_solution(12956649950895757474)
XLA Ops:
  0.6 2.0 %shard_map.67 = (f32[5,128,128]{2,1,0:T(8,128)S(1)}, f32[5,128,128]{2,1,0:T(8,128)S(1)}) custom-call(f32[4,128,512]{2,1,0:T(8,128)} %imb.5, f32[2,4,128,512]{3,2,1,0:T(8,128)} %flow.5, f32[4,128,512]{2,1,0:T(8,128)} %pot.5, f32[128,512]{1,0:T(8,128)} %cost.5), custom_call_target="tpu_custom_call" | custom-call | tf_op jit(solution)/shard_map/pallas_call | solution.py:441
  4.0 3.2 %collective-permute-start.1 = (f32[5,128,128]{2,1,0:T(8,128)S(1)}, f32[5,128,128]{2,1,0:T(8,128)S(1)}, u32[]{:S(2)}, u32[]{:S(2)}) collective-permute-start(f32[5,128,128]{2,1,0:T(8,128)S(1)} %get-tuple-element.88), channel_id=1, source_target_pairs={{0,1},{1,2},{2,3},{4,5},{5,6},{6,7},{8,9},{9,10},{10,11},{12,13},{... | collective-permute-start | bytes 983048 | tf_op jit(solution)/shard_map/ppermute | solution.py:28
  8.6 5.0 %collective-permute-start.2 = (f32[440,128]{1,0:T(8,128)S(1)}, f32[440,128]{1,0:T(8,128)S(1)}, u32[]{:S(2)}, u32[]{:S(2)}) collective-permute-start(f32[440,128]{1,0:T(8,128)S(1)} %get-tuple-element.97), channel_id=1, source_target_pairs={{0,4},{4,8},{8,12},{12,16},{16,20},{20,24},{24,28},{1,5},{5,9},{9,... | collective-permute-start | bytes 675848 | tf_op jit(solution)/shard_map/ppermute | solution.py:28
  17.2 4.4 %collective-permute-done.3.bottom = f32[440,128]{1,0:T(8,128)S(1)} collective-permute-done((f32[440,128]{1,0:T(8,128)S(1)}, f32[440,128]{1,0:T(8,128)S(1)}, u32[]{:S(2)}, u32[]{:S(2)}) %collective-permute-start.3) | collective-permute-done | bytes 225312 | tf_op jit(solution)/shard_map/ppermute | solution.py:28
  22.1 17.1 %all_to_all.130 = f32[32,1,128]{2,1,0:T(1,128)S(1)} all-to-all(f32[32,1,128]{2,1,0:T(1,128)S(1)} %bitcast.60), channel_id=1, replica_groups=mesh['gy'=8,'gx'=4] {'gy','gx'}, dimensions={0} | all-to-all | bytes 32768 | tf_op jit(solution)/shard_map/all_to_all | solution.py:458
  39.2 2.0 %shard_map.74 = (f32[17,160,128]{2,1,0:T(8,128)S(1)}, f32[17,160,128]{2,1,0:T(8,128)S(1)}, f32[17,160,128]{2,1,0:T(8,128)S(1)}, f32[32,128]{1,0:T(8,128)S(1)}, f32[8,128]{1,0:T(8,128)S(1)}) custom-call(f32[32,128]{1,0:T(8,128)S(1)} %bitcast.50, f32[8,128]{1,0:T(8,128)S(1)} %broadcast_in_dim.3.rates, f32[5,160,128]{2,1,0:T(8,128)S(1)} %get-tuple-element.99.price, ...), custom_call_target="tpu_custom_call" | custom-call | tf_op jit(solution)/shard_map/pallas_call | solution.py:441
  41.2 8.9 %all_to_all.131 = f32[32,1,128]{2,1,0:T(1,128)S(1)} all-to-all(f32[32,1,128]{2,1,0:T(1,128)S(1)} %bitcast.61), channel_id=1, replica_groups=mesh['gy'=8,'gx'=4] {'gy','gx'}, dimensions={0} | all-to-all | bytes 32768 | tf_op jit(solution)/shard_map/all_to_all | solution.py:458
  52.0 8.9 %all_to_all.132 = f32[32,1,128]{2,1,0:T(1,128)S(1)} all-to-all(f32[32,1,128]{2,1,0:T(1,128)S(1)} %bitcast.62), channel_id=1, replica_groups=mesh['gy'=8,'gx'=4] {'gy','gx'}, dimensions={0} | all-to-all | bytes 32768 | tf_op jit(solution)/shard_map/all_to_all | solution.py:458
  62.8 8.9 %all_to_all.133 = f32[32,1,128]{2,1,0:T(1,128)S(1)} all-to-all(f32[32,1,128]{2,1,0:T(1,128)S(1)} %bitcast.63), channel_id=1, replica_groups=mesh['gy'=8,'gx'=4] {'gy','gx'}, dimensions={0} | all-to-all | bytes 32768 | tf_op jit(solution)/shard_map/all_to_all | solution.py:458
  71.7 2.0 %shard_map.77 = (f32[17,160,128]{2,1,0:T(8,128)S(1)}, f32[17,160,128]{2,1,0:T(8,128)S(1)}, f32[17,160,128]{2,1,0:T(8,128)S(1)}, f32[32,128]{1,0:T(8,128)S(1)}, f32[8,128]{1,0:T(8,128)S(1)}) custom-call(f32[32,128]{1,0:T(8,128)S(1)} %bitcast.53, f32[8,128]{1,0:T(8,128)S(1)} %get-tuple-element.124.rates, f32[5,160,128]{2,1,0:T(8,128)S(1)} %get-tuple-element.99.price, ...), custom_call_target="tpu_custom_call" | custom-call | tf_op jit(solution)/shard_map/pallas_call | solution.py:441
  73.7 8.9 %all_to_all.134 = f32[32,1,128]{2,1,0:T(1,128)S(1)} all-to-all(f32[32,1,128]{2,1,0:T(1,128)S(1)} %bitcast.64), channel_id=1, replica_groups=mesh['gy'=8,'gx'=4] {'gy','gx'}, dimensions={0} | all-to-all | bytes 32768 | tf_op jit(solution)/shard_map/all_to_all | solution.py:458
  82.6 2.1 %shard_map.78 = (f32[17,160,128]{2,1,0:T(8,128)S(1)}, f32[17,160,128]{2,1,0:T(8,128)S(1)}, f32[17,160,128]{2,1,0:T(8,128)S(1)}, f32[32,128]{1,0:T(8,128)S(1)}, f...) custom-call(f32[32,128]{1,0:T(8,128)S(1)} %bitcast.49, ...), custom_call_target="tpu_custom_call" | custom-call | tf_op jit(solution)/shard_map/pallas_call | solution.py:441
  84.7 2.5 %collective-permute-start.4 = (f32[312,128]{1,0:T(8,128)S(1)}, f32[312,128]{1,0:T(8,128)S(1)}, u32[]{:S(2)}, u32[]{:S(2)}) collective-permute-start(f32[312,128]{1,0:T(8,128)S(1)} %get-tuple-element.135), channel_id=1, source_target_pairs={{0,4},{4,8},{8,12},{12,16},{16,20},{20,24},{24,28},{1,5},{5,9},{9,... | collective-permute-start | bytes 479240 | tf_op jit(solution)/shard_map/ppermute | solution.py:28
  88.5 10.9 %all_to_all.135 = f32[32,1,128]{2,1,0:T(1,128)S(1)} all-to-all(f32[32,1,128]{2,1,0:T(1,128)S(1)} %bitcast.59), channel_id=1, replica_groups=mesh['gy'=8,'gx'=4] {'gy','gx'}, dimensions={0} | all-to-all | bytes 32768 | tf_op jit(solution)/shard_map/all_to_all | solution.py:458
  101.4 8.9 %all_to_all.136 = f32[32,1,128]{2,1,0:T(1,128)S(1)} all-to-all(f32[32,1,128]{2,1,0:T(1,128)S(1)} %bitcast.65), channel_id=1, replica_groups=mesh['gy'=8,'gx'=4] {'gy','gx'}, dimensions={0} | all-to-all | bytes 32768 | tf_op jit(solution)/shard_map/all_to_all | solution.py:458
  112.2 9.1 %all_to_all.137 = f32[32,1,128]{2,1,0:T(1,128)S(1)} all-to-all(f32[32,1,128]{2,1,0:T(1,128)S(1)} %bitcast.66), channel_id=1, replica_groups=mesh['gy'=8,'gx'=4] {'gy','gx'}, dimensions={0} | all-to-all | bytes 32768 | tf_op jit(solution)/shard_map/all_to_all | solution.py:458
  121.3 2.0 %shard_map.82 = (f32[17,160,128]{2,1,0:T(8,128)S(1)}, f32[17,160,128]{2,1,0:T(8,128)S(1)}, f32[17,160,128]{2,1,0:T(8,128)S(1)}, f32[32,128]{1,0:T(8,128)S(1)}, f32[8,128]{1,0:T(8,128)S(1)}) custom-call(f32[32,128]{1,0:T(8,128)S(1)} %bitcast.55, f32[8,128]{1,0:T(8,128)S(1)} %get-tuple-element.149.rates, f32[5,160,128]{2,1,0:T(8,128)S(1)} %get-tuple-element.99.price, ...), custom_call_target="tpu_custom_call" | custom-call | tf_op jit(solution)/shard_map/pallas_call | solution.py:441
  123.3 8.9 %all_to_all.138 = f32[32,1,128]{2,1,0:T(1,128)S(1)} all-to-all(f32[32,1,128]{2,1,0:T(1,128)S(1)} %bitcast.67), channel_id=1, replica_groups=mesh['gy'=8,'gx'=4] {'gy','gx'}, dimensions={0} | all-to-all | bytes 32768 | tf_op jit(solution)/shard_map/all_to_all | solution.py:458
  134.1 8.9 %all_to_all.139 = f32[32,1,128]{2,1,0:T(1,128)S(1)} all-to-all(f32[32,1,128]{2,1,0:T(1,128)S(1)} %bitcast.68), channel_id=1, replica_groups=mesh['gy'=8,'gx'=4] {'gy','gx'}, dimensions={0} | all-to-all | bytes 32768 | tf_op jit(solution)/shard_map/all_to_all | solution.py:458
  143.0 2.0 %shard_map.84 = (f32[17,160,128]{2,1,0:T(8,128)S(1)}, f32[17,160,128]{2,1,0:T(8,128)S(1)}, f32[17,160,128]{2,1,0:T(8,128)S(1)}, f32[32,128]{1,0:T(8,128)S(1)}, f32[8,128]{1,0:T(8,128)S(1)}) custom-call(f32[32,128]{1,0:T(8,128)S(1)} %bitcast.57, f32[8,128]{1,0:T(8,128)S(1)} %get-tuple-element.159.rates, f32[5,160,128]{2,1,0:T(8,128)S(1)} %get-tuple-element.99.price, ...), custom_call_target="tpu_custom_call" | custom-call | tf_op jit(solution)/shard_map/pallas_call | solution.py:441
  145.0 8.9 %all_to_all.140 = f32[32,1,128]{2,1,0:T(1,128)S(1)} all-to-all(f32[32,1,128]{2,1,0:T(1,128)S(1)} %bitcast.69), channel_id=1, replica_groups=mesh['gy'=8,'gx'=4] {'gy','gx'}, dimensions={0} | all-to-all | bytes 32768 | tf_op jit(solution)/shard_map/all_to_all | solution.py:458
  153.9 2.5 %shard_map.85 = (f32[2,4,128,512]{3,2,1,0:T(8,128)S(1)}, f32[4,128,512]{2,1,0:T(8,128)S(1)}, f32[32,128]{1,0:T(8,128)}) custom-call(f32[32,128]{1,0:T(8,128)S(1)} %bitcast.58, f32[8,128]{1,0:T(8,128)S(1)} %get-tuple-element.164.rates, f32[5,160,128]{2,1,0:T(8,128)S(1)} %get-tuple-element.99.price, f32[17,160,128]{2,1,0:T(8,128)S(1)} %get-tuple-element.100.source, ...), custom_call_target="tpu_custom_call" | custom-call | tf_op jit(solution)/shard_map/pallas_call | solution.py:441
  156.3 2.6 %all-to-all-start.11 = ((f32[32,1,128]{2,1,0:T(1,128)}), f32[32,1,128]{2,1,0:T(1,128)S(1)}, u32[]{:S(2)}, u32[]{:S(2)}) async-start(f32[32,1,128]{2,1,0:T(1,128)} %bitcast.34), calls=%async_computation.11 | async-start | bytes 32768 | tf_op jit(solution)/shard_map/all_to_all | solution.py:458
  161.2 4.9 %all-to-all-done.11 = f32[32,1,128]{2,1,0:T(1,128)S(1)} async-done(((f32[32,1,128]{2,1,0:T(1,128)}), f32[32,1,128]{2,1,0:T(1,128)S(1)}, u32[]{:S(2)}, u32[]{:S(2)}) %all-to-all-start.11) | async-done | bytes 16416 | tf_op jit(solution)/shard_map/all_to_all | solution.py:458
  (33 shorter events, 20.6 us)
Async XLA Ops:
  2.6 5.9 %collective-permute-start = (f32[5,128,128]{2,1,0:T(8,128)S(1)}, f32[5,128,128]{2,1,0:T(8,128)S(1)}, u32[]{:S(2)}, u32[]{:S(2)}) collective-permute-start(f32[5,128,128]{2,1,0:T(8,128)S(1)} %get-tuple-element.87), channel_id=1, source_target_pairs={{1,0},{2,1},{3,2},{5,4},{6,5},{7,6},{9,8},{10,9},{11,10},{13,12},{... | collective-permute-start | bytes 983048 | tf_op jit(solution)/shard_map/ppermute | solution.py:28
  3.9 11.0 %copy-start.3 = (f32[128,512]{1,0:T(8,128)S(1)}, f32[128,512]{1,0:T(8,128)}, u32[]{:S(2)}) copy-start(f32[128,512]{1,0:T(8,128)} %cost.5) | copy-start | bytes 786436
  4.0 4.6 %collective-permute-start.1 = (f32[5,128,128]{2,1,0:T(8,128)S(1)}, f32[5,128,128]{2,1,0:T(8,128)S(1)}, u32[]{:S(2)}, u32[]{:S(2)}) collective-permute-start(f32[5,128,128]{2,1,0:T(8,128)S(1)} %get-tuple-element.88), channel_id=1, source_target_pairs={{0,1},{1,2},{2,3},{4,5},{5,6},{6,7},{8,9},{9,10},{10,11},{12,13},{... | collective-permute-start | bytes 983048 | tf_op jit(solution)/shard_map/ppermute | solution.py:28
  7.1 7.8 %copy-start = (f32[2,4,128,512]{3,2,1,0:T(8,128)S(1)}, f32[2,4,128,512]{3,2,1,0:T(8,128)}, u32[]{:S(2)}) copy-start(f32[2,4,128,512]{3,2,1,0:T(8,128)} %flow.5) | copy-start | bytes 6291460
  7.2 7.8 %copy-start.2 = (f32[4,128,512]{2,1,0:T(8,128)S(1)}, f32[4,128,512]{2,1,0:T(8,128)}, u32[]{:S(2)}) copy-start(f32[4,128,512]{2,1,0:T(8,128)} %pot.5) | copy-start | bytes 3145732
  8.5 6.4 %copy-start.1 = (f32[4,128,512]{2,1,0:T(8,128)S(1)}, f32[4,128,512]{2,1,0:T(8,128)}, u32[]{:S(2)}) copy-start(f32[4,128,512]{2,1,0:T(8,128)} %imb.5) | copy-start | bytes 3145732
  8.6 8.6 %collective-permute-start.2 = (f32[440,128]{1,0:T(8,128)S(1)}, f32[440,128]{1,0:T(8,128)S(1)}, u32[]{:S(2)}, u32[]{:S(2)}) collective-permute-start(f32[440,128]{1,0:T(8,128)S(1)} %get-tuple-element.97), channel_id=1, source_target_pairs={{0,4},{4,8},{8,12},{12,16},{16,20},{20,24},{24,28},{1,5},{5,9},{9,... | collective-permute-start | bytes 675848 | tf_op jit(solution)/shard_map/ppermute | solution.py:28
  13.6 8.0 %collective-permute-start.3 = (f32[440,128]{1,0:T(8,128)S(1)}, f32[440,128]{1,0:T(8,128)S(1)}, u32[]{:S(2)}, u32[]{:S(2)}) collective-permute-start(f32[440,128]{1,0:T(8,128)S(1)} %get-tuple-element.98), channel_id=1, source_target_pairs={{4,0},{8,4},{12,8},{16,12},{20,16},{24,20},{28,24},{5,1},{9,5},{13... | collective-permute-start | bytes 675848 | tf_op jit(solution)/shard_map/ppermute | solution.py:28
  84.7 14.7 %collective-permute-start.4 = (f32[312,128]{1,0:T(8,128)S(1)}, f32[312,128]{1,0:T(8,128)S(1)}, u32[]{:S(2)}, u32[]{:S(2)}) collective-permute-start(f32[312,128]{1,0:T(8,128)S(1)} %get-tuple-element.135), channel_id=1, source_target_pairs={{0,4},{4,8},{8,12},{12,16},{16,20},{20,24},{24,28},{1,5},{5,9},{9,... | collective-permute-start | bytes 479240 | tf_op jit(solution)/shard_map/ppermute | solution.py:28
  87.2 12.2 %collective-permute-start.5 = (f32[312,128]{1,0:T(8,128)S(1)}, f32[312,128]{1,0:T(8,128)S(1)}, u32[]{:S(2)}, u32[]{:S(2)}) collective-permute-start(f32[312,128]{1,0:T(8,128)S(1)} %get-tuple-element.136), channel_id=1, source_target_pairs={{4,0},{8,4},{12,8},{16,12},{20,16},{24,20},{28,24},{5,1},{9,5},{13... | collective-permute-start | bytes 479240 | tf_op jit(solution)/shard_map/ppermute | solution.py:28
  156.3 9.7 %all-to-all-start.11 = ((f32[32,1,128]{2,1,0:T(1,128)}), f32[32,1,128]{2,1,0:T(1,128)S(1)}, u32[]{:S(2)}, u32[]{:S(2)}) async-start(f32[32,1,128]{2,1,0:T(1,128)} %bitcast.34), calls=%async_computation.11 | async-start | bytes 32768 | tf_op jit(solution)/shard_map/all_to_all | solution.py:458

commit v7 on v6

--- a/solution.py
+++ b/solution.py
@@ -17,7 +17,7 @@
 PAD = 8
 TOP = PAD + SLAB
 LANES = 128
-CLOSING_CHUNK = 64
+CLOSING_CHUNK = 128
 CHUNK = 32
 AXES = ("gy", "gx")
 
@@ -84,27 +84,47 @@
         copy.start()
     for copy in copies:
         copy.wait()
+    ups, downs = (places(start_depths(pairs * per, per, way)) for way in ("up", "down"))
     for n in range(4 * pairs + 1):
         for c in range(per):
             span = slice(c * LANES, (c + 1) * LANES)
-            up[strip(n * per + c), :] = top[n, 0:DEPTH, span]
-            down[strip(n * per + c), :] = bottom[n, SLAB - DEPTH : SLAB, span]
-
-
-def strip(n):
-    return slice(n * DEPTH, (n + 1) * DEPTH)
-
-
-def strips(count):
-    return kept(-(-count * DEPTH // 8) * 8, LANES)
-
-
-def slab_kernel(rows, count, left, right, own_up, own_down, up, down):
-    up[0 : count * DEPTH, :] = own_up[0 : count * DEPTH, :]
-    down[0 : count * DEPTH, :] = own_down[0 : count * DEPTH, :]
-    for k in range(5):
-        up[strip(count + k), :] = left[k, 0:DEPTH, :] + right[k, 0:DEPTH, :]
-        down[strip(count + k), :] = left[k, rows - DEPTH : rows, :] + right[k, rows - DEPTH : rows, :]
+            into, out_of = ups[n * per + c], downs[n * per + c]
+            up[into, :] = top[n, 0 : height(into), span]
+            down[out_of, :] = bottom[n, SLAB - height(out_of) : SLAB, span]
+
+
+def start_depths(tiles, per, way):
+    less = DEPTH - 1
+    fields = [DEPTH, less, less, less, less] if way == "up" else [DEPTH, DEPTH, DEPTH, less, DEPTH]
+    return [depth for depth in fields[:4] for _ in range(tiles)] + [fields[4]] * per + fields
+
+
+def later_depths(tiles, way):
+    fields = [DEPTH, DEPTH - 1, DEPTH - 1] if way == "up" else [DEPTH] * 3
+    return [depth for depth in fields for _ in range(tiles + 1)]
+
+
+def places(depths):
+    ends = [sum(depths[: n + 1]) for n in range(len(depths))]
+    return [slice(end - depth, end) for end, depth in zip(ends, depths)]
+
+
+def height(place):
+    return place.stop - place.start
+
+
+def strips(depths):
+    return kept(-(-sum(depths) // 8) * 8, LANES)
+
+
+def slab_kernel(rows, tiles, per, left, right, own_up, own_down, up, down):
+    for way, own, out in (("up", own_up, up), ("down", own_down, down)):
+        spots = places(start_depths(tiles, per, way))
+        own_rows = spots[-5].start
+        out[0:own_rows, :] = own[0:own_rows, :]
+        for k, spot in enumerate(spots[-5:]):
+            span = slice(0, height(spot)) if way == "up" else slice(rows - height(spot), rows)
+            out[spot, :] = left[k, span, :] + right[k, span, :]
 
 
 def own_masks(pairs):
@@ -143,16 +163,23 @@
 def adopt_kernel(pairs, rows, early_sums, top, bottom, u, a, b, source, price, u_out, a_out, b_out, source_out, price_out):
     per = price.shape[0] - 1
     tiles = pairs * per
-    end, count = TOP + rows, 4 * tiles + per
+    end = TOP + rows
     above, below, sides = own_masks(pairs)
-    for span, slab, mask in ((slice(TOP - DEPTH, TOP), top, above), (slice(end, end + DEPTH), bottom, below)):
+    for way, slab, mask in (("down", top, above), ("up", bottom, below)):
+        spots = places(start_depths(tiles, per, way))
+
+        def rows_of(spot):
+            return slice(TOP - height(spot), TOP) if way == "down" else slice(end, end + height(spot))
+
         for k, out in enumerate((u_out, a_out, b_out, source_out)):
             for t in range(tiles):
-                out[t, span, :] = slab[strip(k * tiles + t), :]
-            out[tiles, span, :] = slab[strip(count + k), :]
+                spot = spots[k * tiles + t]
+                out[t, rows_of(spot), :] = slab[spot, :]
+            out[tiles, rows_of(spots[-5 + k]), :] = slab[spots[-5 + k], :]
         for c in range(per):
-            price_out[c, span, :] = slab[strip(4 * tiles + c), :] + (1.0 - mask)
-        price_out[per, span, :] = jnp.where(sides * mask > 0.0, slab[strip(count + 4), :], 1.0)
+            spot = spots[4 * tiles + c]
+            price_out[c, rows_of(spot), :] = slab[spot, :] + (1.0 - mask)
+        price_out[per, rows_of(spots[-1]), :] = jnp.where(sides * mask > 0.0, slab[spots[-1], :], 1.0)
 
 
 def from_left(pairs, per, b, start, count, cell, closing=False):
@@ -317,10 +344,12 @@
     put_sums(send, sums_to_send(pairs, primals, duals))
     if sending:
         up, down = slabs
+        ups, downs = (places(later_depths(tiles, way)) for way in ("up", "down"))
         for k, out in enumerate((u_out, a_out, b_out)):
             for t in range(tiles + 1):
-                up[strip(k * (tiles + 1) + t), :] = out[t, TOP : TOP + DEPTH, :]
-                down[strip(k * (tiles + 1) + t), :] = out[t, end - DEPTH : end, :]
+                n = k * (tiles + 1) + t
+                up[ups[n], :] = out[t, TOP : TOP + height(ups[n]), :]
+                down[downs[n], :] = out[t, end - height(downs[n]) : end, :]
 
 
 def largest_chunk(rows):
@@ -380,11 +409,13 @@
 
 
 def merge_kernel(rows, recv, top, bottom, u, a, b, u_out, a_out, b_out):
-    tiles = u.shape[0]
+    tiles, end = u.shape[0] - 1, TOP + rows
+    ups, downs = (places(later_depths(tiles, way)) for way in ("up", "down"))
     for k, out in enumerate((u_out, a_out, b_out)):
-        for t in range(tiles):
-            out[t, TOP - DEPTH : TOP, :] = top[strip(k * tiles + t), :]
-            out[t, TOP + rows : TOP + rows + DEPTH, :] = bottom[strip(k * tiles + t), :]
+        for t in range(tiles + 1):
+            n = k * (tiles + 1) + t
+            out[t, TOP - height(downs[n]) : TOP, :] = top[downs[n], :]
+            out[t, end : end + height(ups[n]), :] = bottom[ups[n], :]
 
 
 def closing_kernel(
@@ -462,10 +493,13 @@
     pairs, rows, cols = imbalance.shape
     per = cols // LANES
     tiles = pairs * per
-    height = rows + 2 * TOP
+    total_rows = rows + 2 * TOP
     devices = lax.axis_size("gy") * lax.axis_size("gx")
 
-    arrays, count = 4 * pairs + 1, 4 * tiles + per
+    arrays = 4 * pairs + 1
+    moving = [strips(start_depths(tiles, per, way)) for way in ("up", "down")]
+    own = [strips(start_depths(tiles, per, way)[:-5]) for way in ("up", "down")]
+    later = [strips(later_depths(tiles, way)) for way in ("up", "down")]
     edge = kept(5, rows, LANES)
     inputs = [imbalance, flow, potential, cost]
     held = [pltpu.with_memory_space_constraint(x, pltpu.MemorySpace.HBM) for x in inputs]
@@ -479,7 +513,7 @@
     )
     own_up, own_down = call(
         functools.partial(edge_rows_kernel, pairs),
-        [strips(count), strips(count)],
+        own,
         held,
         scratch=[kept(arrays, SLAB, cols)] * 2 + [sems],
         space=pltpu.MemorySpace.HBM,
@@ -487,12 +521,12 @@
     )
     left, right = neighbour(left, "gx", -1), neighbour(right, "gx", 1)
     up, down = call(
-        functools.partial(slab_kernel, rows, count), [strips(count + 5)] * 2, [left, right, own_up, own_down]
+        functools.partial(slab_kernel, rows, tiles, per), moving, [left, right, own_up, own_down]
     )
     bottom, top = neighbour(up, "gy", -1), neighbour(down, "gy", 1)
 
-    field = kept(tiles + 1, height, LANES)
-    fields = [field] * 4 + [kept(per + 1, height, LANES)]
+    field = kept(tiles + 1, total_rows, LANES)
+    fields = [field] * 4 + [kept(per + 1, total_rows, LANES)]
     started = call(functools.partial(assemble_kernel, pairs), fields, inputs + [left, right], flops=40_000_000)
     u, a, b, source, price = started
     *early, early_sums = call(
@@ -519,7 +553,7 @@
         sending = k % DEPTH == 0
         u, a, b, send, rates, *slabs = call(
             functools.partial(iterate_kernel, pairs, rows, sending),
-            [field] * 3 + [kept(devices, LANES), kept(8, LANES)] + [strips(3 * (tiles + 1))] * 2 * sending,
+            [field] * 3 + [kept(devices, LANES), kept(8, LANES)] + later * sending,
             [recv, rates, price, source, u, a, b],
             scratch=[field] * 2,
         )

time: 167 us -> 167 us (level)
  no operation moved by 1% of the time
where the time goes in v7:
time: 167 us; the launch traced here: 166 us
  blocking collectives  108 us (65%)
  Pallas kernels  28.5 us (17%)
  starting transfers between devices  17.1 us (10%)
  waiting for transfers between devices  8.9 us (5%)
  local copies, waits for them, and re-layouts  2.32 us (1%)
    all_to_all x11, blocking collectives, exchange(): return lax.all_to_all(send, AXES, 0, 0, tiled=True)  108 us
    pallas_call x19, Pallas kernels, call(): pl.pallas_call(kernel, out_shape=out_shape, in_specs=[pl.BlockSpec(memory...  28.5 us
    ppermute x6, starting transfers between devices, neighbour(): lax.ppermute(value, axis, [(source, source + steps) for source in range(l...  14.6 us
    all_to_all x1, waiting for transfers between devices, exchange(): return lax.all_to_all(send, AXES, 0, 0, tiled=True)  4.88 us
    ppermute x6, waiting for transfers between devices, neighbour(): lax.ppermute(value, axis, [(source, source + steps) for source in range(l...  4.02 us
  transfers between devices with their start and end apart: 7, of which 2 were waited for; matrix products, arithmetic and copies ran while one was open for 1% of the time, Pallas kernels for 2%

profile of v7, /device:TPU:0, one launch (start us, length us, event | category | flops | bytes accessed | tf_op | source)
XLA Modules:
  0.0 166.4 jit_solution(9226022292937356710)
XLA Ops:
  0.6 2.0 %shard_map.67 = (f32[5,128,128]{2,1,0:T(8,128)S(1)}, f32[5,128,128]{2,1,0:T(8,128)S(1)}) custom-call(f32[4,128,512]{2,1,0:T(8,128)} %imb.5, f32[2,4,128,512]{3,2,1,0:T(8,128)} %flow.5, f32[4,128,512]{2,1,0:T(8,128)} %pot.5, f32[128,512]{1,0:T(8,128)} %cost.5), custom_call_target="tpu_custom_call" | custom-call | tf_op jit(solution)/shard_map/pallas_call | solution.py:472
  4.0 3.2 %collective-permute-start.1 = (f32[5,128,128]{2,1,0:T(8,128)S(1)}, f32[5,128,128]{2,1,0:T(8,128)S(1)}, u32[]{:S(2)}, u32[]{:S(2)}) collective-permute-start(f32[5,128,128]{2,1,0:T(8,128)S(1)} %get-tuple-element.88), channel_id=1, source_target_pairs={{0,1},{1,2},{2,3},{4,5},{5,6},{6,7},{8,9},{9,10},{10,11},{12,13},{... | collective-permute-start | bytes 983048 | tf_op jit(solution)/shard_map/ppermute | solution.py:28
  8.6 5.0 %collective-permute-start.2 = (f32[424,128]{1,0:T(8,128)S(1)}, f32[424,128]{1,0:T(8,128)S(1)}, u32[]{:S(2)}, u32[]{:S(2)}) collective-permute-start(f32[424,128]{1,0:T(8,128)S(1)} %get-tuple-element.97), channel_id=1, source_target_pairs={{0,4},{4,8},{8,12},{12,16},{16,20},{20,24},{24,28},{1,5},{5,9},{9,... | collective-permute-start | bytes 651272 | tf_op jit(solution)/shard_map/ppermute | solution.py:28
  17.2 4.0 %collective-permute-done.3.bottom = f32[384,128]{1,0:T(8,128)S(1)} collective-permute-done((f32[384,128]{1,0:T(8,128)S(1)}, f32[384,128]{1,0:T(8,128)S(1)}, u32[]{:S(2)}, u32[]{:S(2)}) %collective-permute-start.3) | collective-permute-done | bytes 196640 | tf_op jit(solution)/shard_map/ppermute | solution.py:28
  21.7 17.2 %all_to_all.130 = f32[32,1,128]{2,1,0:T(1,128)S(1)} all-to-all(f32[32,1,128]{2,1,0:T(1,128)S(1)} %bitcast.60), channel_id=1, replica_groups=mesh['gy'=8,'gx'=4] {'gy','gx'}, dimensions={0} | all-to-all | bytes 32768 | tf_op jit(solution)/shard_map/all_to_all | solution.py:489
  40.9 8.9 %all_to_all.131 = f32[32,1,128]{2,1,0:T(1,128)S(1)} all-to-all(f32[32,1,128]{2,1,0:T(1,128)S(1)} %bitcast.61), channel_id=1, replica_groups=mesh['gy'=8,'gx'=4] {'gy','gx'}, dimensions={0} | all-to-all | bytes 32768 | tf_op jit(solution)/shard_map/all_to_all | solution.py:489
  51.7 8.9 %all_to_all.132 = f32[32,1,128]{2,1,0:T(1,128)S(1)} all-to-all(f32[32,1,128]{2,1,0:T(1,128)S(1)} %bitcast.62), channel_id=1, replica_groups=mesh['gy'=8,'gx'=4] {'gy','gx'}, dimensions={0} | all-to-all | bytes 32768 | tf_op jit(solution)/shard_map/all_to_all | solution.py:489
  62.5 8.9 %all_to_all.133 = f32[32,1,128]{2,1,0:T(1,128)S(1)} all-to-all(f32[32,1,128]{2,1,0:T(1,128)S(1)} %bitcast.63), channel_id=1, replica_groups=mesh['gy'=8,'gx'=4] {'gy','gx'}, dimensions={0} | all-to-all | bytes 32768 | tf_op jit(solution)/shard_map/all_to_all | solution.py:489
  71.4 2.0 %shard_map.77 = (f32[17,160,128]{2,1,0:T(8,128)S(1)}, f32[17,160,128]{2,1,0:T(8,128)S(1)}, f32[17,160,128]{2,1,0:T(8,128)S(1)}, f32[32,128]{1,0:T(8,128)S(1)}, f32[8,128]{1,0:T(8,128)S(1)}) custom-call(f32[32,128]{1,0:T(8,128)S(1)} %bitcast.53, f32[8,128]{1,0:T(8,128)S(1)} %get-tuple-element.124.rates, f32[5,160,128]{2,1,0:T(8,128)S(1)} %get-tuple-element.99.price, ...), custom_call_target="tpu_custom_call" | custom-call | tf_op jit(solution)/shard_map/pallas_call | solution.py:472
  73.4 8.9 %all_to_all.134 = f32[32,1,128]{2,1,0:T(1,128)S(1)} all-to-all(f32[32,1,128]{2,1,0:T(1,128)S(1)} %bitcast.64), channel_id=1, replica_groups=mesh['gy'=8,'gx'=4] {'gy','gx'}, dimensions={0} | all-to-all | bytes 32768 | tf_op jit(solution)/shard_map/all_to_all | solution.py:489
  82.3 2.1 %shard_map.78 = (f32[17,160,128]{2,1,0:T(8,128)S(1)}, f32[17,160,128]{2,1,0:T(8,128)S(1)}, f32[17,160,128]{2,1,0:T(8,128)S(1)}, f32[32,128]{1,0:T(8,128)S(1)}, f...) custom-call(f32[32,128]{1,0:T(8,128)S(1)} %bitcast.49, ...), custom_call_target="tpu_custom_call" | custom-call | tf_op jit(solution)/shard_map/pallas_call | solution.py:472
  84.4 2.5 %collective-permute-start.4 = (f32[312,128]{1,0:T(8,128)S(1)}, f32[312,128]{1,0:T(8,128)S(1)}, u32[]{:S(2)}, u32[]{:S(2)}) collective-permute-start(f32[312,128]{1,0:T(8,128)S(1)} %get-tuple-element.135), channel_id=1, source_target_pairs={{0,4},{4,8},{8,12},{12,16},{16,20},{20,24},{24,28},{1,5},{5,9},{9,... | collective-permute-start | bytes 479240 | tf_op jit(solution)/shard_map/ppermute | solution.py:28
  88.2 10.9 %all_to_all.135 = f32[32,1,128]{2,1,0:T(1,128)S(1)} all-to-all(f32[32,1,128]{2,1,0:T(1,128)S(1)} %bitcast.59), channel_id=1, replica_groups=mesh['gy'=8,'gx'=4] {'gy','gx'}, dimensions={0} | all-to-all | bytes 32768 | tf_op jit(solution)/shard_map/all_to_all | solution.py:489
  99.2 2.0 %shard_map.80 = (f32[17,160,128]{2,1,0:T(8,128)S(1)}, f32[17,160,128]{2,1,0:T(8,128)S(1)}, f32[17,160,128]{2,1,0:T(8,128)S(1)}, f32[32,128]{1,0:T(8,128)S(1)}, f32[8,128]{1,0:T(8,128)S(1)}) custom-call(f32[32,128]{1,0:T(8,128)S(1)} %bitcast.48, f32[8,128]{1,0:T(8,128)S(1)} %get-tuple-element.134.rates, f32[5,160,128]{2,1,0:T(8,128)S(1)} %get-tuple-element.99.price, ...), custom_call_target="tpu_custom_call" | custom-call | tf_op jit(solution)/shard_map/pallas_call | solution.py:472
  101.2 8.9 %all_to_all.136 = f32[32,1,128]{2,1,0:T(1,128)S(1)} all-to-all(f32[32,1,128]{2,1,0:T(1,128)S(1)} %bitcast.65), channel_id=1, replica_groups=mesh['gy'=8,'gx'=4] {'gy','gx'}, dimensions={0} | all-to-all | bytes 32768 | tf_op jit(solution)/shard_map/all_to_all | solution.py:489
  112.0 9.1 %all_to_all.137 = f32[32,1,128]{2,1,0:T(1,128)S(1)} all-to-all(f32[32,1,128]{2,1,0:T(1,128)S(1)} %bitcast.66), channel_id=1, replica_groups=mesh['gy'=8,'gx'=4] {'gy','gx'}, dimensions={0} | all-to-all | bytes 32768 | tf_op jit(solution)/shard_map/all_to_all | solution.py:489
  121.0 2.0 %shard_map.82 = (f32[17,160,128]{2,1,0:T(8,128)S(1)}, f32[17,160,128]{2,1,0:T(8,128)S(1)}, f32[17,160,128]{2,1,0:T(8,128)S(1)}, f32[32,128]{1,0:T(8,128)S(1)}, f32[8,128]{1,0:T(8,128)S(1)}) custom-call(f32[32,128]{1,0:T(8,128)S(1)} %bitcast.55, f32[8,128]{1,0:T(8,128)S(1)} %get-tuple-element.149.rates, f32[5,160,128]{2,1,0:T(8,128)S(1)} %get-tuple-element.99.price, ...), custom_call_target="tpu_custom_call" | custom-call | tf_op jit(solution)/shard_map/pallas_call | solution.py:472
  123.1 8.9 %all_to_all.138 = f32[32,1,128]{2,1,0:T(1,128)S(1)} all-to-all(f32[32,1,128]{2,1,0:T(1,128)S(1)} %bitcast.67), channel_id=1, replica_groups=mesh['gy'=8,'gx'=4] {'gy','gx'}, dimensions={0} | all-to-all | bytes 32768 | tf_op jit(solution)/shard_map/all_to_all | solution.py:489
  133.8 8.9 %all_to_all.139 = f32[32,1,128]{2,1,0:T(1,128)S(1)} all-to-all(f32[32,1,128]{2,1,0:T(1,128)S(1)} %bitcast.68), channel_id=1, replica_groups=mesh['gy'=8,'gx'=4] {'gy','gx'}, dimensions={0} | all-to-all | bytes 32768 | tf_op jit(solution)/shard_map/all_to_all | solution.py:489
  142.7 2.0 %shard_map.84 = (f32[17,160,128]{2,1,0:T(8,128)S(1)}, f32[17,160,128]{2,1,0:T(8,128)S(1)}, f32[17,160,128]{2,1,0:T(8,128)S(1)}, f32[32,128]{1,0:T(8,128)S(1)}, f32[8,128]{1,0:T(8,128)S(1)}) custom-call(f32[32,128]{1,0:T(8,128)S(1)} %bitcast.57, f32[8,128]{1,0:T(8,128)S(1)} %get-tuple-element.159.rates, f32[5,160,128]{2,1,0:T(8,128)S(1)} %get-tuple-element.99.price, ...), custom_call_target="tpu_custom_call" | custom-call | tf_op jit(solution)/shard_map/pallas_call | solution.py:472
  144.7 8.9 %all_to_all.140 = f32[32,1,128]{2,1,0:T(1,128)S(1)} all-to-all(f32[32,1,128]{2,1,0:T(1,128)S(1)} %bitcast.69), channel_id=1, replica_groups=mesh['gy'=8,'gx'=4] {'gy','gx'}, dimensions={0} | all-to-all | bytes 32768 | tf_op jit(solution)/shard_map/all_to_all | solution.py:489
  153.6 2.5 %shard_map.85 = (f32[2,4,128,512]{3,2,1,0:T(8,128)S(1)}, f32[4,128,512]{2,1,0:T(8,128)S(1)}, f32[32,128]{1,0:T(8,128)}) custom-call(f32[32,128]{1,0:T(8,128)S(1)} %bitcast.58, f32[8,128]{1,0:T(8,128)S(1)} %get-tuple-element.164.rates, f32[5,160,128]{2,1,0:T(8,128)S(1)} %get-tuple-element.99.price, f32[17,160,128]{2,1,0:T(8,128)S(1)} %get-tuple-element.100.source, ...), custom_call_target="tpu_custom_call" | custom-call | tf_op jit(solution)/shard_map/pallas_call | solution.py:472
  156.1 2.6 %all-to-all-start.11 = ((f32[32,1,128]{2,1,0:T(1,128)}), f32[32,1,128]{2,1,0:T(1,128)S(1)}, u32[]{:S(2)}, u32[]{:S(2)}) async-start(f32[32,1,128]{2,1,0:T(1,128)} %bitcast.34), calls=%async_computation.11 | async-start | bytes 32768 | tf_op jit(solution)/shard_map/all_to_all | solution.py:489
  161.0 4.9 %all-to-all-done.11 = f32[32,1,128]{2,1,0:T(1,128)S(1)} async-done(((f32[32,1,128]{2,1,0:T(1,128)}), f32[32,1,128]{2,1,0:T(1,128)S(1)}, u32[]{:S(2)}, u32[]{:S(2)}) %all-to-all-start.11) | async-done | bytes 16416 | tf_op jit(solution)/shard_map/all_to_all | solution.py:489
  (33 shorter events, 20.6 us)
Async XLA Ops:
  2.6 5.9 %collective-permute-start = (f32[5,128,128]{2,1,0:T(8,128)S(1)}, f32[5,128,128]{2,1,0:T(8,128)S(1)}, u32[]{:S(2)}, u32[]{:S(2)}) collective-permute-start(f32[5,128,128]{2,1,0:T(8,128)S(1)} %get-tuple-element.87), channel_id=1, source_target_pairs={{1,0},{2,1},{3,2},{5,4},{6,5},{7,6},{9,8},{10,9},{11,10},{13,12},{... | collective-permute-start | bytes 983048 | tf_op jit(solution)/shard_map/ppermute | solution.py:28
  3.9 11.0 %copy-start.3 = (f32[128,512]{1,0:T(8,128)S(1)}, f32[128,512]{1,0:T(8,128)}, u32[]{:S(2)}) copy-start(f32[128,512]{1,0:T(8,128)} %cost.5) | copy-start | bytes 786436
  4.0 4.6 %collective-permute-start.1 = (f32[5,128,128]{2,1,0:T(8,128)S(1)}, f32[5,128,128]{2,1,0:T(8,128)S(1)}, u32[]{:S(2)}, u32[]{:S(2)}) collective-permute-start(f32[5,128,128]{2,1,0:T(8,128)S(1)} %get-tuple-element.88), channel_id=1, source_target_pairs={{0,1},{1,2},{2,3},{4,5},{5,6},{6,7},{8,9},{9,10},{10,11},{12,13},{... | collective-permute-start | bytes 983048 | tf_op jit(solution)/shard_map/ppermute | solution.py:28
  7.1 7.8 %copy-start = (f32[2,4,128,512]{3,2,1,0:T(8,128)S(1)}, f32[2,4,128,512]{3,2,1,0:T(8,128)}, u32[]{:S(2)}) copy-start(f32[2,4,128,512]{3,2,1,0:T(8,128)} %flow.5) | copy-start | bytes 6291460
  7.2 7.8 %copy-start.1 = (f32[4,128,512]{2,1,0:T(8,128)S(1)}, f32[4,128,512]{2,1,0:T(8,128)}, u32[]{:S(2)}) copy-start(f32[4,128,512]{2,1,0:T(8,128)} %imb.5) | copy-start | bytes 3145732
  7.2 7.8 %copy-start.2 = (f32[4,128,512]{2,1,0:T(8,128)S(1)}, f32[4,128,512]{2,1,0:T(8,128)}, u32[]{:S(2)}) copy-start(f32[4,128,512]{2,1,0:T(8,128)} %pot.5) | copy-start | bytes 3145732
  8.6 12.6 %collective-permute-start.2 = (f32[424,128]{1,0:T(8,128)S(1)}, f32[424,128]{1,0:T(8,128)S(1)}, u32[]{:S(2)}, u32[]{:S(2)}) collective-permute-start(f32[424,128]{1,0:T(8,128)S(1)} %get-tuple-element.97), channel_id=1, source_target_pairs={{0,4},{4,8},{8,12},{12,16},{16,20},{20,24},{24,28},{1,5},{5,9},{9,... | collective-permute-start | bytes 651272 | tf_op jit(solution)/shard_map/ppermute | solution.py:28
  13.6 7.6 %collective-permute-start.3 = (f32[384,128]{1,0:T(8,128)S(1)}, f32[384,128]{1,0:T(8,128)S(1)}, u32[]{:S(2)}, u32[]{:S(2)}) collective-permute-start(f32[384,128]{1,0:T(8,128)S(1)} %get-tuple-element.98), channel_id=1, source_target_pairs={{4,0},{8,4},{12,8},{16,12},{20,16},{24,20},{28,24},{5,1},{9,5},{13... | collective-permute-start | bytes 589832 | tf_op jit(solution)/shard_map/ppermute | solution.py:28
  84.4 14.7 %collective-permute-start.4 = (f32[312,128]{1,0:T(8,128)S(1)}, f32[312,128]{1,0:T(8,128)S(1)}, u32[]{:S(2)}, u32[]{:S(2)}) collective-permute-start(f32[312,128]{1,0:T(8,128)S(1)} %get-tuple-element.135), channel_id=1, source_target_pairs={{0,4},{4,8},{8,12},{12,16},{16,20},{20,24},{24,28},{1,5},{5,9},{9,... | collective-permute-start | bytes 479240 | tf_op jit(solution)/shard_map/ppermute | solution.py:28
  86.9 12.2 %collective-permute-start.5 = (f32[272,128]{1,0:T(8,128)S(1)}, f32[272,128]{1,0:T(8,128)S(1)}, u32[]{:S(2)}, u32[]{:S(2)}) collective-permute-start(f32[272,128]{1,0:T(8,128)S(1)} %get-tuple-element.136), channel_id=1, source_target_pairs={{4,0},{8,4},{12,8},{16,12},{20,16},{24,20},{28,24},{5,1},{9,5},{13... | collective-permute-start | bytes 417800 | tf_op jit(solution)/shard_map/ppermute | solution.py:28
  156.1 9.7 %all-to-all-start.11 = ((f32[32,1,128]{2,1,0:T(1,128)}), f32[32,1,128]{2,1,0:T(1,128)S(1)}, u32[]{:S(2)}, u32[]{:S(2)}) async-start(f32[32,1,128]{2,1,0:T(1,128)} %bitcast.34), calls=%async_computation.11 | async-start | bytes 32768 | tf_op jit(solution)/shard_map/all_to_all | solution.py:489
